TPU v7x, 32 devices: a whole 2x2x4 slice. The times are simulated.
32 devices in a mesh: ctx: 4 (over y, x), fsdp: 8 (over z, core).
Axes of the slice: x: 2, y: 2, z: 4, core: 2. Of those that a mesh axis runs over, the one named last changes fastest.
Arguments:
- hidden_in: bfloat16 [8, 512, 2048], P('fsdp', 'ctx'), may hold values from -6 to 6
- block_order: int32 [8, 8], P('fsdp'), may hold values from 0 to 7, each once within a row
- w_query: bfloat16 [2048, 2048], P('fsdp'), may hold values from -0.125 to 0.125
- w_key: bfloat16 [2048, 2048], P('fsdp'), may hold values from -0.125 to 0.125
- w_value: bfloat16 [2048, 2048], P('fsdp'), may hold values from -0.125 to 0.125
- w_output: bfloat16 [2048, 2048], P('fsdp'), may hold values from -0.125 to 0.125
- w_gate: bfloat16 [2048, 8192], P(None, 'fsdp'), may hold values from -0.125 to 0.125
- w_up: bfloat16 [2048, 8192], P(None, 'fsdp'), may hold values from -0.125 to 0.125
- w_down: bfloat16 [8192, 2048], P('fsdp'), may hold values from -0.0625 to 0.0625
- norm_gains: bfloat16 [4, 2048], P(None, 'fsdp'), may hold values from 0.3 to 5.5
- out_grad: bfloat16 [8, 512, 2048], P('fsdp', 'ctx'), may hold values from -6 to 6
Outputs:
- block_out: bfloat16 [8, 512, 2048], P('fsdp', 'ctx')
- input_grad: float32 [8, 512, 2048], P('fsdp', 'ctx')
- grad_query: float32 [2048, 2048], P('fsdp')
- grad_key: float32 [2048, 2048], P('fsdp')
- grad_value: float32 [2048, 2048], P('fsdp')
- grad_output: float32 [2048, 2048], P('fsdp')
- grad_gate: float32 [2048, 8192], P(None, 'fsdp')
- grad_up: float32 [2048, 8192], P(None, 'fsdp')
- grad_down: float32 [8192, 2048], P('fsdp')
- grad_gains: float32 [4, 2048], P(None, 'fsdp')
Inputs may be any that keep to these rules, and one draw needn't show every extreme that they name: `block_order`: each row names every block 0 to 7 once; entry j is the block of that sequence held in rows j * 64 to (j + 1) * 64 - 1.
All inputs are finite; a program needn't handle non-finite values.
Results may differ from a plain program's by a relative error of at most 0.023.
The roundings to bfloat16 on the way count: a program that leaves them out, or rounds other values in their place, can miss the bound.
Values may be sent and summed in bfloat16 or wider, within the bound.
A program may use at most 320 MiB of HBM per device.

v0:
```python
import jax
import jax.numpy as jnp
from jax import lax
from jax.sharding import PartitionSpec as P

HEADS = 16
HEAD_DIM = 128


norm_eps = 1e-06
rope_base = 500000.0
neg_fill = -1e30


def norm_stat(values):
    return lax.rsqrt(jnp.mean(values * values, axis=-1, keepdims=True) + norm_eps)


def norm_back(values, scale, gain, grad_out):
    weighted = grad_out * gain
    grad_values = scale * weighted - values * (scale * scale * scale) * jnp.mean(
        weighted * values, axis=-1, keepdims=True
    )
    grad_gain = jnp.sum(grad_out * (values * scale), axis=0)
    return (grad_values, grad_gain)


def rotate_half(values):
    half_width = values.shape[-1] // 2
    return jnp.concatenate([-values[..., half_width:], values[..., :half_width]], axis=-1)


def rope_tables(positions, width):
    half_width = width // 2
    inverse = rope_base ** (-(jnp.arange(half_width, dtype=jnp.float32) * 2.0) / width)
    angle = positions.astype(jnp.float32)[:, None] * inverse[None, :]
    cosine = jnp.concatenate([jnp.cos(angle), jnp.cos(angle)], axis=-1)
    sine = jnp.concatenate([jnp.sin(angle), jnp.sin(angle)], axis=-1)
    return (cosine[:, None, :], sine[:, None, :])


def apply_rope(values, cosine, sine):
    shaped = values.reshape(values.shape[0], HEADS, HEAD_DIM)
    return shaped * cosine + rotate_half(shaped) * sine


def rope_back(grads, cosine, sine):
    shaped = grads.reshape(grads.shape[0], HEADS, HEAD_DIM)
    return (shaped * cosine - rotate_half(shaped * sine)).reshape(grads.shape)


def shards(
    hidden_in,
    block_order,
    w_query,
    w_key,
    w_value,
    w_output,
    w_gate,
    w_up,
    w_down,
    norm_gains,
    out_grad,
):
    num_rows = hidden_in.shape[1]
    width = hidden_in.shape[2]
    block_rows = num_rows // 2
    seq_rows = num_rows * lax.axis_size("ctx")
    score_scale = HEAD_DIM ** (-0.5)
    tokens_b = hidden_in[0]
    tokens_f = tokens_b.astype(jnp.float32)
    full_query, full_key, full_value, full_output, gains_b = (
        lax.all_gather(w_query, "fsdp", axis=0, tiled=True),
        lax.all_gather(w_key, "fsdp", axis=0, tiled=True),
        lax.all_gather(w_value, "fsdp", axis=0, tiled=True),
        lax.all_gather(w_output, "fsdp", axis=0, tiled=True),
        lax.all_gather(norm_gains, "fsdp", axis=1, tiled=True),
    )
    gains = gains_b.astype(jnp.float32)
    offsets = jnp.arange(block_rows, dtype=jnp.int32)
    all_pos = (block_order[0][:, None] * block_rows + offsets[None, :]).reshape(seq_rows)
    own_pos = lax.dynamic_slice_in_dim(all_pos, lax.axis_index("ctx") * num_rows, num_rows)
    cosine, sine = rope_tables(own_pos, HEAD_DIM)
    query_raw = jnp.dot(tokens_b, full_query, preferred_element_type=jnp.float32)
    key_raw = jnp.dot(tokens_b, full_key, preferred_element_type=jnp.float32)
    query_scale = norm_stat(query_raw)
    key_scale = norm_stat(key_raw)
    query_heads = apply_rope(query_raw * query_scale * gains[0], cosine, sine).astype(jnp.bfloat16)
    key_b = (
        apply_rope(key_raw * key_scale * gains[1], cosine, sine)
        .astype(jnp.bfloat16)
        .reshape(num_rows, width)
    )
    value_b = jnp.dot(tokens_b, full_value, preferred_element_type=jnp.float32).astype(jnp.bfloat16)
    key_all, value_all = (
        lax.all_gather(key_b, "ctx", axis=0, tiled=True),
        lax.all_gather(value_b, "ctx", axis=0, tiled=True),
    )
    query_major = query_heads.transpose(1, 0, 2)
    key_major = key_all.reshape(seq_rows, HEADS, HEAD_DIM).transpose(1, 0, 2)
    value_major = value_all.reshape(seq_rows, HEADS, HEAD_DIM).transpose(1, 0, 2)
    allowed = all_pos[None, :] <= own_pos[:, None]

    def head_scores(query_one, key_one):
        raw_scores = jnp.dot(query_one, key_one.T, preferred_element_type=jnp.float32) * score_scale
        return jnp.where(allowed, raw_scores, neg_fill)

    def head_forward(items):
        query_one, key_one, value_one = items
        scores = head_scores(query_one, key_one)
        peak = jnp.max(scores, axis=-1, keepdims=True)
        expd = jnp.exp(scores - peak)
        denom = jnp.sum(expd, axis=-1, keepdims=True)
        probs = expd / denom
        mixed_one = jnp.dot(
            probs.astype(jnp.bfloat16), value_one, preferred_element_type=jnp.float32
        )
        return (mixed_one, peak + jnp.log(denom))

    mixed_major, log_total = lax.map(head_forward, (query_major, key_major, value_major))
    mixed_b = mixed_major.transpose(1, 0, 2).reshape(num_rows, width).astype(jnp.bfloat16)
    projected = jnp.dot(mixed_b, full_output, preferred_element_type=jnp.float32)
    proj_scale = norm_stat(projected)
    residual = tokens_f + projected * proj_scale * gains[2]
    residual_b = residual.astype(jnp.bfloat16)
    gate_w, up_w, down_w = (w_gate, w_up, w_down)
    mlp_rows_in = lax.all_gather(residual_b, "fsdp", axis=0, tiled=True)
    gate = jnp.dot(mlp_rows_in, gate_w, preferred_element_type=jnp.float32)
    upward = jnp.dot(mlp_rows_in, up_w, preferred_element_type=jnp.float32)
    sigma = jax.nn.sigmoid(gate)
    hidden_b = (gate * sigma * upward).astype(jnp.bfloat16)
    partial_out = jnp.dot(hidden_b, down_w, preferred_element_type=jnp.float32)
    mlp_out = lax.psum_scatter(partial_out, "fsdp", scatter_dimension=0, tiled=True)
    mlp_scale = norm_stat(mlp_out)
    block_out = residual + mlp_out * mlp_scale * gains[3]
    grad_y = out_grad[0].astype(jnp.float32)
    grad_mlp, gain_ff = norm_back(mlp_out, mlp_scale, gains[3], grad_y)
    grad_mlp_b = grad_mlp.astype(jnp.bfloat16)
    grad_rows = lax.all_gather(grad_mlp_b, "fsdp", axis=0, tiled=True)
    grad_hidden = jnp.dot(grad_rows, down_w.T, preferred_element_type=jnp.float32)
    grad_gate_b = (grad_hidden * upward * sigma * (1.0 + gate * (1.0 - sigma))).astype(jnp.bfloat16)
    grad_up_b = (grad_hidden * (gate * sigma)).astype(jnp.bfloat16)
    back_part = jnp.dot(grad_gate_b, gate_w.T, preferred_element_type=jnp.float32) + jnp.dot(
        grad_up_b, up_w.T, preferred_element_type=jnp.float32
    )
    grad_mlp_in = lax.psum_scatter(back_part, "fsdp", scatter_dimension=0, tiled=True)
    gate_grad_own = jnp.dot(mlp_rows_in.T, grad_gate_b, preferred_element_type=jnp.float32)
    up_grad_own = jnp.dot(mlp_rows_in.T, grad_up_b, preferred_element_type=jnp.float32)
    down_grad_own = jnp.dot(hidden_b.T, grad_rows, preferred_element_type=jnp.float32)
    grad_res = grad_y + grad_mlp_in
    grad_proj, gain_attn = norm_back(projected, proj_scale, gains[2], grad_res)
    grad_proj_b = grad_proj.astype(jnp.bfloat16)
    grad_mixed_b = jnp.dot(grad_proj_b, full_output.T, preferred_element_type=jnp.float32).astype(
        jnp.bfloat16
    )
    grad_mixed_major = grad_mixed_b.reshape(num_rows, HEADS, HEAD_DIM).transpose(1, 0, 2)

    def head_backward(items):
        query_one, key_one, value_one, grad_one, total_one = items
        probs_again = jnp.exp(head_scores(query_one, key_one) - total_one)
        grad_probs = jnp.dot(grad_one, value_one.T, preferred_element_type=jnp.float32)
        grad_value_one = jnp.dot(
            probs_again.astype(jnp.bfloat16).T, grad_one, preferred_element_type=jnp.float32
        )
        grad_scores_b = (
            probs_again * (grad_probs - jnp.sum(probs_again * grad_probs, axis=-1, keepdims=True))
        ).astype(jnp.bfloat16)
        grad_query_one = (
            jnp.dot(grad_scores_b, key_one, preferred_element_type=jnp.float32) * score_scale
        )
        grad_key_one = (
            jnp.dot(grad_scores_b.T, query_one, preferred_element_type=jnp.float32) * score_scale
        )
        return (grad_query_one, grad_key_one, grad_value_one)

    grad_query_major, grad_key_major, grad_value_major = lax.map(
        head_backward, (query_major, key_major, value_major, grad_mixed_major, log_total)
    )
    grad_queries = grad_query_major.transpose(1, 0, 2).reshape(num_rows, width)
    grad_key_all = grad_key_major.transpose(1, 0, 2).reshape(seq_rows, width)
    grad_value_all = grad_value_major.transpose(1, 0, 2).reshape(seq_rows, width)
    grad_keys, grad_values = (
        lax.psum_scatter(grad_key_all, "ctx", scatter_dimension=0, tiled=True),
        lax.psum_scatter(grad_value_all, "ctx", scatter_dimension=0, tiled=True),
    )
    grad_value_b = grad_values.astype(jnp.bfloat16)
    grad_key_raw, gain_key = norm_back(
        key_raw, key_scale, gains[1], rope_back(grad_keys, cosine, sine)
    )
    grad_query_raw, gain_query = norm_back(
        query_raw, query_scale, gains[0], rope_back(grad_queries, cosine, sine)
    )
    grad_key_b = grad_key_raw.astype(jnp.bfloat16)
    grad_query_b = grad_query_raw.astype(jnp.bfloat16)
    input_grad = grad_res + jnp.dot(grad_query_b, full_query.T, preferred_element_type=jnp.float32)
    input_grad = input_grad + jnp.dot(grad_key_b, full_key.T, preferred_element_type=jnp.float32)
    input_grad = input_grad + jnp.dot(
        grad_value_b, full_value.T, preferred_element_type=jnp.float32
    )
    stacked_in = jnp.concatenate([grad_query_b, grad_key_b, grad_value_b], axis=1)
    attn_stack = lax.psum_scatter(
        jnp.concatenate(
            [
                jnp.dot(tokens_b.T, stacked_in, preferred_element_type=jnp.float32),
                jnp.dot(mixed_b.T, grad_proj_b, preferred_element_type=jnp.float32),
            ],
            axis=1,
        ).astype(jnp.bfloat16),
        "fsdp",
        scatter_dimension=0,
        tiled=True,
    )
    gain_stack = jnp.stack([gain_query, gain_key, gain_attn, gain_ff], axis=0)
    gain_total = lax.psum(gain_stack, ("ctx", "fsdp"))
    gain_width = gain_total.shape[1] // lax.axis_size("fsdp")
    gain_own = lax.dynamic_slice_in_dim(
        gain_total, lax.axis_index("fsdp") * gain_width, gain_width, 1
    )
    attn_summed, gate_summed, up_summed, down_summed = (
        lax.psum(attn_stack, "ctx").astype(jnp.float32),
        lax.psum(gate_grad_own.astype(jnp.bfloat16), "ctx").astype(jnp.float32),
        lax.psum(up_grad_own.astype(jnp.bfloat16), "ctx").astype(jnp.float32),
        lax.psum(down_grad_own.astype(jnp.bfloat16), "ctx").astype(jnp.float32),
    )
    return (
        block_out.astype(jnp.bfloat16)[None],
        input_grad[None],
        attn_summed[:, :width],
        attn_summed[:, width : 2 * width],
        attn_summed[:, 2 * width : 3 * width],
        attn_summed[:, 3 * width :],
        gate_summed,
        up_summed,
        down_summed,
        gain_own,
    )


def solution(mesh):
    return jax.shard_map(
        shards,
        mesh=mesh,
        in_specs=(
            P("fsdp", "ctx", None),
            P("fsdp", None),
            P("fsdp", None),
            P("fsdp", None),
            P("fsdp", None),
            P("fsdp", None),
            P(None, "fsdp"),
            P(None, "fsdp"),
            P("fsdp", None),
            P(None, "fsdp"),
            P("fsdp", "ctx", None),
        ),
        out_specs=(
            P("fsdp", "ctx", None),
            P("fsdp", "ctx", None),
            P("fsdp", None),
            P("fsdp", None),
            P("fsdp", None),
            P("fsdp", None),
            P(None, "fsdp"),
            P(None, "fsdp"),
            P("fsdp", None),
            P(None, "fsdp"),
        ),
        check_vma=False,
    )
```

profile of v0, /device:TPU:0, one launch (start us, length us, event | category | flops | bytes accessed | tf_op | source)
XLA Modules:
  0.0 1702.8 jit_solution(14575378265479232911)
XLA Ops:
  10.3 14.6 all_gather.28
  25.4 69.0 %all-gather.15.cloned.1.call-done = bf16[2048,2048]{1,0:T(8,128)(2,1)} async-done(((bf16[256,2048]{1,0:T(8,128)(2,1)}), bf16[2048,2048]{1,0:T(8,128)(2,1)}) %all-gather.15.cloned.1.call-update) | async-done | bytes 8388624 | tf_op jit(solution)/shard_map/all_gather | solution.py:75
  99.9 76.6 %all-gather.11.cloned.1.call-done = bf16[2048,2048]{1,0:T(8,128)(2,1)} async-done(((bf16[256,2048]{1,0:T(8,128)(2,1)}), bf16[2048,2048]{1,0:T(8,128)(2,1)}) %all-gather.11.cloned.1.call-update) | async-done | bytes 8388624 | tf_op jit(solution)/shard_map/all_gather | solution.py:74
  184.2 74.4 %all-gather.9.cloned.1.call-done = bf16[2048,2048]{1,0:T(8,128)(2,1)} async-done(((bf16[256,2048]{1,0:T(8,128)(2,1)}), bf16[2048,2048]{1,0:T(8,128)(2,1)}) %all-gather.9.cloned.1.call-update) | async-done | bytes 8388624 | tf_op jit(solution)/shard_map/all_gather | solution.py:73
  269.3 25.3 %all-gather.17.cloned.1.call-done = bf16[512,2048]{1,0:T(8,128)(2,1)} async-done(((bf16[128,2048]{1,0:T(8,128)(2,1)}), bf16[512,2048]{1,0:T(8,128)(2,1)}) %all-gather.17.cloned.1.call-update) | async-done | bytes 2097168 | tf_op jit(solution)/shard_map/all_gather | solution.py:97
  298.1 34.0 %all-gather.13.cloned.1.call-done = bf16[512,2048]{1,0:T(8,128)(2,1)} async-done(((bf16[128,2048]{1,0:T(8,128)(2,1)}), bf16[512,2048]{1,0:T(8,128)(2,1)}) %all-gather.13.cloned.1.call-update) | async-done | bytes 2097168 | tf_op jit(solution)/shard_map/all_gather | solution.py:96
  335.6 42.3 %while.28 = (s32[]{:T(128)}, bf16[16,128,128]{1,2,0:T(8,128)(2,1)S(1)}, f32[16,128,1]{1,2,0:T(1,128)S(1)}, bf16[16,128,128]{2,1,0:T(8,128)(2,1)}, bf16[16,512,12...) while((s32[]{:T(128)}, ...), condition=%wide.region_5.6_spmd.clone, body=%wide.region_2.5_spmd.clone.sunk | while | flops 34144128 | bytes 1155689 | solution.py:120
  377.9 37.7 %all-gather.19.cloned.1.call-done = bf16[2048,2048]{1,0:T(8,128)(2,1)} async-done(((bf16[256,2048]{1,0:T(8,128)(2,1)}), bf16[2048,2048]{1,0:T(8,128)(2,1)}) %all-gather.19.cloned.1.call-update) | async-done | bytes 8388624 | tf_op jit(solution)/shard_map/all_gather | solution.py:76
  422.7 45.3 %all-gather.21.cloned.1.call-done = bf16[1024,2048]{1,0:T(8,128)(2,1)} async-done(((bf16[128,2048]{1,0:T(8,128)(2,1)}), bf16[1024,2048]{1,0:T(8,128)(2,1)}) %all-gather.21.cloned.1.call-update) | async-done | bytes 4194320 | tf_op jit(solution)/shard_map/all_gather | solution.py:127
  468.0 7.7 fusion.85
  475.7 6.5 multiply_convert_fusion.3
  483.5 6.7 fusion.86
  490.2 88.4 %reduce-scatter.6.cloned.1.call-done = f32[128,2048]{1,0:T(8,128)} async-done(((f32[1024,2048]{1,0:T(8,128)}), f32[128,2048]{1,0:T(8,128)}) %reduce-scatter.6.cloned.1.call-update) | async-done | bytes 1048592 | tf_op jit(solution)/shard_map/reduce_scatter | solution.py:133
  584.4 45.0 %all-gather.23.cloned.1.call-done = bf16[1024,2048]{1,0:T(8,128)(2,1)} async-done(((bf16[128,2048]{1,0:T(8,128)(2,1)}), bf16[1024,2048]{1,0:T(8,128)(2,1)}) %all-gather.23.cloned.1.call-update) | async-done | bytes 4194320 | tf_op jit(solution)/shard_map/all_gather | solution.py:139
  629.5 13.0 multiply_convert_fusion.1
  642.5 7.0 fusion.87
  649.5 6.8 convolution_add_fusion
  656.6 88.3 %reduce-scatter.8.cloned.1.call-done = f32[128,2048]{1,0:T(8,128)} async-done(((f32[1024,2048]{1,0:T(8,128)}), f32[128,2048]{1,0:T(8,128)}) %reduce-scatter.8.cloned.1.call-update) | async-done | bytes 1048592 | tf_op jit(solution)/shard_map/reduce_scatter | solution.py:146
  750.0 6.5 fusion.56
  757.4 120.4 %while.29 = (s32[]{:T(128)}, f32[16,128,128]{2,1,0:T(8,128)}, f32[16,512,128]{2,1,0:T(8,128)}, f32[16,512,128]{2,1,0:T(8,128)}, bf16[16,128,128]{2,1,0:T(8,128)(...) while((s32[]{:T(128)}, f32[16,128,128]{2,1,0:T(8,128)}, ...), condition=%wide.region_14.15_spmd.clone, body=%wide.region_12.14_spmd.clone.sunk | while | flops 84623232 | bytes 3090561 | solution.py:176
  897.4 36.3 %reduce-scatter.10.cloned.1.call-done = f32[128,2048]{1,0:T(8,128)} async-done(((f32[512,2048]{1,0:T(8,128)}), f32[128,2048]{1,0:T(8,128)}) %reduce-scatter.10.cloned.1.call-update) | async-done | bytes 1048592 | tf_op jit(solution)/shard_map/reduce_scatter | solution.py:183
  936.8 52.9 %reduce-scatter.12.cloned.1.call-done = f32[128,2048]{1,0:T(8,128)} async-done(((f32[512,2048]{1,0:T(8,128)}), f32[128,2048]{1,0:T(8,128)}) %reduce-scatter.12.cloned.1.call-update) | async-done | bytes 1048592 | tf_op jit(solution)/shard_map/reduce_scatter | solution.py:184
  991.1 11.8 convert_bitcast_fusion
  1002.9 23.9 %pad_maximum_fusion = bf16[2048,8192]{0,1:T(8,128)(2,1)} fusion(bf16[2048,2048]{0,1:T(8,128)(2,1)} %convolution_convert_fusion, bf16[2048,6144]{0,1:T(8,128)(2,1)} %convert_bitcast_fusion), kind=kLoop, calls=%fused_computation.57 | loop fusion | flops 67108864 | bytes 67108864 | tf_op jit(solution)/shard_map/concatenate | solution.py:202
  1027.1 9.6 convolution_convert_fusion.1
  1049.1 303.3 %reduce-scatter.14.cloned.1.call-done = bf16[256,8192]{0,1:T(8,128)(2,1)} async-done(((bf16[2048,8192]{0,1:T(8,128)(2,1)}), bf16[256,8192]{0,1:T(8,128)(2,1)}) %reduce-scatter.14.cloned.1.call-update) | async-done | bytes 4194320 | tf_op jit(solution)/shard_map/reduce_scatter | solution.py:201
  1353.7 7.2 convolution_add_fusion.3
  1361.0 39.4 %psum.39 = f32[4,2048]{1,0:T(4,128)S(1)} all-reduce(f32[4,2048]{1,0:T(4,128)S(1)} %pad_maximum_fusion.3), channel_id=1, replica_groups=mesh['ctx'=4,'fsdp'=8] {'ctx','fsdp'}, use_global_device_ids=true, to_apply=%region_28.29 | all-reduce | flops 8192 | bytes 65536 | tf_op jit(solution)/shard_map/psum | solution.py:214
  1401.0 6.9 convolution_add_fusion.2
  1407.9 7.3 fusion.48
  1415.2 249.5 %all-reduce.3.cloned.1.call-done = (bf16[256,8192]{0,1:T(8,128)(2,1)}, bf16[2048,1024]{1,0:T(8,128)(2,1)}, bf16[2048,1024]{1,0:T(8,128)(2,1)}, bf16[1024,2048]{1,0:T(8,128)(2,1)}) async-done(((bf16[256,8192]{0,1:T(8,128)(2,1)}, bf16[2048,1024]{1,0:T(8,128)(2,1)}, bf16[2048,1024]{1,0:T(8,128)(2,1)}, bf16[1024,2048]{1,0:T(8,128)(2,1)}), (bf16[256,8192]{0,1:T(8,128)(2,1)}, bf16[2048,1024]{1,0:T(8,128)(2,1)}, ...) | async-done | bytes 16777232 | tf_op jit(solution)/shard_map/psum | solution.py:220
  1680.2 6.8 convert_element_type.122
  (326 shorter events, 279.6 us)
Async XLA Ops:
  7.2 87.2 %copy-start = (bf16[1,128,2048]{2,1,0:T(8,128)(2,1)S(1)}, bf16[1,128,2048]{2,1,0:T(8,128)(2,1)}, u32[]{:S(2)}) copy-start(bf16[1,128,2048]{2,1,0:T(8,128)(2,1)} %param.15) | copy-start | bytes 1572868
  7.2 87.2 %all-gather.15.cloned.1.call-start = ((), (), s32[]{:S(2)}) async-start(), calls=%async_computation.8 | async-start | bytes 9437184 | tf_op jit(solution)/shard_map/all_gather | solution.py:75
  7.9 168.6 %all-gather.11.cloned.1.call-start = ((), (), s32[]{:S(2)}) async-start(), calls=%async_computation.6 | async-start | bytes 9437184 | tf_op jit(solution)/shard_map/all_gather | solution.py:74
  8.7 250.0 %all-gather.9.cloned.1.call-start = ((), (), s32[]{:S(2)}) async-start(), calls=%async_computation.5 | async-start | bytes 9437184 | tf_op jit(solution)/shard_map/all_gather | solution.py:73
  9.4 285.3 %all-gather.17.cloned.1.call-start = ((), (), s32[]{:S(2)}) async-start(), calls=%async_computation.9 | async-start | bytes 2621440 | tf_op jit(solution)/shard_map/all_gather | solution.py:97
  99.8 232.3 %all-gather.13.cloned.1.call-start = ((), (), s32[]{:S(2)}) async-start(), calls=%async_computation.7 | async-start | bytes 2621440 | tf_op jit(solution)/shard_map/all_gather | solution.py:96
  258.7 5.0 copy-start.16
  268.7 147.0 %all-gather.19.cloned.1.call-start = ((), (), s32[]{:S(2)}) async-start(), calls=%async_computation.10 | async-start | bytes 9437184 | tf_op jit(solution)/shard_map/all_gather | solution.py:76
  269.3 198.7 %all-gather.21.cloned.1.call-start = ((), (), s32[]{:S(2)}) async-start(), calls=%async_computation.11 | async-start | bytes 4718592 | tf_op jit(solution)/shard_map/all_gather | solution.py:127
  377.9 42.5 %copy-start.10 = (bf16[16,128,128]{1,2,0:T(8,128)(2,1)}, bf16[16,128,128]{1,2,0:T(8,128)(2,1)S(1)}, u32[]{:S(2)}) copy-start(bf16[16,128,128]{1,2,0:T(8,128)(2,1)S(1)} %get-tuple-element.102) | copy-start | bytes 1572868
  422.4 156.2 %reduce-scatter.6.cloned.1.call-start = ((), (), s32[]{:S(2)}) async-start(), calls=%async_computation.12 | async-start | bytes 9437184 | tf_op jit(solution)/shard_map/reduce_scatter | solution.py:133
  468.0 7.7 copy-start.19
  468.0 7.7 copy-start.21
  475.7 6.5 copy-start.26
  475.7 7.8 copy-start.17
  490.2 89.9 %copy-start.2 = (bf16[1,128,2048]{2,1,0:T(8,128)(2,1)S(1)}, bf16[1,128,2048]{2,1,0:T(8,128)(2,1)}, u32[]{:S(2)}) copy-start(bf16[1,128,2048]{2,1,0:T(8,128)(2,1)} %param.25) | copy-start | bytes 1572868
  490.2 139.3 %all-gather.23.cloned.1.call-start = ((), (), s32[]{:S(2)}) async-start(), calls=%async_computation.13 | async-start | bytes 4718592 | tf_op jit(solution)/shard_map/all_gather | solution.py:139
  584.0 160.9 %reduce-scatter.8.cloned.1.call-start = ((), (), s32[]{:S(2)}) async-start(), calls=%async_computation.14 | async-start | bytes 9437184 | tf_op jit(solution)/shard_map/reduce_scatter | solution.py:146
  629.5 13.0 copy-start.18
  642.5 7.0 copy-start.24
  642.5 7.0 copy-start.20
  656.3 277.4 %reduce-scatter.10.cloned.1.call-start = ((), (), s32[]{:S(2)}) async-start(), calls=%async_computation.15 | async-start | bytes 5242880 | tf_op jit(solution)/shard_map/reduce_scatter | solution.py:183
  750.0 6.5 copy-start.8
  882.5 107.2 %reduce-scatter.12.cloned.1.call-start = ((), (), s32[]{:S(2)}) async-start(), calls=%async_computation.16 | async-start | bytes 5242880 | tf_op jit(solution)/shard_map/reduce_scatter | solution.py:184
  887.4 465.1 %reduce-scatter.14.cloned.1.call-start = ((), (), s32[]{:S(2)}) async-start(), calls=%async_computation.17 | async-start | bytes 37748736 | tf_op jit(solution)/shard_map/reduce_scatter | solution.py:201
  935.6 55.5 %copy-start.7 = (bf16[128,2048]{1,0:T(8,128)(2,1)S(1)}, bf16[128,2048]{1,0:T(8,128)(2,1)}, u32[]{:S(2)}) copy-start(bf16[128,2048]{1,0:T(8,128)(2,1)} %subtract_convert_fusion.1) | copy-start | bytes 1572868
  1026.8 637.9 %all-reduce.3.cloned.1.call-start = ((), (), s32[]{:S(2)}) async-start(), calls=%async_computation.18 | async-start | bytes 33554432 | tf_op jit(solution)/shard_map/psum | solution.py:220
  1027.1 9.6 copy-start.22
  1027.1 9.6 copy-start.25
  1036.7 6.2 copy-start.27
  1680.2 6.8 copy-start.13
  1687.0 4.4 copy-start.12
  (10 other events, 13.7 us)
Sparse Core Ops, SparseCore 0:
  9.6 84.7 all-gather.14
  96.0 80.5 all-gather.10
  178.1 80.5 all-gather.8
  261.0 33.6 all-gather.16
  296.9 35.1 all-gather.12
  333.6 82.0 all-gather.18
  422.6 45.3 all-gather.20
  490.3 88.3 reduce-scatter.5
  584.1 45.3 all-gather.22
  656.4 88.3 reduce-scatter.7
  882.6 51.0 reduce-scatter.9
  937.1 52.5 reduce-scatter.11
  1027.0 325.4 reduce-scatter.13
  1357.5 307.2 all-reduce.2
where the time goes:
time: 1720 us; the launch traced here: 1700 us
  waiting for transfers between devices  1230 us (72%)
  matrix products  292 us (17%)
  other arithmetic  69.6 us (4%)
  blocking collectives  54 us (3%)
  local copies, waits for them, and re-layouts  41.3 us (2%)
    reduce_scatter x1, waiting for transfers between devices, shards(): lax.psum_scatter(jnp.concatenate([jnp.dot(tokens_b.T, stacked_in, preferr...  303 us
    psum x1, waiting for transfers between devices, shards(): lax.psum(attn_stack, 'ctx').astype(jnp.float32)  250 us
    reduce_scatter x1, waiting for transfers between devices, shards(): lax.psum_scatter(partial_out, 'fsdp', scatter_dimension=0, tiled=True)  88.4 us
    reduce_scatter x1, waiting for transfers between devices, shards(): lax.psum_scatter(back_part, 'fsdp', scatter_dimension=0, tiled=True)  88.3 us
    all_gather x1, waiting for transfers between devices, shards(): lax.all_gather(w_key, 'fsdp', axis=0, tiled=True)  76.6 us
    all_gather x1, waiting for transfers between devices, shards(): lax.all_gather(w_query, 'fsdp', axis=0, tiled=True)  74.4 us
    all_gather x1, waiting for transfers between devices, shards(): lax.all_gather(w_value, 'fsdp', axis=0, tiled=True)  69 us
    reduce_scatter x1, waiting for transfers between devices, shards(): lax.psum_scatter(grad_value_all, 'ctx', scatter_dimension=0, tiled=True)  52.9 us
  transfers between devices with their start and end apart: 14, of which 14 were waited for; matrix products, arithmetic and copies ran while one was open for 8% of the time, Pallas kernels for 0%

commit v1 on v0

v1 whole, which is shorter than its diff:
```python
import functools

import jax
import jax.numpy as jnp
from jax import lax
from jax.experimental import pallas as pl
from jax.experimental.pallas import tpu as pltpu
from jax.sharding import PartitionSpec as P

HEADS = 16
HEAD_DIM = 128

norm_eps = 1e-06
rope_base = 500000.0
neg_fill = -1e30

MESH = pl.DeviceIdType.MESH
f32 = jnp.float32
bf16 = jnp.bfloat16


def anywhere():
    return pl.BlockSpec(memory_space=pl.ANY)


def in_vmem():
    return pl.BlockSpec(memory_space=pltpu.VMEM)


def remote(source, target, sent, landed, where):
    return pltpu.make_async_remote_copy(
        src_ref=source,
        dst_ref=target,
        send_sem=sent,
        recv_sem=landed,
        device_id=where,
        device_id_type=MESH,
    )


def exchange_kernel(axis, size, scatter, count, *refs):
    given, kept = refs[:count], refs[count : 2 * count]
    own_sem, send_sem, land_sem = refs[2 * count :]
    own = lax.axis_index(axis)
    barrier = pltpu.get_barrier_semaphore()
    for step in range(1, size):
        pl.semaphore_signal(
            barrier, inc=1, device_id={axis: lax.rem(own + step, size)}, device_id_type=MESH
        )
    local = []
    for item in range(count):
        source = given[item].at[own] if scatter else given[item]
        local.append(pltpu.make_async_copy(source, kept[item].at[own], own_sem.at[item]))
        local[-1].start()
    pl.semaphore_wait(barrier, size - 1)
    copies = []
    for step in range(1, size):
        peer = lax.rem(own + step, size)
        for item in range(count):
            source = given[item].at[peer] if scatter else given[item]
            copies.append(
                remote(
                    source,
                    kept[item].at[own],
                    send_sem.at[item, step],
                    land_sem.at[item, step],
                    {axis: peer},
                )
            )
            copies[-1].start()
    for copy in local:
        copy.wait()
    for copy in copies:
        copy.wait()


def exchange(axis, arrays, key, scatter=True):
    size = lax.axis_size(axis)
    count = len(arrays)
    shapes = [
        jax.ShapeDtypeStruct(item.shape if scatter else (size,) + item.shape, item.dtype)
        for item in arrays
    ]
    return pl.pallas_call(
        functools.partial(exchange_kernel, axis, size, scatter, count),
        out_shape=shapes,
        in_specs=[in_vmem()] * count,
        out_specs=[anywhere()] * count,
        scratch_shapes=[
            pltpu.SemaphoreType.DMA((count,)),
            pltpu.SemaphoreType.DMA((count, size)),
            pltpu.SemaphoreType.DMA((count, size)),
        ],
        compiler_params=pltpu.CompilerParams(collective_id=key, has_side_effects=True),
        name=f"exchange_{axis}_{key}",
    )(*arrays)


def greet_line(own, chips):
    chip, core = own // 2, own % 2
    barrier = pltpu.get_barrier_semaphore()

    def greet(place):
        pl.semaphore_signal(barrier, inc=1, device_id={"fsdp": place}, device_id_type=MESH)

    greet(chip * 2 + 1 - core)

    @pl.when(chip > 0)
    def _():
        greet(own - 2)

    @pl.when(chip < chips - 1)
    def _():
        greet(own + 2)

    expected = 1 + jnp.minimum(chip, 1) + jnp.minimum(chips - 1 - chip, 1)
    pl.semaphore_wait(barrier, expected)


def gather_kernel(chips, given, kept, own_sem, send_sem, land_sem):
    own = lax.axis_index("fsdp")
    chip, core = own // 2, own % 2
    sibling = chip * 2 + 1 - core
    local = pltpu.make_async_copy(given, kept.at[own], own_sem)
    local.start()
    greet_line(own, chips)

    def copy(source, place, way, step, target):
        return remote(
            source, kept.at[place], send_sem.at[way, step], land_sem.at[place], {"fsdp": target}
        )

    @pl.when(chip < chips - 1)
    def _():
        copy(given, own, 0, 0, own + 2).start()

    @pl.when(chip > 0)
    def _():
        copy(given, own, 1, 0, own - 2).start()

    copy(given, own, 2, 0, sibling).start()
    local.wait()
    for step in range(1, chips):
        from_left, from_right = own - 2 * step, own + 2 * step

        @pl.when(chip >= step)
        def _():
            copy(kept.at[from_left], from_left, 0, step, own).wait_recv()

            @pl.when(chip < chips - 1)
            def _():
                copy(kept.at[from_left], from_left, 0, step, own + 2).start()

            copy(kept.at[from_left], from_left, 2, step, sibling).start()

        @pl.when(chip + step < chips)
        def _():
            copy(kept.at[from_right], from_right, 1, step, own).wait_recv()

            @pl.when(chip > 0)
            def _():
                copy(kept.at[from_right], from_right, 1, step, own - 2).start()

            copy(kept.at[from_right], from_right, 3, step, sibling).start()

    for other in range(chips):
        place = other * 2 + 1 - core
        copy(kept.at[place], place, 2, 0, sibling).wait_recv()

    @pl.when(chip < chips - 1)
    def _():
        copy(given, own, 0, 0, own + 2).wait_send()

    @pl.when(chip > 0)
    def _():
        copy(given, own, 1, 0, own - 2).wait_send()

    copy(given, own, 2, 0, sibling).wait_send()
    for step in range(1, chips):
        from_left, from_right = own - 2 * step, own + 2 * step

        @pl.when(chip >= step)
        def _():
            @pl.when(chip < chips - 1)
            def _():
                copy(kept.at[from_left], from_left, 0, step, own + 2).wait_send()

            copy(kept.at[from_left], from_left, 2, step, sibling).wait_send()

        @pl.when(chip + step < chips)
        def _():
            @pl.when(chip > 0)
            def _():
                copy(kept.at[from_right], from_right, 1, step, own - 2).wait_send()

            copy(kept.at[from_right], from_right, 3, step, sibling).wait_send()


def gather_line(shard, key):
    size = lax.axis_size("fsdp")
    chips = size // 2
    kept = pl.pallas_call(
        functools.partial(gather_kernel, chips),
        out_shape=jax.ShapeDtypeStruct((size,) + shard.shape, shard.dtype),
        in_specs=[in_vmem()],
        out_specs=anywhere(),
        scratch_shapes=[
            pltpu.SemaphoreType.DMA,
            pltpu.SemaphoreType.DMA((4, chips)),
            pltpu.SemaphoreType.DMA((size,)),
        ],
        compiler_params=pltpu.CompilerParams(collective_id=key, has_side_effects=True),
        name=f"gather_line_{key}",
    )(shard)
    return kept.reshape((size * shard.shape[0],) + shard.shape[1:])


def reduce_kernel(
    chips,
    wire,
    given,
    total,
    mine,
    beside,
    from_left,
    from_right,
    outgoing,
    load_sem,
    side_send,
    side_land,
    line_send,
    left_land,
    right_land,
):
    own = lax.axis_index("fsdp")
    chip, core = own // 2, own % 2
    sibling = chip * 2 + 1 - core

    def load(other):
        return pltpu.make_async_copy(given.at[other * 2 + core], mine.at[other], load_sem.at[other])

    def side(other):
        return remote(
            given.at[other * 2 + 1 - core],
            beside.at[other],
            side_send.at[other],
            side_land.at[other],
            {"fsdp": sibling},
        )

    def rightward(other, target):
        return remote(
            outgoing.at[other],
            from_left.at[other],
            line_send.at[other],
            left_land.at[other],
            {"fsdp": target},
        )

    def leftward(other, target):
        return remote(
            outgoing.at[other],
            from_right.at[other],
            line_send.at[other],
            right_land.at[other],
            {"fsdp": target},
        )

    for other in range(chips):
        load(other).start()
    greet_line(own, chips)
    for tick in range(chips - 1):
        right_to = chips - 1 - (tick - chip)
        left_to = tick - (chips - 1 - chip)

        @pl.when((tick >= chip) & (right_to > chip))
        def _():
            side(right_to).start()

        @pl.when((left_to >= 0) & (left_to < chip))
        def _():
            side(left_to).start()

    side(chip).start()
    for tick in range(chips - 1):
        right_to = chips - 1 - (tick - chip)
        left_to = tick - (chips - 1 - chip)

        @pl.when((tick >= chip) & (right_to > chip))
        def _():
            load(right_to).wait()
            side(right_to).wait_recv()

            @pl.when(chip > 0)
            def _():
                rightward(right_to, own).wait_recv()
                outgoing[right_to] = (
                    mine[right_to] + beside[right_to] + from_left[right_to].astype(f32)
                ).astype(wire)

            @pl.when(chip == 0)
            def _():
                outgoing[right_to] = (mine[right_to] + beside[right_to]).astype(wire)

            rightward(right_to, own + 2).start()

        @pl.when((left_to >= 0) & (left_to < chip))
        def _():
            load(left_to).wait()
            side(left_to).wait_recv()

            @pl.when(chip < chips - 1)
            def _():
                leftward(left_to, own).wait_recv()
                outgoing[left_to] = (
                    mine[left_to] + beside[left_to] + from_right[left_to].astype(f32)
                ).astype(wire)

            @pl.when(chip == chips - 1)
            def _():
                outgoing[left_to] = (mine[left_to] + beside[left_to]).astype(wire)

            leftward(left_to, own - 2).start()

    load(chip).wait()
    side(chip).wait_recv()
    total[...] = mine[chip] + beside[chip]

    @pl.when(chip > 0)
    def _():
        rightward(chip, own).wait_recv()
        total[...] += from_left[chip].astype(f32)

    @pl.when(chip < chips - 1)
    def _():
        leftward(chip, own).wait_recv()
        total[...] += from_right[chip].astype(f32)

    for other in range(chips):
        side(other).wait_send()

        @pl.when(chip != other)
        def _():
            rightward(other, own).wait_send()


def reduce_line(partial, key, wire=f32):
    size, rows, width = partial.shape
    chips = size // 2
    return pl.pallas_call(
        functools.partial(reduce_kernel, chips, wire),
        out_shape=jax.ShapeDtypeStruct((rows, width), f32),
        in_specs=[anywhere()],
        out_specs=in_vmem(),
        scratch_shapes=[
            pltpu.VMEM((chips, rows, width), f32),
            pltpu.VMEM((chips, rows, width), f32),
            pltpu.VMEM((chips, rows, width), wire),
            pltpu.VMEM((chips, rows, width), wire),
            pltpu.VMEM((chips, rows, width), wire),
            pltpu.SemaphoreType.DMA((chips,)),
            pltpu.SemaphoreType.DMA((chips,)),
            pltpu.SemaphoreType.DMA((chips,)),
            pltpu.SemaphoreType.DMA((chips,)),
            pltpu.SemaphoreType.DMA((chips,)),
            pltpu.SemaphoreType.DMA((chips,)),
        ],
        compiler_params=pltpu.CompilerParams(
            collective_id=key, has_side_effects=True, vmem_limit_bytes=60 * 1024 * 1024
        ),
        name=f"reduce_line_{key}",
    )(partial)


def probs_of(query, key, query_pos, key_pos):
    scores = lax.dot_general(
        query, key, (((1,), (1,)), ((), ())), preferred_element_type=f32
    ) * (HEAD_DIM ** (-0.5))
    scores = jnp.where(key_pos <= query_pos, scores, neg_fill)
    expd = jnp.exp(scores - jnp.max(scores, axis=-1, keepdims=True))
    return expd / jnp.sum(expd, axis=-1, keepdims=True)


def flat(ref):
    return ref[...].reshape(ref.shape[0] * ref.shape[-2], ref.shape[-1])


def attend_kernel(query_ref, key_ref, value_ref, query_pos, key_pos, mixed_ref):
    probs = probs_of(flat(query_ref), flat(key_ref), query_pos[...], key_pos[...])
    mixed_ref[...] = jnp.dot(
        probs.astype(bf16), flat(value_ref), preferred_element_type=f32
    ).astype(bf16)


def attend_back_kernel(
    query_ref,
    key_ref,
    value_ref,
    query_pos,
    key_pos,
    grad_ref,
    grad_query_ref,
    grad_key_ref,
    grad_value_ref,
    key_sum,
    value_sum,
):
    step, steps = pl.program_id(2), pl.num_programs(2)
    score_scale = HEAD_DIM ** (-0.5)
    query, key, value = flat(query_ref), flat(key_ref), flat(value_ref)
    grad = grad_ref[...]
    probs = probs_of(query, key, query_pos[...], key_pos[...])
    grad_probs = lax.dot_general(
        grad, value, (((1,), (1,)), ((), ())), preferred_element_type=f32
    )
    grad_scores = (
        probs * (grad_probs - jnp.sum(probs * grad_probs, axis=-1, keepdims=True))
    ).astype(bf16)
    grad_query_ref[...] = jnp.dot(grad_scores, key, preferred_element_type=f32) * score_scale
    value_part = lax.dot_general(
        probs.astype(bf16), grad, (((0,), (0,)), ((), ())), preferred_element_type=f32
    )
    key_part = lax.dot_general(
        grad_scores, query, (((0,), (0,)), ((), ())), preferred_element_type=f32
    )

    @pl.when(step == 0)
    def _():
        key_sum[...] = key_part
        value_sum[...] = value_part

    @pl.when(step > 0)
    def _():
        key_sum[...] += key_part
        value_sum[...] += value_part

    @pl.when(step == steps - 1)
    def _():
        grad_key_ref[...] = (key_sum[...] * score_scale).reshape(grad_key_ref.shape)
        grad_value_ref[...] = value_sum[...].astype(bf16).reshape(grad_value_ref.shape)


def attention_specs(parts, rows, seq_rows):
    query = pl.BlockSpec((1, None, None, rows, HEAD_DIM), lambda i, h, c: (c, 0, i, 0, h))
    key = pl.BlockSpec((parts, None, None, rows, HEAD_DIM), lambda i, h, c: (0, 1, i, 0, h))
    value = pl.BlockSpec((parts, None, None, rows, HEAD_DIM), lambda i, h, c: (0, 2, i, 0, h))
    query_pos = pl.BlockSpec((None, None, rows, 1), lambda i, h, c: (i, c, 0, 0))
    key_pos = pl.BlockSpec((None, 1, seq_rows), lambda i, h, c: (i, 0, 0))
    row_block = pl.BlockSpec((None, None, rows, HEAD_DIM), lambda i, h, c: (c, i, 0, h))
    all_block = pl.BlockSpec((parts, None, rows, HEAD_DIM), lambda i, h, c: (0, i, 0, h))
    return [query, key, value, query_pos, key_pos], row_block, all_block


def attend(packed, query_pos, key_pos):
    parts, _, pair, rows, width = packed.shape
    seq_rows = parts * rows
    in_specs, row_block, _ = attention_specs(parts, rows, seq_rows)
    return pl.pallas_call(
        attend_kernel,
        grid=(pair, width // HEAD_DIM, parts),
        out_shape=jax.ShapeDtypeStruct((parts, pair, rows, width), bf16),
        in_specs=in_specs,
        out_specs=row_block,
        name="attend",
    )(packed, packed, packed, query_pos, key_pos)


def attend_back(packed, query_pos, key_pos, grad):
    parts, _, pair, rows, width = packed.shape
    seq_rows = parts * rows
    in_specs, row_block, all_block = attention_specs(parts, rows, seq_rows)
    return pl.pallas_call(
        attend_back_kernel,
        grid=(pair, width // HEAD_DIM, parts),
        out_shape=[
            jax.ShapeDtypeStruct((parts, pair, rows, width), f32),
            jax.ShapeDtypeStruct((parts, pair, rows, width), f32),
            jax.ShapeDtypeStruct((parts, pair, rows, width), bf16),
        ],
        in_specs=in_specs + [row_block],
        out_specs=[row_block, all_block, all_block],
        scratch_shapes=[
            pltpu.VMEM((seq_rows, HEAD_DIM), f32),
            pltpu.VMEM((seq_rows, HEAD_DIM), f32),
        ],
        name="attend_back",
    )(packed, packed, packed, query_pos, key_pos, grad)


def norm_stat(values):
    return lax.rsqrt(jnp.mean(values * values, axis=-1, keepdims=True) + norm_eps)


def norm_back(values, scale, gain, grad_out):
    weighted = grad_out * gain
    grad_values = scale * weighted - values * (scale * scale * scale) * jnp.mean(
        weighted * values, axis=-1, keepdims=True
    )
    grad_gain = jnp.sum(grad_out * (values * scale), axis=0)
    return (grad_values, grad_gain)


def rotate_half(values):
    half_width = values.shape[-1] // 2
    return jnp.concatenate([-values[..., half_width:], values[..., :half_width]], axis=-1)


def rope_tables(positions, width):
    half_width = width // 2
    inverse = rope_base ** (-(jnp.arange(half_width, dtype=f32) * 2.0) / width)
    angle = positions.astype(f32)[:, None] * inverse[None, :]
    cosine = jnp.concatenate([jnp.cos(angle), jnp.cos(angle)], axis=-1)
    sine = jnp.concatenate([jnp.sin(angle), jnp.sin(angle)], axis=-1)
    return (cosine[:, None, :], sine[:, None, :])


def by_head(values):
    return values.reshape(values.shape[0], values.shape[1] // HEAD_DIM, HEAD_DIM)


def apply_rope(values, cosine, sine):
    shaped = by_head(values)
    return (shaped * cosine + rotate_half(shaped) * sine).reshape(values.shape)


def rope_back(grads, cosine, sine):
    shaped = by_head(grads)
    return (shaped * cosine - rotate_half(shaped * sine)).reshape(grads.shape)


def mm(left, right):
    return jnp.dot(left, right, preferred_element_type=f32)


def mm_nt(left, right):
    return lax.dot_general(left, right, (((1,), (1,)), ((), ())), preferred_element_type=f32)


def mm_tn(left, right):
    return lax.dot_general(left, right, (((0,), (0,)), ((), ())), preferred_element_type=f32)


def shards(
    hidden_in,
    block_order,
    w_query,
    w_key,
    w_value,
    w_output,
    w_gate,
    w_up,
    w_down,
    norm_gains,
    out_grad,
):
    rows, width = hidden_in.shape[1:]
    parts, owners = lax.axis_size("ctx"), lax.axis_size("fsdp")
    part, owner = lax.axis_index("ctx"), lax.axis_index("fsdp")
    group = owners * rows
    own_width = width // owners
    pair = owners // parts
    blocks = block_order.shape[1]
    block_rows = parts * rows // blocks
    piece = w_query.shape[0] // parts
    tokens_b = hidden_in[0]
    tokens_f = tokens_b.astype(f32)

    small = jnp.concatenate(
        [
            norm_gains.astype(f32),
            jnp.pad(block_order.astype(f32), ((0, 0), (0, own_width - blocks))),
        ],
        axis=0,
    )
    (small_all,) = exchange("fsdp", [small], 0, scatter=False)
    gains = small_all[:, :4].transpose(1, 0, 2).reshape(4, width)
    orders = small_all[:, 4, :blocks].astype(jnp.int32)
    own_gains = norm_gains.astype(f32)
    stacked = jnp.stack(
        [
            lax.dynamic_slice_in_dim(item, part * piece, piece)
            for item in (w_query, w_key, w_value)
        ]
    )
    stacked = stacked.reshape(3, piece, owners, own_width).transpose(2, 1, 0, 3)
    (columns,) = exchange("fsdp", [stacked.reshape(owners, piece, 3 * own_width)], 1)
    (columns,) = exchange("ctx", [columns], 2, scatter=False)
    w_heads = columns.transpose(1, 0, 2, 3).reshape(width, 3 * own_width)
    group_tokens = gather_line(tokens_b, 3)
    full_output = lax.all_gather(w_output, "fsdp", axis=0, tiled=True)

    offsets = jnp.arange(block_rows, dtype=jnp.int32)
    seq_pos = (orders[:, :, None] * block_rows + offsets[None, None, :]).reshape(
        owners, parts * rows
    )
    group_pos = lax.dynamic_slice_in_dim(seq_pos, part * rows, rows, 1).reshape(group)
    pair_pos = lax.dynamic_slice_in_dim(seq_pos, part * pair, pair, 0)
    query_pos = pair_pos.reshape(pair, parts, rows, 1)
    key_pos = pair_pos.reshape(pair, 1, parts * rows)
    cosine, sine = rope_tables(group_pos, HEAD_DIM)

    raw = mm(group_tokens, w_heads)
    query_raw, key_raw = raw[:, :own_width], raw[:, own_width : 2 * own_width]
    values = raw[:, 2 * own_width :].astype(bf16)
    squares = jnp.stack(
        [jnp.sum(query_raw * query_raw, axis=-1), jnp.sum(key_raw * key_raw, axis=-1)]
    )
    (squares,) = exchange("fsdp", [squares], 4, scatter=False)
    scales = lax.rsqrt(jnp.sum(squares, axis=0) / width + norm_eps)
    query_scale, key_scale = scales[0][:, None], scales[1][:, None]
    queries = apply_rope(query_raw * query_scale * own_gains[0], cosine, sine).astype(bf16)
    keys = apply_rope(key_raw * key_scale * own_gains[1], cosine, sine).astype(bf16)
    packed = jnp.stack(
        [item.reshape(parts, pair, rows, own_width) for item in (queries, keys, values)], axis=1
    )
    (packed,) = exchange("ctx", [packed], 5)
    mixed_pair = attend(packed, query_pos, key_pos)
    (mixed_group,) = exchange("ctx", [mixed_pair], 6)
    mixed_group = mixed_group.reshape(owners, rows, own_width)
    (mixed_own,) = exchange("fsdp", [mixed_group], 7)
    mixed_own = mixed_own.transpose(1, 0, 2).reshape(rows, width)
    projected = mm(mixed_own, full_output)
    proj_scale = norm_stat(projected)
    residual = tokens_f + projected * proj_scale * gains[2]
    mlp_rows_in = gather_line(residual.astype(bf16), 8)
    gate = mm(mlp_rows_in, w_gate)
    upward = mm(mlp_rows_in, w_up)
    sigma = jax.nn.sigmoid(gate)
    hidden_b = (gate * sigma * upward).astype(bf16)
    mlp_out = reduce_line(mm(hidden_b, w_down).reshape(owners, rows, width), 9)
    mlp_scale = norm_stat(mlp_out)
    block_out = residual + mlp_out * mlp_scale * gains[3]

    grad_y = out_grad[0].astype(f32)
    grad_mlp, gain_ff = norm_back(mlp_out, mlp_scale, gains[3], grad_y)
    grad_rows = gather_line(grad_mlp.astype(bf16), 10)
    grad_hidden = mm_nt(grad_rows, w_down)
    grad_gate_b = (grad_hidden * upward * sigma * (1.0 + gate * (1.0 - sigma))).astype(bf16)
    grad_up_b = (grad_hidden * (gate * sigma)).astype(bf16)
    down_sum = lax.psum(mm_tn(hidden_b, grad_rows).astype(bf16), "ctx").astype(f32)
    gate_sum = lax.psum(mm_tn(mlp_rows_in, grad_gate_b).astype(bf16), "ctx").astype(f32)
    up_sum = lax.psum(mm_tn(mlp_rows_in, grad_up_b).astype(bf16), "ctx").astype(f32)
    back_part = mm_nt(grad_gate_b, w_gate) + mm_nt(grad_up_b, w_up)
    grad_res = grad_y + reduce_line(back_part.reshape(owners, rows, width), 11)
    grad_proj, gain_attn = norm_back(projected, proj_scale, gains[2], grad_res)
    grad_proj_rows = gather_line(grad_proj.astype(bf16), 12)
    grad_mixed = mm_nt(grad_proj_rows, w_output).astype(bf16)
    (grad_mixed,) = exchange("ctx", [grad_mixed.reshape(parts, pair, rows, own_width)], 13)
    grad_queries, grad_keys, grad_values = exchange(
        "ctx", attend_back(packed, query_pos, key_pos, grad_mixed), 14
    )
    grad_queries = rope_back(grad_queries.reshape(group, own_width), cosine, sine)
    grad_keys = rope_back(grad_keys.reshape(group, own_width), cosine, sine)
    grad_value_b = grad_values.reshape(group, own_width)
    query_weighted, key_weighted = grad_queries * own_gains[0], grad_keys * own_gains[1]
    products = jnp.stack(
        [jnp.sum(query_weighted * query_raw, axis=-1), jnp.sum(key_weighted * key_raw, axis=-1)]
    )
    (products,) = exchange("fsdp", [products], 15, scatter=False)
    means = jnp.sum(products, axis=0) / width
    grad_query_b = (
        query_scale * query_weighted - query_raw * (query_scale**3 * means[0][:, None])
    ).astype(bf16)
    grad_key_b = (
        key_scale * key_weighted - key_raw * (key_scale**3 * means[1][:, None])
    ).astype(bf16)
    gain_query = jnp.sum(grad_queries * (query_raw * query_scale), axis=0)
    gain_key = jnp.sum(grad_keys * (key_raw * key_scale), axis=0)
    grad_heads = jnp.concatenate([grad_query_b, grad_key_b, grad_value_b], axis=1)
    input_grad = grad_res + reduce_line(
        mm_nt(grad_heads, w_heads).reshape(owners, rows, width), 16
    )

    (gain_post,) = exchange(
        "fsdp",
        [jnp.stack([gain_attn, gain_ff]).reshape(2, owners, own_width).transpose(1, 0, 2)],
        17,
    )
    gain_own = jnp.concatenate(
        [gain_query[None], gain_key[None], jnp.sum(gain_post, axis=0)], axis=0
    )
    (gain_own,) = exchange("ctx", [gain_own], 18, scatter=False)
    gain_own = jnp.sum(gain_own, axis=0)

    output_sum = lax.psum(
        mm_tn(mixed_group.reshape(owners, rows, own_width).reshape(group, own_width), grad_proj_rows).astype(bf16),
        "ctx",
    ).astype(f32)
    heads_part = (
        mm_tn(group_tokens, grad_heads)
        .astype(bf16)
        .reshape(owners, parts, piece, 3 * own_width)
        .transpose(1, 0, 2, 3)
    )
    heads_part = lax.psum_scatter(heads_part, "ctx", scatter_dimension=0, tiled=False)
    (heads_part,) = exchange("fsdp", [heads_part], 19)
    heads_all = lax.all_gather(heads_part, "ctx", axis=0)
    heads_all = (
        heads_all.reshape(parts, owners, piece, 3, own_width)
        .transpose(3, 0, 2, 1, 4)
        .reshape(3, parts * piece, width)
        .astype(f32)
    )
    return (
        block_out.astype(bf16)[None],
        input_grad[None],
        heads_all[0],
        heads_all[1],
        heads_all[2],
        output_sum,
        gate_sum,
        up_sum,
        down_sum,
        gain_own,
    )


def solution(mesh):
    return jax.shard_map(
        shards,
        mesh=mesh,
        in_specs=(
            P("fsdp", "ctx", None),
            P("fsdp", None),
            P("fsdp", None),
            P("fsdp", None),
            P("fsdp", None),
            P("fsdp", None),
            P(None, "fsdp"),
            P(None, "fsdp"),
            P("fsdp", None),
            P(None, "fsdp"),
            P("fsdp", "ctx", None),
        ),
        out_specs=(
            P("fsdp", "ctx", None),
            P("fsdp", "ctx", None),
            P("fsdp", None),
            P("fsdp", None),
            P("fsdp", None),
            P("fsdp", None),
            P(None, "fsdp"),
            P(None, "fsdp"),
            P("fsdp", None),
            P(None, "fsdp"),
        ),
        check_vma=False,
    )
```

time: 1720 us -> 1130 us (0.66)
  waiting for transfers between devices: 1230 us -> 187 us
  Pallas kernels: 0 us -> 661 us
  matrix products: 292 us -> 101 us
  blocking collectives: 54 us -> 0 us
  local copies, waits for them, and re-layouts: 41.3 us -> 87.9 us
    pallas_call x0 -> x22, Pallas kernels: none -> 661 us  [the longest x3 238 us: reduce_line(): pl.pallas_call(functools.partial(reduce_kernel, chips, wire), out_shape=j...]
    reduce_scatter x5 -> x0, waiting for transfers between devices: 569 us -> none  [the longest x1 303 us: shards(): lax.psum_scatter(jnp.concatenate([jnp.dot(tokens_b.T, stacked_in, preferr...]
    all_gather x8 -> x2, waiting for transfers between devices: 407 us -> 0.02 us  [the longest x1 0.02 us: shards(): full_output = lax.all_gather(w_output, 'fsdp', axis=0, tiled=True)]
    dot_general x131 -> x15, matrix products: 292 us -> 101 us  [the longest x5 38.6 us: mm_nt(): lax.dot_general(left, right, (((1,), (1,)), ((), ())), preferred_element_...]
    psum x1, waiting for transfers between devices: 250 us -> 142 us  [shards(): lax.psum(mm_tn(mixed_group.reshape(owners, rows, own_width).reshape(group...]
    unnamed x14 -> x5, waiting for transfers between devices: 2.74 us -> 45.1 us
    psum x1 -> x0, blocking collectives: 39.4 us -> none  [shards(): gain_total = lax.psum(gain_stack, ('ctx', 'fsdp'))]
    concatenate x1 -> x4, other arithmetic: 23.9 us -> 3.51 us  [the longest x2 2.29 us: rotate_half(): jnp.concatenate([-values[..., half_width:], values[..., :half_width]], ax...]
  transfers between devices with their start and end apart: 14 -> 4, of which waited for: 14 -> 2; matrix products, arithmetic and copies ran while one was open for 8% -> 11% of each run, Pallas kernels for 0% -> 26%
where the time goes in v1:
time: 1130 us; the launch traced here: 1120 us
  Pallas kernels  661 us (58%)
  waiting for transfers between devices  187 us (17%)
  matrix products  101 us (9%)
  local copies, waits for them, and re-layouts  87.9 us (8%)
  other arithmetic  73 us (6%)
  between operations  14.7 us (1%)
    pallas_call x3, Pallas kernels, reduce_line(): pl.pallas_call(functools.partial(reduce_kernel, chips, wire), out_shape=j...  238 us
    pallas_call x13, Pallas kernels, exchange(): pl.pallas_call(functools.partial(exchange_kernel, axis, size, scatter, co...  210 us
    pallas_call x4, Pallas kernels, gather_line(): pl.pallas_call(functools.partial(gather_kernel, chips), out_shape=jax.Sha...  184 us
    psum x1, waiting for transfers between devices, shards(): lax.psum(mm_tn(mixed_group.reshape(owners, rows, own_width).reshape(group...  142 us
    unnamed x5, waiting for transfers between devices  45.1 us
    dot_general x5, matrix products, mm_nt(): lax.dot_general(left, right, (((1,), (1,)), ((), ())), preferred_element_...  38.6 us
    dot_general x5, matrix products, mm(): return jnp.dot(left, right, preferred_element_type=f32)  32.2 us
    dot_general x5, matrix products, mm_tn(): lax.dot_general(left, right, (((0,), (0,)), ((), ())), preferred_element_...  29.7 us
  transfers between devices with their start and end apart: 4, of which 2 were waited for; matrix products, arithmetic and copies ran while one was open for 11% of the time, Pallas kernels for 26%

profile of v1, /device:TPU:0, one launch (start us, length us, event | category | flops | bytes accessed | tf_op | source)
XLA Modules:
  0.0 1124.3 jit_solution(13380393473741597899)
XLA Ops:
  9.9 8.5 exchange_fsdp_0.1
  25.2 30.6 %exchange_fsdp_1.1.refs_0_ = bf16[8,64,768]{2,1,0:T(8,128)(2,1)} custom-call(bf16[8,64,768]{2,1,0:T(8,128)(2,1)} %reshape.234.refs_0_), custom_call_target="tpu_custom_call" | custom-call | tf_op jit(solution)/shard_map/exchange_fsdp_1/pallas_call | solution.py:84
  55.8 38.3 %exchange_ctx_2.1 = bf16[4,8,64,768]{3,2,1,0:T(8,128)(2,1)} custom-call(bf16[8,64,768]{2,1,0:T(8,128)(2,1)} %exchange_fsdp_1.1.refs_0_), custom_call_target="tpu_custom_call" | custom-call | tf_op jit(solution)/shard_map/exchange_ctx_2/pallas_call | solution.py:84
  98.0 54.5 %gather_line_3.1 = bf16[8,128,2048]{2,1,0:T(8,128)(2,1)} custom-call(bf16[128,2048]{1,0:T(8,128)(2,1)} %bitcast.171), custom_call_target="tpu_custom_call" | custom-call | tf_op jit(solution)/shard_map/gather_line_3/pallas_call | solution.py:202
  163.9 6.4 exchange_fsdp_4.1
  203.5 22.2 %exchange_ctx_5.1.query_ref.key_ref.value_ref = bf16[4,3,2,128,256]{4,3,2,1,0:T(8,128)(2,1)} custom-call(bf16[4,3,2,128,256]{4,3,2,1,0:T(8,128)(2,1)} %pad_maximum_fusion.refs_0_), custom_call_target="tpu_custom_call" | custom-call | tf_op jit(solution)/shard_map/exchange_ctx_5/pallas_call | solution.py:84
  225.8 13.4 %attend.1.refs_0_ = bf16[4,2,128,256]{3,2,1,0:T(8,128)(2,1)} custom-call(bf16[4,3,2,128,256]{4,3,2,1,0:T(8,128)(2,1)} %exchange_ctx_5.1.query_ref.key_ref.value_ref, bf16[4,3,2,128,256]{4,3,2,1,0:T(8,128)(2,1)} %exchange_ctx_5.1.query_ref.key_ref.value_ref, bf16[4,3,2,128,256]{4,3,2,1,0:T(8,128)(2,1)} %exchange_ctx_5.1.query_ref.key_ref.value_ref, ...), custom_call_target="tpu_custom_call" | custom-call | tf_op jit(solution)/shard_map/attend/pallas_call | solution.py:458
  239.2 10.0 exchange_ctx_6.1
  249.2 13.6 %exchange_fsdp_7.1 = bf16[8,128,256]{2,1,0:T(8,128)(2,1)} custom-call(bf16[8,128,256]{2,1,0:T(8,128)(2,1)} %bitcast.190), custom_call_target="tpu_custom_call" | custom-call | tf_op jit(solution)/shard_map/exchange_fsdp_7/pallas_call | solution.py:84
  270.0 45.7 %gather_line_8.1 = bf16[8,128,2048]{2,1,0:T(8,128)(2,1)} custom-call(bf16[128,2048]{1,0:T(8,128)(2,1)} %fusion.25.given), custom_call_target="tpu_custom_call" | custom-call | tf_op jit(solution)/shard_map/gather_line_8/pallas_call | solution.py:202
  315.7 8.0 fusion.40
  323.8 6.5 multiply_convert_fusion.2
  330.3 6.7 fusion.41
  337.0 77.6 %reduce_line_9.1 = f32[128,2048]{1,0:T(8,128)} custom-call(f32[8,128,2048]{2,1,0:T(8,128)} %bitcast.167), custom_call_target="tpu_custom_call" | custom-call | tf_op jit(solution)/shard_map/reduce_line_9/pallas_call | solution.py:350
  419.9 41.5 %gather_line_10.1 = bf16[8,128,2048]{2,1,0:T(8,128)(2,1)} custom-call(bf16[128,2048]{1,0:T(8,128)(2,1)} %fusion.16.given), custom_call_target="tpu_custom_call" | custom-call | tf_op jit(solution)/shard_map/gather_line_10/pallas_call | solution.py:202
  461.5 13.0 %multiply_convert_fusion = (bf16[1024,1024]{1,0:T(8,128)(2,1)S(1)}, bf16[1024,1024]{1,0:T(8,128)(2,1)}) fusion(f32[1024,1024]{1,0:T(8,128)} %copy-done.32, f32[1024,1024]{1,0:T(8,128)} %get-tuple-element.82, bf16[1024,2048]{1,0:T(8,128)(2,1)} %bitcast.178, bf16[1024,2048]{1,0:T(8,128)(2,1)} %param.19), kind=kOutput, calls=%fused_computation | convolution fusion | flops 4308598784 | bytes 20971520 | tf_op jit(solution)/shard_map/dot_general | solution.py:536
  474.5 7.0 fusion.42
  481.5 6.8 convolution_add_fusion
  488.3 77.5 %reduce_line_11.1 = f32[128,2048]{1,0:T(8,128)} custom-call(f32[8,128,2048]{2,1,0:T(8,128)} %bitcast.166), custom_call_target="tpu_custom_call" | custom-call | tf_op jit(solution)/shard_map/reduce_line_11/pallas_call | solution.py:350
  570.1 41.8 %gather_line_12.1 = bf16[8,128,2048]{2,1,0:T(8,128)(2,1)} custom-call(bf16[128,2048]{1,0:T(8,128)(2,1)} %get-tuple-element.49.given), custom_call_target="tpu_custom_call" | custom-call | tf_op jit(solution)/shard_map/gather_line_12/pallas_call | solution.py:202
  616.2 10.2 exchange_ctx_13.1.grad_ref
  626.5 15.8 %attend_back.1 = (f32[4,2,128,256]{3,2,1,0:T(8,128)}, f32[4,2,128,256]{3,2,1,0:T(8,128)}, bf16[4,2,128,256]{3,2,1,0:T(8,128)(2,1)}) custom-call(bf16[4,3,2,128,256]{4,3,2,1,0:T(8,128)(2,1)} %exchange_ctx_5.1.query_ref.key_ref.value_ref, bf16[4,3,2,128,256]{4,3,2,1,0:T(8,128)(2,1)} %exchange_ctx_5.1.query_ref.key_ref.value_ref, ...), custom_call_target="tpu_custom_call" | custom-call | tf_op jit(solution)/shard_map/attend_back/pallas_call | solution.py:472
  642.2 33.7 %exchange_ctx_14.1 = (f32[4,2,128,256]{3,2,1,0:T(8,128)}, f32[4,2,128,256]{3,2,1,0:T(8,128)}, bf16[4,2,128,256]{3,2,1,0:T(8,128)(2,1)}) custom-call(f32[4,2,128,256]{3,2,1,0:T(8,128)} %get-tuple-element.16.refs_0_, f32[4,2,128,256]{3,2,1,0:T(8,128)} %get-tuple-element.17.refs_1_, bf16[4,2,128,256]{3,2,1,0:T(8,128)(2,1)} %get-tuple-element.18.refs_2_), custom_call_target="tpu_custom_call" | custom-call | tf_op jit(solution)/shard_map/exchange_ctx_14/pallas_call | solution.py:84
  701.2 6.8 exchange_fsdp_15.1
  728.2 44.4 %reduce-scatter.4.cloned.1.call-done = bf16[1,8,64,768]{3,2,1,0:T(8,128)(2,1)} async-done(((bf16[4,8,64,768]{3,2,1,0:T(8,128)(2,1)}), bf16[1,8,64,768]{3,2,1,0:T(8,128)(2,1)}) %reduce-scatter.4.cloned.1.call-update) | async-done | bytes 786448
  772.5 17.8 %exchange_fsdp_19.1 = bf16[8,64,768]{2,1,0:T(8,128)(2,1)} custom-call(bf16[8,64,768]{2,1,0:T(8,128)(2,1)} %bitcast.202), custom_call_target="tpu_custom_call" | custom-call | tf_op jit(solution)/shard_map/exchange_fsdp_19/pallas_call | solution.py:84
  814.3 7.6 fusion.2.given
  821.9 83.1 %reduce_line_16.1 = f32[128,2048]{1,0:T(8,128)} custom-call(f32[8,128,2048]{2,1,0:T(8,128)} %fusion.2.given), custom_call_target="tpu_custom_call" | custom-call | tf_op jit(solution)/shard_map/reduce_line_16/pallas_call | solution.py:350
  922.8 10.1 reshape.252
  932.9 14.4 %fusion.33 = (f32[1,4,64,8,256]{4,0,2,3,1:T(1,128)S(1)}, f32[1,4,64,8,256]{4,0,2,3,1:T(1,128)S(1)}, f32[1,4,64,8,256]{4,0,2,3,1:T(1,128)S(1)}) fusion(f32[3,4,64,8,256]{4,0,2,3,1:T(4,128)} %bitcast.161), kind=kLoop, calls=%fused_computation.108 | loop fusion | bytes 12582912 | tf_op jit(solution)/shard_map/slice | solution.py:709
  957.6 141.5 %all-reduce.5.cloned.1.call-done = (bf16[256,2048]{1,0:T(8,128)(2,1)}, bf16[2048,1024]{1,0:T(8,128)(2,1)}, bf16[2048,1024]{1,0:T(8,128)(2,1)}, bf16[1024,2048]{1,0:T(8,128)(2,1)}) async-done(((bf16[256,2048]{1,0:T(8,128)(2,1)}, bf16[2048,1024]{1,0:T(8,128)(2,1)}, bf16[2048,1024]{1,0:T(8,128)(2,1)}, bf16[1024,2048]{1,0:T(8,128)(2,1)}), (bf16[256,2048]{1,0:T(8,128)(2,1)}, bf16[2048,1024]{1,0:T(8,128)(2,1)}, ...) | async-done | bytes 13631504 | tf_op jit(solution)/shard_map/psum | solution.py:685
  1101.9 6.8 convert_element_type.141
  (189 shorter events, 187.7 us)
Async XLA Ops:
  7.2 15.4 %copy-start = (bf16[256,2048]{1,0:T(8,128)(2,1)S(1)}, bf16[256,2048]{1,0:T(8,128)(2,1)}, u32[]{:S(2)}) copy-start(bf16[256,2048]{1,0:T(8,128)(2,1)} %param.13) | copy-start | bytes 3145732
  7.2 257.0 %all-gather.4.cloned.1.call-start = ((), (), s32[]{:S(2)}) async-start(), calls=%async_computation.1 | async-start | bytes 9437184 | tf_op jit(solution)/shard_map/all_gather | solution.py:590
  7.9 764.6 %reduce-scatter.4.cloned.1.call-start = ((), (), s32[]{:S(2)}) async-start(), calls=%async_computation.3 | async-start | bytes 3932160
  160.5 10.7 copy-start.23
  194.1 6.8 copy-start.7
  196.6 5.6 copy-start.18
  225.8 38.3 %copy-start.22 = (f32[8,5,256]{2,1,0:T(8,128)S(1)}, f32[8,5,256]{2,1,0:T(8,128)}, u32[]{:S(2)}) copy-start(f32[8,5,256]{2,1,0:T(8,128)} %exchange_fsdp_0.1) | copy-start | bytes 122884
  264.2 4.8 copy-start.6
  315.7 8.1 copy-start.14
  315.7 8.1 copy-start.26
  323.8 6.5 copy-start.32
  323.8 6.5 copy-start.24
  330.3 6.7 copy-start.28
  337.0 79.0 %copy-start.5 = (bf16[1,128,2048]{2,1,0:T(8,128)(2,1)S(1)}, bf16[1,128,2048]{2,1,0:T(8,128)(2,1)}, u32[]{:S(2)}) copy-start(bf16[1,128,2048]{2,1,0:T(8,128)(2,1)} %param.21) | copy-start | bytes 1572868
  461.4 13.0 %copy-start.25 = (bf16[2048,1024]{1,0:T(8,128)(2,1)S(1)}, bf16[2048,1024]{1,0:T(8,128)(2,1)}, u32[]{:S(2)}) copy-start(bf16[2048,1024]{1,0:T(8,128)(2,1)} %param.17) | copy-start | bytes 12582916
  474.5 7.0 copy-start.30
  474.5 7.0 copy-start.27
  488.3 79.0 %copy-start.2 = (f32[128,2048]{1,0:T(8,128)S(1)}, f32[128,2048]{1,0:T(8,128)}, u32[]{:S(2)}) copy-start(f32[128,2048]{1,0:T(8,128)} %reduce_line_9.1) | copy-start | bytes 3145732
  570.1 41.8 %copy-start.19 = (bf16[256,2048]{1,0:T(8,128)(2,1)S(1)}, bf16[256,2048]{1,0:T(8,128)(2,1)}, u32[]{:S(2)}) copy-start(bf16[256,2048]{1,0:T(8,128)(2,1)} %param.16) | copy-start | bytes 3145732
  642.2 39.1 %copy-start.10 = (f32[1024,128]{1,0:T(8,128)S(1)}, f32[1024,128]{1,0:T(8,128)}, u32[]{:S(2)}) copy-start(f32[1024,128]{1,0:T(8,128)} %copy-done.9) | copy-start | bytes 1572868
  691.1 5.0 copy-start.8
  696.1 12.9 %copy-start.20 = (bf16[4,2,128,256]{3,2,1,0:T(8,128)(2,1)S(1)}, bf16[4,2,128,256]{3,2,1,0:T(8,128)(2,1)}, u32[]{:S(2)}) copy-start(bf16[4,2,128,256]{3,2,1,0:T(8,128)(2,1)} %get-tuple-element.21) | copy-start | bytes 1572868
  728.1 62.4 %copy-start.17 = (bf16[4,2,128,256]{3,2,1,0:T(8,128)(2,1)S(1)}, bf16[4,2,128,256]{3,2,1,0:T(8,128)(2,1)}, u32[]{:S(2)}) copy-start(bf16[4,2,128,256]{3,2,1,0:T(8,128)(2,1)} %exchange_ctx_6.1) | copy-start | bytes 1572868
  728.1 194.7 %all-gather.6.cloned.1.call-start = ((), (), s32[]{:S(2)}) async-start(), calls=%async_computation.2 | async-start | bytes 3932160 | tf_op jit(solution)/shard_map/all_gather | solution.py:697
  790.4 308.7 %all-reduce.5.cloned.1.call-start = ((), (), s32[]{:S(2)}) async-start(), calls=%async_computation.4 | async-start | bytes 27262976 | tf_op jit(solution)/shard_map/psum | solution.py:685
  790.4 4.7 copy-start.15
  790.4 4.7 copy-start.33
  795.1 6.2 copy-start.31
  801.4 6.2 copy-start.16
  801.4 6.2 copy-start.29
  821.9 98.5 %copy-start.4 = (f32[128,2048]{1,0:T(8,128)S(1)}, f32[128,2048]{1,0:T(8,128)}, u32[]{:S(2)}) copy-start(f32[128,2048]{1,0:T(8,128)} %reduce_line_11.1) | copy-start | bytes 3145732
  1101.9 6.8 copy-start.12
  (6 other events, 17.8 us)
Sparse Core Ops, SparseCore 0:
  9.6 101.2 all-gather.3
  728.2 44.2 reduce-scatter.3
  790.5 47.6 all-gather.5
  842.5 256.5 all-reduce.4

commit v2 on v1

--- a/solution.py
+++ b/solution.py
@@ -2,6 +2,7 @@
 
 import jax
 import jax.numpy as jnp
+import numpy as np
 from jax import lax
 from jax.experimental import pallas as pl
 from jax.experimental.pallas import tpu as pltpu
@@ -25,6 +26,12 @@
 
 def in_vmem():
     return pl.BlockSpec(memory_space=pltpu.VMEM)
+
+
+def lasting(microseconds):
+    return pl.CostEstimate(
+        flops=0, transcendentals=0, bytes_accessed=int(microseconds * 3_300_000)
+    )
 
 
 def remote(source, target, sent, landed, where):
@@ -74,7 +81,7 @@
         copy.wait()
 
 
-def exchange(axis, arrays, key, scatter=True):
+def exchange(axis, arrays, key, scatter=True, takes=6):
     size = lax.axis_size(axis)
     count = len(arrays)
     shapes = [
@@ -92,6 +99,7 @@
             pltpu.SemaphoreType.DMA((count, size)),
         ],
         compiler_params=pltpu.CompilerParams(collective_id=key, has_side_effects=True),
+        cost_estimate=lasting(takes),
         name=f"exchange_{axis}_{key}",
     )(*arrays)
 
@@ -117,13 +125,10 @@
     pl.semaphore_wait(barrier, expected)
 
 
-def gather_kernel(chips, given, kept, own_sem, send_sem, land_sem):
+def pass_along(chips, given, kept, local, send_sem, land_sem, between=None):
     own = lax.axis_index("fsdp")
     chip, core = own // 2, own % 2
     sibling = chip * 2 + 1 - core
-    local = pltpu.make_async_copy(given, kept.at[own], own_sem)
-    local.start()
-    greet_line(own, chips)
 
     def copy(source, place, way, step, target):
         return remote(
@@ -140,6 +145,7 @@
 
     copy(given, own, 2, 0, sibling).start()
     local.wait()
+    result = between() if between else None
     for step in range(1, chips):
         from_left, from_right = own - 2 * step, own + 2 * step
 
@@ -194,6 +200,15 @@
                 copy(kept.at[from_right], from_right, 1, step, own - 2).wait_send()
 
             copy(kept.at[from_right], from_right, 3, step, sibling).wait_send()
+    return result
+
+
+def gather_kernel(chips, given, kept, own_sem, send_sem, land_sem):
+    own = lax.axis_index("fsdp")
+    local = pltpu.make_async_copy(given, kept.at[own], own_sem)
+    local.start()
+    greet_line(own, chips)
+    pass_along(chips, given, kept, local, send_sem, land_sem)
 
 
 def gather_line(shard, key):
@@ -210,6 +225,7 @@
             pltpu.SemaphoreType.DMA((size,)),
         ],
         compiler_params=pltpu.CompilerParams(collective_id=key, has_side_effects=True),
+        cost_estimate=lasting(40),
         name=f"gather_line_{key}",
     )(shard)
     return kept.reshape((size * shard.shape[0],) + shard.shape[1:])
@@ -368,8 +384,604 @@
         compiler_params=pltpu.CompilerParams(
             collective_id=key, has_side_effects=True, vmem_limit_bytes=60 * 1024 * 1024
         ),
+        cost_estimate=lasting(78 if wire == f32 else 42),
         name=f"reduce_line_{key}",
     )(partial)
+
+
+def greet_peers(axes):
+    barrier = pltpu.get_barrier_semaphore()
+    expected = 0
+    for axis in axes:
+        own, size = lax.axis_index(axis), lax.axis_size(axis)
+        for step in range(1, size):
+            pl.semaphore_signal(
+                barrier, inc=1, device_id={axis: lax.rem(own + step, size)}, device_id_type=MESH
+            )
+        expected += size - 1
+    pl.semaphore_wait(barrier, expected)
+
+
+def start_kernel(
+    owners,
+    parts,
+    tokens,
+    small,
+    inverse,
+    w_query,
+    w_key,
+    w_value,
+    group_tokens,
+    small_all,
+    heads_w,
+    cosines,
+    sines,
+    own_sem,
+    small_send,
+    small_land,
+    piece_send,
+    piece_land,
+    part_send,
+    part_land,
+    line_send,
+    line_land,
+):
+    own, part = lax.axis_index("fsdp"), lax.axis_index("ctx")
+    piece, own_width = heads_w.shape[2], heads_w.shape[3] // 3
+    weights = (w_query, w_key, w_value)
+
+    def cut(item, place):
+        return weights[item].at[
+            pl.ds(pl.multiple_of(part * piece, piece), piece),
+            pl.ds(pl.multiple_of(place * own_width, own_width), own_width),
+        ]
+
+    def slot(item, place):
+        return heads_w.at[place, part, :, pl.ds(item * own_width, own_width)]
+
+    local_tokens = pltpu.make_async_copy(tokens, group_tokens.at[own], own_sem.at[0])
+    local_small = pltpu.make_async_copy(small, small_all.at[own], own_sem.at[1])
+    local_pieces = [
+        pltpu.make_async_copy(cut(item, own), slot(item, own), own_sem.at[2 + item])
+        for item in range(3)
+    ]
+    for copy in [local_tokens, local_small] + local_pieces:
+        copy.start()
+    greet_peers(("fsdp", "ctx"))
+    first = []
+    for step in range(1, owners):
+        peer = lax.rem(own + step, owners)
+        for item in range(3):
+            first.append(
+                remote(
+                    cut(item, peer),
+                    slot(item, own),
+                    piece_send.at[item, step],
+                    piece_land.at[item, step],
+                    {"fsdp": peer},
+                )
+            )
+        first.append(
+            remote(
+                small,
+                small_all.at[own],
+                small_send.at[step],
+                small_land.at[step],
+                {"fsdp": peer},
+            )
+        )
+    for copy in first:
+        copy.start()
+    for copy in [local_small] + local_pieces:
+        copy.wait()
+
+    seq_rows = cosines.shape[0]
+    angle = (
+        lax.broadcasted_iota(jnp.int32, (seq_rows, HEAD_DIM), 0).astype(f32) * inverse[...]
+    )
+    cosines[...] = jnp.cos(angle)
+    lane = lax.broadcasted_iota(jnp.int32, (seq_rows, HEAD_DIM), 1)
+    sines[...] = jnp.sin(angle) * jnp.where(lane < HEAD_DIM // 2, -1.0, 1.0)
+
+    def relay():
+        for copy in first:
+            copy.wait_recv()
+        second = []
+        for step in range(1, parts):
+            second.append(
+                remote(
+                    heads_w.at[:, part],
+                    heads_w.at[:, part],
+                    part_send.at[step],
+                    part_land.at[step],
+                    {"ctx": lax.rem(part + step, parts)},
+                )
+            )
+            second[-1].start()
+        return second
+
+    second = pass_along(
+        owners // 2, tokens, group_tokens, local_tokens, line_send, line_land, relay
+    )
+    for copy in first:
+        copy.wait_send()
+    for copy in second:
+        copy.wait()
+
+
+def start(tokens, small, weights, parts, owners):
+    rows, width = tokens.shape
+    own_width = width // owners
+    piece = weights[0].shape[0] // parts
+    inverse = rope_base ** (-(np.arange(HEAD_DIM // 2, dtype=np.float32) * 2.0) / HEAD_DIM)
+    inverse = jnp.asarray(np.concatenate([inverse, inverse])[None], f32)
+    chips = owners // 2
+    return pl.pallas_call(
+        functools.partial(start_kernel, owners, parts),
+        out_shape=[
+            jax.ShapeDtypeStruct((owners, rows, width), bf16),
+            jax.ShapeDtypeStruct((owners,) + small.shape, f32),
+            jax.ShapeDtypeStruct((owners, parts, piece, 3 * own_width), bf16),
+            jax.ShapeDtypeStruct((parts * rows, HEAD_DIM), f32),
+            jax.ShapeDtypeStruct((parts * rows, HEAD_DIM), f32),
+        ],
+        in_specs=[in_vmem(), in_vmem(), in_vmem(), anywhere(), anywhere(), anywhere()],
+        out_specs=[anywhere(), anywhere(), anywhere(), in_vmem(), in_vmem()],
+        scratch_shapes=[
+            pltpu.SemaphoreType.DMA((5,)),
+            pltpu.SemaphoreType.DMA((owners,)),
+            pltpu.SemaphoreType.DMA((owners,)),
+            pltpu.SemaphoreType.DMA((3, owners)),
+            pltpu.SemaphoreType.DMA((3, owners)),
+            pltpu.SemaphoreType.DMA((parts,)),
+            pltpu.SemaphoreType.DMA((parts,)),
+            pltpu.SemaphoreType.DMA((4, chips)),
+            pltpu.SemaphoreType.DMA((owners,)),
+        ],
+        compiler_params=pltpu.CompilerParams(collective_id=0, has_side_effects=True),
+        cost_estimate=lasting(60),
+        name="start",
+    )(tokens, small, inverse, *weights)
+
+
+def as_row(column):
+    rows = column.shape[0]
+    return jnp.broadcast_to(column, (rows, 128)).T[:1]
+
+
+def as_column(row):
+    rows = row.shape[1]
+    return jnp.broadcast_to(row, (128, rows)).T[:, :1]
+
+
+def share_stats(stats, everyone, send_sem, land_sem):
+    own, owners = lax.axis_index("fsdp"), lax.axis_size("fsdp")
+    copies = []
+    for step in range(1, owners):
+        copies.append(
+            remote(
+                stats,
+                everyone.at[own],
+                send_sem.at[step],
+                land_sem.at[step],
+                {"fsdp": lax.rem(own + step, owners)},
+            )
+        )
+        copies[-1].start()
+    everyone[own] = stats[...]
+    for copy in copies:
+        copy.wait()
+    total = everyone[0]
+    for place in range(1, owners):
+        total += everyone[place]
+    return total
+
+
+def table_rows(table, row_block, rows, block_rows):
+    def block(at):
+        taken = table[at * block_rows : (at + 1) * block_rows]
+        return jnp.concatenate([taken] * (rows // block_rows), axis=0)
+
+    found = block(0)
+    for at in range(1, table.shape[0] // block_rows):
+        found = jnp.where(row_block == at, block(at), found)
+    return found
+
+
+def each_head(width):
+    return [slice(at, at + HEAD_DIM) for at in range(0, width, HEAD_DIM)]
+
+
+def heads_kernel(
+    block_rows,
+    row_blocks,
+    tokens,
+    weights,
+    cosines,
+    sines,
+    gains,
+    packed,
+    raw,
+    scales,
+    stage,
+    stats,
+    everyone,
+    own_sem,
+    stat_send,
+    stat_land,
+    part_send,
+    part_land,
+):
+    owners, rows, width = tokens.shape
+    parts, own_width = stage.shape[0], stage.shape[-1]
+    pair = owners // parts
+    part = lax.axis_index("ctx")
+    greet_peers(("fsdp", "ctx"))
+
+    def project(seq, carry):
+        product = jnp.dot(tokens[seq], weights[...], preferred_element_type=f32)
+        for kind in range(2):
+            values = product[:, kind * own_width : (kind + 1) * own_width]
+            raw[kind, seq] = values
+            stats[pl.ds(kind * owners + seq, 1), :] = as_row(
+                jnp.sum(values * values, axis=-1, keepdims=True)
+            )
+        stage[seq // pair, 2, seq % pair] = product[:, 2 * own_width :].astype(bf16)
+        return carry
+
+    lax.fori_loop(0, owners, project, 0)
+    scales[...] = lax.rsqrt(share_stats(stats, everyone, stat_send, stat_land) / width + norm_eps)
+
+    def rotate(seq, carry):
+        row_block = row_blocks[seq]
+        cosine = table_rows(cosines, row_block, rows, block_rows)
+        sine = table_rows(sines, row_block, rows, block_rows)
+        for kind in range(2):
+            scale = as_column(scales[pl.ds(kind * owners + seq, 1), :])
+            for head in each_head(own_width):
+                values = raw[kind, seq, :, head] * scale * gains[kind : kind + 1, head]
+                stage[seq // pair, kind, seq % pair, :, head] = (
+                    values * cosine + pltpu.roll(values, HEAD_DIM // 2, 1) * sine
+                ).astype(bf16)
+        return carry
+
+    copies = []
+    for step in range(1, parts + 1):
+        peer = lax.rem(part + step, parts)
+        lax.fori_loop(peer * pair, (peer + 1) * pair, rotate, 0)
+        if step < parts:
+            copies.append(
+                remote(
+                    stage.at[peer],
+                    packed.at[part],
+                    part_send.at[step],
+                    part_land.at[step],
+                    {"ctx": peer},
+                )
+            )
+        else:
+            copies.append(pltpu.make_async_copy(stage.at[part], packed.at[part], own_sem))
+        copies[-1].start()
+    for copy in copies:
+        copy.wait()
+
+
+def heads(row_blocks, tokens, weights, cosines, sines, gains, parts, block_rows):
+    owners, rows, width = tokens.shape
+    own_width = width // owners
+    pair = owners // parts
+    packed = (parts, 3, pair, rows, own_width)
+    return pl.pallas_call(
+        functools.partial(heads_kernel, block_rows),
+        out_shape=[
+            jax.ShapeDtypeStruct(packed, bf16),
+            jax.ShapeDtypeStruct((2, owners, rows, own_width), f32),
+            jax.ShapeDtypeStruct((2 * owners, rows), f32),
+        ],
+        in_specs=[in_vmem()] * 6,
+        out_specs=[anywhere(), in_vmem(), in_vmem()],
+        scratch_shapes=[
+            pltpu.VMEM(packed, bf16),
+            pltpu.VMEM((2 * owners, rows), f32),
+            pltpu.VMEM((owners, 2 * owners, rows), f32),
+            pltpu.SemaphoreType.DMA,
+            pltpu.SemaphoreType.DMA((owners,)),
+            pltpu.SemaphoreType.DMA((owners,)),
+            pltpu.SemaphoreType.DMA((parts,)),
+            pltpu.SemaphoreType.DMA((parts,)),
+        ],
+        compiler_params=pltpu.CompilerParams(
+            collective_id=1, has_side_effects=True, vmem_limit_bytes=60 * 1024 * 1024
+        ),
+        cost_estimate=lasting(35),
+        name="heads",
+    )(row_blocks, tokens, weights, cosines, sines, gains)
+
+
+def heads_back_kernel(
+    block_rows,
+    row_blocks,
+    grad_query,
+    grad_key,
+    grad_value,
+    cosines,
+    sines,
+    gains,
+    raw,
+    scales,
+    grads,
+    gain_sums,
+    pair_grads,
+    pair_values,
+    stats,
+    everyone,
+    own_sem,
+    stat_send,
+    stat_land,
+    part_send,
+    part_land,
+):
+    kinds, owners, rows, own_width = raw.shape
+    parts = pair_values.shape[0]
+    pair = owners // parts
+    width = owners * own_width
+    part = lax.axis_index("ctx")
+    sources = (grad_query, grad_key, grad_value)
+
+    def landing(item, place):
+        return pair_values.at[place] if item == 2 else pair_grads.at[item, place]
+
+    local = [
+        pltpu.make_async_copy(sources[item].at[part], landing(item, part), own_sem.at[item])
+        for item in range(3)
+    ]
+    for copy in local:
+        copy.start()
+    greet_peers(("fsdp", "ctx"))
+    copies = []
+    for step in range(1, parts):
+        peer = lax.rem(part + step, parts)
+        for item in range(3):
+            copies.append(
+                remote(
+                    sources[item].at[peer],
+                    landing(item, part),
+                    part_send.at[item, step],
+                    part_land.at[item, step],
+                    {"ctx": peer},
+                )
+            )
+            copies[-1].start()
+    gain_sums[...] = jnp.zeros_like(gain_sums)
+    for copy in local:
+        copy.wait()
+    for copy in copies:
+        copy.wait()
+
+    def unrotate(seq, carry):
+        row_block = row_blocks[seq]
+        cosine = table_rows(cosines, row_block, rows, block_rows)
+        sine = table_rows(sines, row_block, rows, block_rows)
+        for kind in range(kinds):
+            scale = as_column(scales[pl.ds(kind * owners + seq, 1), :])
+            products = jnp.zeros((rows, 1), f32)
+            for head in each_head(own_width):
+                rotated = pair_grads[kind, seq // pair, seq % pair, :, head]
+                values = rotated * cosine - pltpu.roll(rotated, HEAD_DIM // 2, 1) * sine
+                plain = raw[kind, seq, :, head]
+                gain_sums[kind : kind + 1, head] += jnp.sum(
+                    values * (plain * scale), axis=0, keepdims=True
+                )
+                values = values * gains[kind : kind + 1, head]
+                pair_grads[kind, seq // pair, seq % pair, :, head] = values
+                products += jnp.sum(values * plain, axis=-1, keepdims=True)
+            stats[pl.ds(kind * owners + seq, 1), :] = as_row(products)
+        return carry
+
+    lax.fori_loop(0, owners, unrotate, 0)
+    means = share_stats(stats, everyone, stat_send, stat_land) / width
+    stats[...] = means
+
+    def through_norm(seq, carry):
+        for kind in range(kinds):
+            row = pl.ds(kind * owners + seq, 1)
+            scale, mean = as_column(scales[row, :]), as_column(stats[row, :])
+            grads[seq, :, kind * own_width : (kind + 1) * own_width] = (
+                scale * pair_grads[kind, seq // pair, seq % pair]
+                - raw[kind, seq] * (scale * scale * scale * mean)
+            ).astype(bf16)
+        grads[seq, :, 2 * own_width :] = pair_values[seq // pair, seq % pair]
+        return carry
+
+    lax.fori_loop(0, owners, through_norm, 0)
+
+
+def heads_back(row_blocks, pair_grads, cosines, sines, gains, raw, scales, block_rows):
+    kinds, owners, rows, own_width = raw.shape
+    parts, pair = pair_grads[0].shape[:2]
+    return pl.pallas_call(
+        functools.partial(heads_back_kernel, block_rows),
+        out_shape=[
+            jax.ShapeDtypeStruct((owners, rows, 3 * own_width), bf16),
+            jax.ShapeDtypeStruct((2, own_width), f32),
+        ],
+        in_specs=[in_vmem()] * 9,
+        out_specs=[in_vmem(), in_vmem()],
+        scratch_shapes=[
+            pltpu.VMEM((2, parts, pair, rows, own_width), f32),
+            pltpu.VMEM((parts, pair, rows, own_width), bf16),
+            pltpu.VMEM((2 * owners, rows), f32),
+            pltpu.VMEM((owners, 2 * owners, rows), f32),
+            pltpu.SemaphoreType.DMA((3,)),
+            pltpu.SemaphoreType.DMA((owners,)),
+            pltpu.SemaphoreType.DMA((owners,)),
+            pltpu.SemaphoreType.DMA((3, parts)),
+            pltpu.SemaphoreType.DMA((3, parts)),
+        ],
+        compiler_params=pltpu.CompilerParams(
+            collective_id=2, has_side_effects=True, vmem_limit_bytes=60 * 1024 * 1024
+        ),
+        cost_estimate=lasting(45),
+        name="heads_back",
+    )(row_blocks, *pair_grads, cosines, sines, gains, raw, scales)
+
+
+def finish_kernel(
+    owners,
+    parts,
+    sums,
+    gain_post,
+    gain_heads,
+    kept,
+    gain_own,
+    post_all,
+    gain_mine,
+    part_all,
+    own_sem,
+    piece_send,
+    piece_land,
+    part_send,
+    part_land,
+    post_send,
+    post_land,
+    gain_send,
+    gain_land,
+):
+    own, part = lax.axis_index("fsdp"), lax.axis_index("ctx")
+    width = kept.shape[3]
+    own_width = width // owners
+
+    def cut(item, place):
+        start = pl.multiple_of((place * 3 + item) * own_width, own_width)
+        return sums.at[:, pl.ds(start, own_width)]
+
+    def slot(item):
+        return kept.at[
+            part, item, :, pl.ds(pl.multiple_of(own * own_width, own_width), own_width)
+        ]
+
+    output_rows = sums.at[:, pl.ds(3 * width, width)]
+    local = [
+        pltpu.make_async_copy(cut(item, own), slot(item), own_sem.at[item]) for item in range(3)
+    ]
+    local.append(pltpu.make_async_copy(output_rows, kept.at[part, 3], own_sem.at[3]))
+    for copy in local:
+        copy.start()
+    greet_peers(("fsdp", "ctx"))
+    first, posts, second = [], [], []
+    for step in range(1, owners):
+        peer = lax.rem(own + step, owners)
+        for item in range(3):
+            first.append(
+                remote(
+                    cut(item, peer),
+                    slot(item),
+                    piece_send.at[item, step],
+                    piece_land.at[item, step],
+                    {"fsdp": peer},
+                )
+            )
+        posts.append(
+            remote(
+                gain_post.at[peer],
+                post_all.at[own],
+                post_send.at[step],
+                post_land.at[step],
+                {"fsdp": peer},
+            )
+        )
+    for copy in first + posts:
+        copy.start()
+    for step in range(1, parts):
+        second.append(
+            remote(
+                output_rows,
+                kept.at[part, 3],
+                part_send.at[0, step],
+                part_land.at[0, step],
+                {"ctx": lax.rem(part + step, parts)},
+            )
+        )
+        second[-1].start()
+    post_all[own] = gain_post[own]
+    for copy in local:
+        copy.wait()
+    for copy in first:
+        copy.wait_recv()
+    for step in range(1, parts):
+        second.append(
+            remote(
+                kept.at[part, pl.ds(0, 3)],
+                kept.at[part, pl.ds(0, 3)],
+                part_send.at[1, step],
+                part_land.at[1, step],
+                {"ctx": lax.rem(part + step, parts)},
+            )
+        )
+        second[-1].start()
+    for copy in posts:
+        copy.wait()
+    post = post_all[0]
+    for place in range(1, owners):
+        post += post_all[place]
+    gain_mine[:2, :] = gain_heads[...]
+    gain_mine[2:, :] = post
+    gains = []
+    for step in range(1, parts):
+        gains.append(
+            remote(
+                gain_mine,
+                part_all.at[part],
+                gain_send.at[step],
+                gain_land.at[step],
+                {"ctx": lax.rem(part + step, parts)},
+            )
+        )
+        gains[-1].start()
+    part_all[part] = gain_mine[...]
+    for copy in gains:
+        copy.wait()
+    total = part_all[0]
+    for place in range(1, parts):
+        total += part_all[place]
+    gain_own[...] = total
+    for copy in first:
+        copy.wait_send()
+    for copy in second:
+        copy.wait()
+
+
+def finish(sums, gain_post, gain_heads):
+    owners, parts = lax.axis_size("fsdp"), lax.axis_size("ctx")
+    piece, columns = sums.shape
+    width = columns // 4
+    own_width = width // owners
+    return pl.pallas_call(
+        functools.partial(finish_kernel, owners, parts),
+        out_shape=[
+            jax.ShapeDtypeStruct((parts, 4, piece, width), bf16),
+            jax.ShapeDtypeStruct((4, own_width), f32),
+        ],
+        in_specs=[in_vmem(), in_vmem(), in_vmem()],
+        out_specs=[anywhere(), in_vmem()],
+        scratch_shapes=[
+            pltpu.VMEM((owners, 2, own_width), f32),
+            pltpu.VMEM((4, own_width), f32),
+            pltpu.VMEM((parts, 4, own_width), f32),
+            pltpu.SemaphoreType.DMA((4,)),
+            pltpu.SemaphoreType.DMA((3, owners)),
+            pltpu.SemaphoreType.DMA((3, owners)),
+            pltpu.SemaphoreType.DMA((2, parts)),
+            pltpu.SemaphoreType.DMA((2, parts)),
+            pltpu.SemaphoreType.DMA((owners,)),
+            pltpu.SemaphoreType.DMA((owners,)),
+            pltpu.SemaphoreType.DMA((parts,)),
+            pltpu.SemaphoreType.DMA((parts,)),
+        ],
+        compiler_params=pltpu.CompilerParams(collective_id=3, has_side_effects=True),
+        cost_estimate=lasting(50),
+        name="finish",
+    )(sums, gain_post, gain_heads)
 
 
 def probs_of(query, key, query_pos, key_pos):
@@ -461,6 +1073,7 @@
         out_shape=jax.ShapeDtypeStruct((parts, pair, rows, width), bf16),
         in_specs=in_specs,
         out_specs=row_block,
+        cost_estimate=lasting(12),
         name="attend",
     )(packed, packed, packed, query_pos, key_pos)
 
@@ -483,6 +1096,7 @@
             pltpu.VMEM((seq_rows, HEAD_DIM), f32),
             pltpu.VMEM((seq_rows, HEAD_DIM), f32),
         ],
+        cost_estimate=lasting(16),
         name="attend_back",
     )(packed, packed, packed, query_pos, key_pos, grad)
 
@@ -498,34 +1112,6 @@
     )
     grad_gain = jnp.sum(grad_out * (values * scale), axis=0)
     return (grad_values, grad_gain)
-
-
-def rotate_half(values):
-    half_width = values.shape[-1] // 2
-    return jnp.concatenate([-values[..., half_width:], values[..., :half_width]], axis=-1)
-
-
-def rope_tables(positions, width):
-    half_width = width // 2
-    inverse = rope_base ** (-(jnp.arange(half_width, dtype=f32) * 2.0) / width)
-    angle = positions.astype(f32)[:, None] * inverse[None, :]
-    cosine = jnp.concatenate([jnp.cos(angle), jnp.cos(angle)], axis=-1)
-    sine = jnp.concatenate([jnp.sin(angle), jnp.sin(angle)], axis=-1)
-    return (cosine[:, None, :], sine[:, None, :])
-
-
-def by_head(values):
-    return values.reshape(values.shape[0], values.shape[1] // HEAD_DIM, HEAD_DIM)
-
-
-def apply_rope(values, cosine, sine):
-    shaped = by_head(values)
-    return (shaped * cosine + rotate_half(shaped) * sine).reshape(values.shape)
-
-
-def rope_back(grads, cosine, sine):
-    shaped = by_head(grads)
-    return (shaped * cosine - rotate_half(shaped * sine)).reshape(grads.shape)
 
 
 def mm(left, right):
@@ -555,69 +1141,44 @@
 ):
     rows, width = hidden_in.shape[1:]
     parts, owners = lax.axis_size("ctx"), lax.axis_size("fsdp")
-    part, owner = lax.axis_index("ctx"), lax.axis_index("fsdp")
+    part = lax.axis_index("ctx")
     group = owners * rows
     own_width = width // owners
     pair = owners // parts
     blocks = block_order.shape[1]
     block_rows = parts * rows // blocks
-    piece = w_query.shape[0] // parts
     tokens_b = hidden_in[0]
     tokens_f = tokens_b.astype(f32)
+    own_gains = norm_gains.astype(f32)
 
     small = jnp.concatenate(
-        [
-            norm_gains.astype(f32),
-            jnp.pad(block_order.astype(f32), ((0, 0), (0, own_width - blocks))),
-        ],
-        axis=0,
-    )
-    (small_all,) = exchange("fsdp", [small], 0, scatter=False)
+        [own_gains, jnp.pad(block_order.astype(f32), ((0, 0), (0, own_width - blocks)))], axis=0
+    )
+    group_tokens, small_all, w_heads, cosines, sines = start(
+        tokens_b, small, (w_query, w_key, w_value), parts, owners
+    )
+    w_heads = w_heads.reshape(width, 3 * own_width)
+    group_tokens, w_output_in = lax.optimization_barrier((group_tokens, w_output))
+    full_output = lax.all_gather(w_output_in, "fsdp", axis=0, tiled=True)
     gains = small_all[:, :4].transpose(1, 0, 2).reshape(4, width)
     orders = small_all[:, 4, :blocks].astype(jnp.int32)
-    own_gains = norm_gains.astype(f32)
-    stacked = jnp.stack(
-        [
-            lax.dynamic_slice_in_dim(item, part * piece, piece)
-            for item in (w_query, w_key, w_value)
-        ]
-    )
-    stacked = stacked.reshape(3, piece, owners, own_width).transpose(2, 1, 0, 3)
-    (columns,) = exchange("fsdp", [stacked.reshape(owners, piece, 3 * own_width)], 1)
-    (columns,) = exchange("ctx", [columns], 2, scatter=False)
-    w_heads = columns.transpose(1, 0, 2, 3).reshape(width, 3 * own_width)
-    group_tokens = gather_line(tokens_b, 3)
-    full_output = lax.all_gather(w_output, "fsdp", axis=0, tiled=True)
-
+
+    own_blocks = rows // block_rows
+    row_blocks = jnp.repeat(
+        lax.dynamic_slice_in_dim(orders, part * own_blocks, own_blocks, 1), block_rows, axis=1
+    )[:, :, None]
+    packed, raw, scales = heads(
+        row_blocks, group_tokens, w_heads, cosines, sines, own_gains[:2], parts, block_rows
+    )
     offsets = jnp.arange(block_rows, dtype=jnp.int32)
-    seq_pos = (orders[:, :, None] * block_rows + offsets[None, None, :]).reshape(
-        owners, parts * rows
-    )
-    group_pos = lax.dynamic_slice_in_dim(seq_pos, part * rows, rows, 1).reshape(group)
-    pair_pos = lax.dynamic_slice_in_dim(seq_pos, part * pair, pair, 0)
+    pair_orders = lax.dynamic_slice_in_dim(orders, part * pair, pair, 0)
+    pair_pos = pair_orders[:, :, None] * block_rows + offsets[None, None, :]
     query_pos = pair_pos.reshape(pair, parts, rows, 1)
     key_pos = pair_pos.reshape(pair, 1, parts * rows)
-    cosine, sine = rope_tables(group_pos, HEAD_DIM)
-
-    raw = mm(group_tokens, w_heads)
-    query_raw, key_raw = raw[:, :own_width], raw[:, own_width : 2 * own_width]
-    values = raw[:, 2 * own_width :].astype(bf16)
-    squares = jnp.stack(
-        [jnp.sum(query_raw * query_raw, axis=-1), jnp.sum(key_raw * key_raw, axis=-1)]
-    )
-    (squares,) = exchange("fsdp", [squares], 4, scatter=False)
-    scales = lax.rsqrt(jnp.sum(squares, axis=0) / width + norm_eps)
-    query_scale, key_scale = scales[0][:, None], scales[1][:, None]
-    queries = apply_rope(query_raw * query_scale * own_gains[0], cosine, sine).astype(bf16)
-    keys = apply_rope(key_raw * key_scale * own_gains[1], cosine, sine).astype(bf16)
-    packed = jnp.stack(
-        [item.reshape(parts, pair, rows, own_width) for item in (queries, keys, values)], axis=1
-    )
-    (packed,) = exchange("ctx", [packed], 5)
     mixed_pair = attend(packed, query_pos, key_pos)
-    (mixed_group,) = exchange("ctx", [mixed_pair], 6)
+    (mixed_group,) = exchange("ctx", [mixed_pair], 6, takes=10)
     mixed_group = mixed_group.reshape(owners, rows, own_width)
-    (mixed_own,) = exchange("fsdp", [mixed_group], 7)
+    (mixed_own,) = exchange("fsdp", [mixed_group], 7, takes=14)
     mixed_own = mixed_own.transpose(1, 0, 2).reshape(rows, width)
     projected = mm(mixed_own, full_output)
     proj_scale = norm_stat(projected)
@@ -627,90 +1188,74 @@
     upward = mm(mlp_rows_in, w_up)
     sigma = jax.nn.sigmoid(gate)
     hidden_b = (gate * sigma * upward).astype(bf16)
-    mlp_out = reduce_line(mm(hidden_b, w_down).reshape(owners, rows, width), 9)
+    mlp_out = reduce_line(mm(hidden_b, w_down).reshape(owners, rows, width), 9, wire=bf16)
     mlp_scale = norm_stat(mlp_out)
     block_out = residual + mlp_out * mlp_scale * gains[3]
 
     grad_y = out_grad[0].astype(f32)
     grad_mlp, gain_ff = norm_back(mlp_out, mlp_scale, gains[3], grad_y)
     grad_rows = gather_line(grad_mlp.astype(bf16), 10)
+    grad_rows, down_part = lax.optimization_barrier(
+        (grad_rows, mm_tn(hidden_b, grad_rows).astype(bf16))
+    )
     grad_hidden = mm_nt(grad_rows, w_down)
     grad_gate_b = (grad_hidden * upward * sigma * (1.0 + gate * (1.0 - sigma))).astype(bf16)
     grad_up_b = (grad_hidden * (gate * sigma)).astype(bf16)
-    down_sum = lax.psum(mm_tn(hidden_b, grad_rows).astype(bf16), "ctx").astype(f32)
-    gate_sum = lax.psum(mm_tn(mlp_rows_in, grad_gate_b).astype(bf16), "ctx").astype(f32)
-    up_sum = lax.psum(mm_tn(mlp_rows_in, grad_up_b).astype(bf16), "ctx").astype(f32)
+    grad_gate_b, grad_up_b, gate_part, up_part = lax.optimization_barrier(
+        (
+            grad_gate_b,
+            grad_up_b,
+            mm_tn(mlp_rows_in, grad_gate_b).astype(bf16),
+            mm_tn(mlp_rows_in, grad_up_b).astype(bf16),
+        )
+    )
+    down_sum, gate_sum, up_sum = lax.psum((down_part, gate_part, up_part), "ctx")
     back_part = mm_nt(grad_gate_b, w_gate) + mm_nt(grad_up_b, w_up)
-    grad_res = grad_y + reduce_line(back_part.reshape(owners, rows, width), 11)
+    grad_res = grad_y + reduce_line(back_part.reshape(owners, rows, width), 11, wire=bf16)
     grad_proj, gain_attn = norm_back(projected, proj_scale, gains[2], grad_res)
     grad_proj_rows = gather_line(grad_proj.astype(bf16), 12)
     grad_mixed = mm_nt(grad_proj_rows, w_output).astype(bf16)
-    (grad_mixed,) = exchange("ctx", [grad_mixed.reshape(parts, pair, rows, own_width)], 13)
-    grad_queries, grad_keys, grad_values = exchange(
-        "ctx", attend_back(packed, query_pos, key_pos, grad_mixed), 14
-    )
-    grad_queries = rope_back(grad_queries.reshape(group, own_width), cosine, sine)
-    grad_keys = rope_back(grad_keys.reshape(group, own_width), cosine, sine)
-    grad_value_b = grad_values.reshape(group, own_width)
-    query_weighted, key_weighted = grad_queries * own_gains[0], grad_keys * own_gains[1]
-    products = jnp.stack(
-        [jnp.sum(query_weighted * query_raw, axis=-1), jnp.sum(key_weighted * key_raw, axis=-1)]
-    )
-    (products,) = exchange("fsdp", [products], 15, scatter=False)
-    means = jnp.sum(products, axis=0) / width
-    grad_query_b = (
-        query_scale * query_weighted - query_raw * (query_scale**3 * means[0][:, None])
-    ).astype(bf16)
-    grad_key_b = (
-        key_scale * key_weighted - key_raw * (key_scale**3 * means[1][:, None])
-    ).astype(bf16)
-    gain_query = jnp.sum(grad_queries * (query_raw * query_scale), axis=0)
-    gain_key = jnp.sum(grad_keys * (key_raw * key_scale), axis=0)
-    grad_heads = jnp.concatenate([grad_query_b, grad_key_b, grad_value_b], axis=1)
+    (grad_mixed,) = exchange(
+        "ctx", [grad_mixed.reshape(parts, pair, rows, own_width)], 13, takes=10
+    )
+    pair_grads = attend_back(packed, query_pos, key_pos, grad_mixed)
+    grad_heads, gain_heads = heads_back(
+        row_blocks, pair_grads, cosines, sines, own_gains[:2], raw, scales, block_rows
+    )
+    grad_heads = grad_heads.reshape(group, 3 * own_width)
+
+    piece = own_width // parts
+    output_part = mm_tn(mixed_group.reshape(group, own_width), grad_proj_rows).astype(bf16)
+    heads_part = mm_tn(group_tokens.reshape(group, width), grad_heads).astype(bf16)
+    attention_part = jnp.concatenate(
+        [
+            heads_part.reshape(owners, parts, piece, 3 * own_width)
+            .transpose(1, 2, 0, 3)
+            .reshape(parts, piece, 3 * width),
+            output_part.reshape(parts, piece, width),
+        ],
+        axis=2,
+    )
+    attention_part, down_sum, gate_sum, up_sum = lax.optimization_barrier(
+        (attention_part, down_sum, gate_sum, up_sum)
+    )
+    attention_part = lax.psum_scatter(attention_part, "ctx", scatter_dimension=0, tiled=False)
     input_grad = grad_res + reduce_line(
-        mm_nt(grad_heads, w_heads).reshape(owners, rows, width), 16
-    )
-
-    (gain_post,) = exchange(
-        "fsdp",
-        [jnp.stack([gain_attn, gain_ff]).reshape(2, owners, own_width).transpose(1, 0, 2)],
-        17,
-    )
-    gain_own = jnp.concatenate(
-        [gain_query[None], gain_key[None], jnp.sum(gain_post, axis=0)], axis=0
-    )
-    (gain_own,) = exchange("ctx", [gain_own], 18, scatter=False)
-    gain_own = jnp.sum(gain_own, axis=0)
-
-    output_sum = lax.psum(
-        mm_tn(mixed_group.reshape(owners, rows, own_width).reshape(group, own_width), grad_proj_rows).astype(bf16),
-        "ctx",
-    ).astype(f32)
-    heads_part = (
-        mm_tn(group_tokens, grad_heads)
-        .astype(bf16)
-        .reshape(owners, parts, piece, 3 * own_width)
-        .transpose(1, 0, 2, 3)
-    )
-    heads_part = lax.psum_scatter(heads_part, "ctx", scatter_dimension=0, tiled=False)
-    (heads_part,) = exchange("fsdp", [heads_part], 19)
-    heads_all = lax.all_gather(heads_part, "ctx", axis=0)
-    heads_all = (
-        heads_all.reshape(parts, owners, piece, 3, own_width)
-        .transpose(3, 0, 2, 1, 4)
-        .reshape(3, parts * piece, width)
-        .astype(f32)
-    )
+        mm_nt(grad_heads, w_heads).reshape(owners, rows, width), 16, wire=bf16
+    )
+    attention_part, input_grad = lax.optimization_barrier((attention_part, input_grad))
+    gain_post = jnp.stack([gain_attn, gain_ff]).reshape(2, owners, own_width).transpose(1, 0, 2)
+    attention_all, gain_own = finish(attention_part, gain_post, gain_heads)
+    attention_all = [
+        attention_all[:, item].reshape(own_width, width).astype(f32) for item in range(4)
+    ]
     return (
         block_out.astype(bf16)[None],
         input_grad[None],
-        heads_all[0],
-        heads_all[1],
-        heads_all[2],
-        output_sum,
-        gate_sum,
-        up_sum,
-        down_sum,
+        *attention_all,
+        gate_sum.astype(f32),
+        up_sum.astype(f32),
+        down_sum.astype(f32),
         gain_own,
     )
 

time: 1130 us -> 783 us (0.69)
  waiting for transfers between devices: 187 us -> 54.5 us
  Pallas kernels: 661 us -> 562 us
  local copies, waits for them, and re-layouts: 87.9 us -> 10.2 us
  other arithmetic: 73 us -> 41.2 us
    pallas_call x0 -> x4, Pallas kernels: none -> 230 us  [the longest x1 70.6 us: heads_back(): pl.pallas_call(functools.partial(heads_back_kernel, block_rows), out_shap...]
    pallas_call x13 -> x3, Pallas kernels: 210 us -> 42.9 us  [exchange(): pl.pallas_call(functools.partial(exchange_kernel, axis, size, scatter, co...]
    pallas_call x3, Pallas kernels: 238 us -> 134 us  [reduce_line(): pl.pallas_call(functools.partial(reduce_kernel, chips, wire), out_shape=j...]
    psum x1, waiting for transfers between devices: 142 us -> 49.1 us  [shards(): lax.psum((down_part, gate_part, up_part), 'ctx')]
    pallas_call x4 -> x3, Pallas kernels: 184 us -> 125 us  [gather_line(): pl.pallas_call(functools.partial(gather_kernel, chips), out_shape=jax.Sha...]
    unnamed x5 -> x4, waiting for transfers between devices: 45.1 us -> 0.05 us
    slice x11 -> x2, local copies, waits for them, and re-layouts: 20.9 us -> 3.34 us  [the longest x1 2.76 us: shards(): attention_all[:, item].reshape(own_width, width).astype(f32)]
    convert_element_type x4 -> x0, local copies, waits for them, and re-layouts: 17.3 us -> none  [the longest x1 10.1 us: shards(): heads_all = heads_all.reshape(parts, owners, piece, 3, own_width).transpo...]
  transfers between devices with their start and end apart: 4 -> 3, of which waited for: 2 -> 2; matrix products, arithmetic and copies ran while one was open for 11% -> 9% of each run, Pallas kernels for 26% -> 41%
where the time goes in v2:
time: 783 us; the launch traced here: 773 us
  Pallas kernels  562 us (72%)
  matrix products  90.4 us (12%)
  waiting for transfers between devices  54.5 us (7%)
  other arithmetic  41.2 us (5%)
  between operations  14.4 us (2%)
  local copies, waits for them, and re-layouts  10.2 us (1%)
    pallas_call x3, Pallas kernels, reduce_line(): pl.pallas_call(functools.partial(reduce_kernel, chips, wire), out_shape=j...  134 us
    pallas_call x3, Pallas kernels, gather_line(): pl.pallas_call(functools.partial(gather_kernel, chips), out_shape=jax.Sha...  125 us
    pallas_call x1, Pallas kernels, heads_back(): pl.pallas_call(functools.partial(heads_back_kernel, block_rows), out_shap...  70.6 us
    pallas_call x1, Pallas kernels, start(): pl.pallas_call(functools.partial(start_kernel, owners, parts), out_shape=...  65.9 us
    pallas_call x1, Pallas kernels, finish(): pl.pallas_call(functools.partial(finish_kernel, owners, parts), out_shape...  54.2 us
    psum x1, waiting for transfers between devices, shards(): lax.psum((down_part, gate_part, up_part), 'ctx')  49.1 us
    pallas_call x3, Pallas kernels, exchange(): pl.pallas_call(functools.partial(exchange_kernel, axis, size, scatter, co...  42.9 us
    pallas_call x1, Pallas kernels, heads(): pl.pallas_call(functools.partial(heads_kernel, block_rows), out_shape=[ja...  39.6 us
  transfers between devices with their start and end apart: 3, of which 2 were waited for; matrix products, arithmetic and copies ran while one was open for 9% of the time, Pallas kernels for 41%

profile of v2, /device:TPU:0, one launch (start us, length us, event | category | flops | bytes accessed | tf_op | source)
XLA Modules:
  0.0 773.1 jit_solution(14309519198518359178)
XLA Ops:
  9.2 65.9 %start.1 = (bf16[8,128,2048]{2,1,0:T(8,128)(2,1)}, f32[8,5,256]{2,1,0:T(8,128)}, bf16[8,4,64,768]{3,2,1,0:T(8,128)(2,1)}, f32[512,128]{1,0:T(8,128)}, f32[512,128]{1,0:T(8,128)}) custom-call(bf16[128,2048]{1,0:T(8,128)(2,1)} %bitcast.96, f32[5,256]{1,0:T(8,128)} %select_maximum_fusion.small, f32[1,128]{1,0:T(1,128)} %constant.30.clone.inverse, ...), custom_call_target="tpu_custom_call" | custom-call | bytes 198000000 | tf_op jit(solution)/shard_map/start/pallas_call | solution.py:519
  78.8 39.6 %heads.1 = (bf16[4,3,2,128,256]{4,3,2,1,0:T(8,128)(2,1)}, f32[2,8,128,256]{3,2,1,0:T(8,128)}, f32[16,128]{1,0:T(8,128)}) custom-call(s32[8,128,1]{2,1,0:T(8,128)} %broadcast_in_dim_reshape.4.row_blocks, bf16[8,128,2048]{2,1,0:T(8,128)(2,1)} %get-tuple-element.41.tokens, bf16[2048,768]{1,0:T(8,128)(2,1)} %bitcast.106, f32[512,128]{1,0:T(8,128)} %get-tuple-element.43.cosines, ...), custom_call_target="tpu_custom_call" | custom-call | bytes 115500000 | tf_op jit(solution)/shard_map/heads/pallas_call | solution.py:674
  119.9 13.0 %attend.1.refs_0_ = bf16[4,2,128,256]{3,2,1,0:T(8,128)(2,1)} custom-call(bf16[4,3,2,128,256]{4,3,2,1,0:T(8,128)(2,1)} %get-tuple-element.45.query_ref.key_ref.value_ref, bf16[4,3,2,128,256]{4,3,2,1,0:T(8,128)(2,1)} %get-tuple-element.45.query_ref.key_ref.value_ref, bf16[4,3,2,128,256]{4,3,2,1,0:T(8,128)(2,1)} %get-tuple-element.45.query_ref.key_ref.value_ref, ...), custom_call_target="tpu_custom_call" | custom-call | bytes 39600000 | tf_op jit(solution)/shard_map/attend/pallas_call | solution.py:1070
  132.9 10.2 %exchange_ctx_6.1 = bf16[4,2,128,256]{3,2,1,0:T(8,128)(2,1)} custom-call(bf16[4,2,128,256]{3,2,1,0:T(8,128)(2,1)} %attend.1.refs_0_), custom_call_target="tpu_custom_call" | custom-call | bytes 33000000 | tf_op jit(solution)/shard_map/exchange_ctx_6/pallas_call | solution.py:91
  143.1 17.6 %exchange_fsdp_7.1 = bf16[8,128,256]{2,1,0:T(8,128)(2,1)} custom-call(bf16[8,128,256]{2,1,0:T(8,128)(2,1)} %bitcast.109), custom_call_target="tpu_custom_call" | custom-call | bytes 46200000 | tf_op jit(solution)/shard_map/exchange_fsdp_7/pallas_call | solution.py:91
  162.1 5.3 all-gather.2.cloned.1.call-done
  167.4 4.8 multiply_reduce_fusion.3
  173.2 42.9 %gather_line_8.1 = bf16[8,128,2048]{2,1,0:T(8,128)(2,1)} custom-call(bf16[128,2048]{1,0:T(8,128)(2,1)} %fusion.7.given), custom_call_target="tpu_custom_call" | custom-call | bytes 132000000 | tf_op jit(solution)/shard_map/gather_line_8/pallas_call | solution.py:217
  216.2 8.0 %fusion.12 = f32[1024,1024]{1,0:T(8,128)S(1)} fusion(bf16[1024,2048]{1,0:T(8,128)(2,1)} %bitcast.97, bf16[2048,1024]{1,0:T(8,128)(2,1)} %param.18), kind=kOutput, calls=%fused_computation.53 | convolution fusion | flops 4294967296 | bytes 12582912 | tf_op jit(solution)/shard_map/dot_general | solution.py:1118
  224.2 6.5 multiply_convert_fusion.2
  230.7 6.7 fusion.13
  237.4 44.4 %reduce_line_9.1 = f32[128,2048]{1,0:T(8,128)} custom-call(f32[8,128,2048]{2,1,0:T(8,128)} %bitcast.95), custom_call_target="tpu_custom_call" | custom-call | bytes 138600000 | tf_op jit(solution)/shard_map/reduce_line_9/pallas_call | solution.py:366
  287.0 41.2 %gather_line_10.1 = bf16[8,128,2048]{2,1,0:T(8,128)(2,1)} custom-call(bf16[128,2048]{1,0:T(8,128)(2,1)} %fusion.4.given), custom_call_target="tpu_custom_call" | custom-call | bytes 132000000 | tf_op jit(solution)/shard_map/gather_line_10/pallas_call | solution.py:217
  328.2 9.5 %convolution_convert_fusion.2 = bf16[1024,2048]{1,0:T(8,128)(2,1)} fusion(bf16[1024,1024]{1,0:T(8,128)(2,1)} %copy-done.20, bf16[1024,2048]{1,0:T(8,128)(2,1)} %bitcast.103), kind=kOutput, calls=%fused_computation.10 | convolution fusion | flops 4297064448 | bytes 10485760 | tf_op jit(solution)/shard_map/dot_general | solution.py:1126
  337.8 8.8 %multiply_convert_fusion = (bf16[1024,1024]{1,0:T(8,128)(2,1)S(1)}, bf16[1024,1024]{1,0:T(8,128)(2,1)}) fusion(f32[1024,1024]{1,0:T(8,128)S(1)} %copy-done.24, f32[1024,1024]{1,0:T(8,128)} %get-tuple-element.92, bf16[1024,2048]{1,0:T(8,128)(2,1)S(1)} %bitcast.104, bf16[1024,2048]{1,0:T(8,128)(2,1)S(1)} %copy-done.16), kind=kOutput, calls=%fused_computation.2 | convolution fusion | flops 4308598784 | bytes 20971520 | tf_op jit(solution)/shard_map/dot_general | solution.py:1122
  346.6 6.2 convolution_convert_fusion
  352.9 6.2 convolution_convert_fusion.1
  359.6 7.2 fusion.14
  366.8 6.8 convolution_add_fusion
  373.6 44.6 %reduce_line_11.1 = f32[128,2048]{1,0:T(8,128)} custom-call(f32[8,128,2048]{2,1,0:T(8,128)} %bitcast.94), custom_call_target="tpu_custom_call" | custom-call | bytes 138600000 | tf_op jit(solution)/shard_map/reduce_line_11/pallas_call | solution.py:366
  422.7 41.4 %gather_line_12.1 = bf16[8,128,2048]{2,1,0:T(8,128)(2,1)} custom-call(bf16[128,2048]{1,0:T(8,128)(2,1)} %get-tuple-element.81.given), custom_call_target="tpu_custom_call" | custom-call | bytes 132000000 | tf_op jit(solution)/shard_map/gather_line_12/pallas_call | solution.py:217
  468.3 15.1 %exchange_ctx_13.1.grad_ref = bf16[4,2,128,256]{3,2,1,0:T(8,128)(2,1)} custom-call(bf16[4,2,128,256]{3,2,1,0:T(8,128)(2,1)} %bitcast.115), custom_call_target="tpu_custom_call" | custom-call | bytes 33000000 | tf_op jit(solution)/shard_map/exchange_ctx_13/pallas_call | solution.py:91
  483.4 15.8 %attend_back.1 = (f32[4,2,128,256]{3,2,1,0:T(8,128)}, f32[4,2,128,256]{3,2,1,0:T(8,128)}, bf16[4,2,128,256]{3,2,1,0:T(8,128)(2,1)}) custom-call(bf16[4,3,2,128,256]{4,3,2,1,0:T(8,128)(2,1)} %get-tuple-element.45.query_ref.key_ref.value_ref, bf16[4,3,2,128,256]{4,3,2,1,0:T(8,128)(2,1)} %get-tuple-element.45.query_ref.key_ref.value_ref, ...), custom_call_target="tpu_custom_call" | custom-call | bytes 52800000 | tf_op jit(solution)/shard_map/attend_back/pallas_call | solution.py:1085
  499.3 70.6 %heads_back.1 = (bf16[8,128,768]{2,1,0:T(8,128)(2,1)}, f32[2,256]{1,0:T(2,128)}) custom-call(s32[8,128,1]{2,1,0:T(8,128)} %broadcast_in_dim_reshape.4.row_blocks, f32[4,2,128,256]{3,2,1,0:T(8,128)} %get-tuple-element.50.grad_query, f32[4,2,128,256]{3,2,1,0:T(8,128)} %get-tuple-element.51.grad_key, bf16[4,2,128,256]{3,2,1,0:T(8,128)(2,1)} %get-tuple-element.52.grad_value, ...), custom_call_target="tpu_custom_call" | custom-call | bytes 148500000 | tf_op jit(solution)/shard_map/heads_back/pallas_call | solution.py:802
  569.8 6.5 bitcast_convert_fusion
  582.5 49.1 %all-reduce.5.cloned.1.call-done = (bf16[1024,2048]{1,0:T(8,128)(2,1)}, bf16[2048,1024]{1,0:T(8,128)(2,1)}, bf16[2048,1024]{1,0:T(8,128)(2,1)}) async-done(((bf16[1024,2048]{1,0:T(8,128)(2,1)}, bf16[2048,1024]{1,0:T(8,128)(2,1)}, bf16[2048,1024]{1,0:T(8,128)(2,1)}), (bf16[1024,2048]{1,0:T(8,128)(2,1)}, bf16[2048,1024]{1,0:T(8,128)(2,1)}, bf16[2048,1024]{1,0:T(8,128)(2,1)})) %all-reduce.5.cloned.1.call-update) | async-done | bytes 12582928 | tf_op jit(solution)/shard_map/psum | solution.py:1212
  631.7 7.6 fusion.15.given
  639.2 45.4 %reduce_line_16.1 = f32[128,2048]{1,0:T(8,128)} custom-call(f32[8,128,2048]{2,1,0:T(8,128)} %fusion.15.given), custom_call_target="tpu_custom_call" | custom-call | bytes 138600000 | tf_op jit(solution)/shard_map/reduce_line_16/pallas_call | solution.py:366
  687.7 6.8 convert_element_type.120
  694.5 4.4 convert_element_type.121
  698.9 4.4 convert_element_type.122
  703.4 54.2 %finish.1 = (bf16[4,4,64,2048]{3,2,1,0:T(8,128)(2,1)}, f32[4,256]{1,0:T(4,128)}) custom-call(bf16[64,8192]{1,0:T(8,128)(2,1)} %bitcast.113, f32[8,2,256]{2,1,0:T(2,128)} %maximum_bitcast_fusion.gain_post, f32[2,256]{1,0:T(2,128)} %get-tuple-element.62.gain_heads), custom_call_target="tpu_custom_call" | custom-call | bytes 165000000 | tf_op jit(solution)/shard_map/finish/pallas_call | solution.py:959
  (100 shorter events, 41.9 us)
Async XLA Ops:
  7.2 68.0 %copy-start.13 = (bf16[4,256]{1,0:T(4,128)(2,1)S(1)}, bf16[4,256]{1,0:T(4,128)(2,1)}, u32[]{:S(2)}) copy-start(bf16[4,256]{1,0:T(4,128)(2,1)} %param.21) | copy-start | bytes 6148
  7.2 160.2 %all-gather.2.cloned.1.call-start = ((), (), s32[]{:S(2)}) async-start(), calls=%async_computation.1 | async-start | bytes 9437184 | tf_op jit(solution)/shard_map/all_gather | solution.py:1162
  75.1 556.5 %all-reduce.5.cloned.1.call-start = ((), (), s32[]{:S(2)}) async-start(), calls=%async_computation.3 | async-start | bytes 25165824 | tf_op jit(solution)/shard_map/psum | solution.py:1212
  119.9 42.1 %copy-start.12 = (f32[8,5,256]{2,1,0:T(8,128)S(1)}, f32[8,5,256]{2,1,0:T(8,128)}, u32[]{:S(2)}) copy-start(f32[8,5,256]{2,1,0:T(8,128)} %get-tuple-element.39) | copy-start | bytes 122884
  167.4 4.8 copy-start.3
  216.1 8.0 %copy-start.6 = (bf16[8,128,2048]{2,1,0:T(8,128)(2,1)S(1)}, bf16[8,128,2048]{2,1,0:T(8,128)(2,1)}, u32[]{:S(2)}) copy-start(bf16[8,128,2048]{2,1,0:T(8,128)(2,1)} %gather_line_8.1) | copy-start | bytes 12582916
  216.2 8.0 %copy-start.17 = (bf16[2048,1024]{1,0:T(8,128)(2,1)S(1)}, bf16[2048,1024]{1,0:T(8,128)(2,1)}, u32[]{:S(2)}) copy-start(bf16[2048,1024]{1,0:T(8,128)(2,1)} %param.19) | copy-start | bytes 12582916
  224.2 6.5 copy-start.23
  224.2 6.5 copy-start.15
  230.7 6.7 copy-start.20
  237.4 45.8 %copy-start.2 = (bf16[1,128,2048]{2,1,0:T(8,128)(2,1)S(1)}, bf16[1,128,2048]{2,1,0:T(8,128)(2,1)}, u32[]{:S(2)}) copy-start(bf16[1,128,2048]{2,1,0:T(8,128)(2,1)} %param.22) | copy-start | bytes 1572868
  328.2 9.5 %copy-start.9 = (bf16[8,128,2048]{2,1,0:T(8,128)(2,1)S(1)}, bf16[8,128,2048]{2,1,0:T(8,128)(2,1)}, u32[]{:S(2)}) copy-start(bf16[8,128,2048]{2,1,0:T(8,128)(2,1)} %gather_line_10.1) | copy-start | bytes 12582916
  328.2 9.5 %copy-start.16 = (bf16[1024,2048]{1,0:T(8,128)(2,1)S(1)}, bf16[1024,2048]{1,0:T(8,128)(2,1)}, u32[]{:S(2)}) copy-start(bf16[1024,2048]{1,0:T(8,128)(2,1)} %param.20) | copy-start | bytes 12582916
  328.2 9.5 %copy-start.24 = (f32[1024,1024]{1,0:T(8,128)S(1)}, f32[1024,1024]{1,0:T(8,128)}, u32[]{:S(2)}) copy-start(f32[1024,1024]{1,0:T(8,128)} %copy-done.23) | copy-start | bytes 12582916
  337.8 8.8 %copy-start.7 = (bf16[8,128,2048]{2,1,0:T(8,128)(2,1)S(1)}, bf16[8,128,2048]{2,1,0:T(8,128)(2,1)}, u32[]{:S(2)}) copy-start(bf16[8,128,2048]{2,1,0:T(8,128)(2,1)} %gather_line_8.1) | copy-start | bytes 12582916
  346.6 6.2 copy-start.21
  346.6 6.2 copy-start.25
  359.1 344.3 %reduce-scatter.4.cloned.1.call-start = ((), (), s32[]{:S(2)}) async-start(), calls=%async_computation.2 | async-start | bytes 5242880
  359.6 7.2 copy-start.18
  359.6 7.2 copy-start.22
  373.6 46.1 %copy-start = (f32[128,2048]{1,0:T(8,128)S(1)}, f32[128,2048]{1,0:T(8,128)}, u32[]{:S(2)}) copy-start(f32[128,2048]{1,0:T(8,128)} %reduce_line_9.1) | copy-start | bytes 3145732
  422.7 41.4 %copy-start.11 = (bf16[256,2048]{1,0:T(8,128)(2,1)S(1)}, bf16[256,2048]{1,0:T(8,128)(2,1)}, u32[]{:S(2)}) copy-start(bf16[256,2048]{1,0:T(8,128)(2,1)} %param.17) | copy-start | bytes 3145732
  576.4 2.4 copy-start.8
  576.4 2.6 copy-start.10
  582.5 49.2 %copy-start.19 = (bf16[8,128,768]{2,1,0:T(8,128)(2,1)S(1)}, bf16[8,128,768]{2,1,0:T(8,128)(2,1)}, u32[]{:S(2)}) copy-start(bf16[8,128,768]{2,1,0:T(8,128)(2,1)} %get-tuple-element.55) | copy-start | bytes 4718596
  639.2 46.1 %copy-start.1 = (f32[128,2048]{1,0:T(8,128)S(1)}, f32[128,2048]{1,0:T(8,128)}, u32[]{:S(2)}) copy-start(f32[128,2048]{1,0:T(8,128)} %reduce_line_11.1) | copy-start | bytes 3145732
  687.7 6.8 copy-start.5
  694.5 4.4 copy-start.4
  763.1 2.7 copy-start.14
Sparse Core Ops, SparseCore 0:
  75.2 92.0 all-gather.1
  359.2 272.3 all-reduce.4
  634.6 52.6 reduce-scatter.3

commit v3 on v2

--- a/solution.py
+++ b/solution.py
@@ -125,82 +125,112 @@
     pl.semaphore_wait(barrier, expected)
 
 
-def pass_along(chips, given, kept, local, send_sem, land_sem, between=None):
+CUTS = 4
+
+
+def pass_along(chips, given, kept, local, send_sem, land_sem, between=None, use=None):
     own = lax.axis_index("fsdp")
     chip, core = own // 2, own % 2
     sibling = chip * 2 + 1 - core
-
-    def copy(source, place, way, step, target):
+    height = given.shape[0] // CUTS
+
+    def copy(source, place, way, step, cut, target):
+        rows = pl.ds(cut * height, height)
         return remote(
-            source, kept.at[place], send_sem.at[way, step], land_sem.at[place], {"fsdp": target}
+            source.at[rows],
+            kept.at[place, rows],
+            send_sem.at[way, step, cut],
+            land_sem.at[place, cut],
+            {"fsdp": target},
         )
 
-    @pl.when(chip < chips - 1)
-    def _():
-        copy(given, own, 0, 0, own + 2).start()
-
-    @pl.when(chip > 0)
-    def _():
-        copy(given, own, 1, 0, own - 2).start()
-
-    copy(given, own, 2, 0, sibling).start()
+    def both_ways(step, cut, left_does, right_does):
+        from_left, from_right = own - 2 * step, own + 2 * step
+
+        @pl.when(chip >= step)
+        def _():
+            left_does(from_left, step, cut)
+
+        @pl.when(chip + step < chips)
+        def _():
+            right_does(from_right, step, cut)
+
+    def hand_on(way, nearer, side):
+        def does(place, step, cut):
+            copy(kept.at[place], place, way, step, cut, own).wait_recv()
+
+            @pl.when((chip < chips - 1) if way == 0 else (chip > 0))
+            def _():
+                copy(kept.at[place], place, way, step, cut, nearer).start()
+
+            copy(kept.at[place], place, side, step, cut, sibling).start()
+
+        return does
+
+    def sent(way, nearer, side):
+        def does(place, step, cut):
+            @pl.when((chip < chips - 1) if way == 0 else (chip > 0))
+            def _():
+                copy(kept.at[place], place, way, step, cut, nearer).wait_send()
+
+            copy(kept.at[place], place, side, step, cut, sibling).wait_send()
+
+        return does
+
+    def from_sibling(other):
+        place = other * 2 + 1 - core
+        for cut in range(CUTS):
+            copy(kept.at[place], place, 2, 0, cut, sibling).wait_recv()
+        if use:
+            use(other)
+
+    for cut in range(CUTS):
+
+        @pl.when(chip < chips - 1)
+        def _():
+            copy(given, own, 0, 0, cut, own + 2).start()
+
+        @pl.when(chip > 0)
+        def _():
+            copy(given, own, 1, 0, cut, own - 2).start()
+
+        copy(given, own, 2, 0, cut, sibling).start()
     local.wait()
     result = between() if between else None
+    from_sibling(chip)
     for step in range(1, chips):
-        from_left, from_right = own - 2 * step, own + 2 * step
+        for cut in range(CUTS):
+            both_ways(step, cut, hand_on(0, own + 2, 2), hand_on(1, own - 2, 3))
 
         @pl.when(chip >= step)
         def _():
-            copy(kept.at[from_left], from_left, 0, step, own).wait_recv()
-
-            @pl.when(chip < chips - 1)
-            def _():
-                copy(kept.at[from_left], from_left, 0, step, own + 2).start()
-
-            copy(kept.at[from_left], from_left, 2, step, sibling).start()
+            from_sibling(chip - step)
 
         @pl.when(chip + step < chips)
         def _():
-            copy(kept.at[from_right], from_right, 1, step, own).wait_recv()
-
-            @pl.when(chip > 0)
-            def _():
-                copy(kept.at[from_right], from_right, 1, step, own - 2).start()
-
-            copy(kept.at[from_right], from_right, 3, step, sibling).start()
-
-    for other in range(chips):
-        place = other * 2 + 1 - core
-        copy(kept.at[place], place, 2, 0, sibling).wait_recv()
-
-    @pl.when(chip < chips - 1)
-    def _():
-        copy(given, own, 0, 0, own + 2).wait_send()
-
-    @pl.when(chip > 0)
-    def _():
-        copy(given, own, 1, 0, own - 2).wait_send()
-
-    copy(given, own, 2, 0, sibling).wait_send()
-    for step in range(1, chips):
-        from_left, from_right = own - 2 * step, own + 2 * step
-
-        @pl.when(chip >= step)
+            from_sibling(chip + step)
+
+    for cut in range(CUTS):
+
+        @pl.when(chip < chips - 1)
         def _():
-            @pl.when(chip < chips - 1)
-            def _():
-                copy(kept.at[from_left], from_left, 0, step, own + 2).wait_send()
-
-            copy(kept.at[from_left], from_left, 2, step, sibling).wait_send()
-
-        @pl.when(chip + step < chips)
+            copy(given, own, 0, 0, cut, own + 2).wait_send()
+
+        @pl.when(chip > 0)
         def _():
-            @pl.when(chip > 0)
-            def _():
-                copy(kept.at[from_right], from_right, 1, step, own - 2).wait_send()
-
-            copy(kept.at[from_right], from_right, 3, step, sibling).wait_send()
+            copy(given, own, 1, 0, cut, own - 2).wait_send()
+
+        copy(given, own, 2, 0, cut, sibling).wait_send()
+        for step in range(1, chips):
+            both_ways(step, cut, sent(0, own + 2, 2), sent(1, own - 2, 3))
     return result
+
+
+def line_semaphores(owners):
+    return [
+        pltpu.SemaphoreType.DMA((4, owners // 2, CUTS)),
+        pltpu.SemaphoreType.DMA((owners, CUTS)),
+    ]
 
 
 def gather_kernel(chips, given, kept, own_sem, send_sem, land_sem):
@@ -213,17 +243,12 @@
 
 def gather_line(shard, key):
     size = lax.axis_size("fsdp")
-    chips = size // 2
     kept = pl.pallas_call(
-        functools.partial(gather_kernel, chips),
+        functools.partial(gather_kernel, size // 2),
         out_shape=jax.ShapeDtypeStruct((size,) + shard.shape, shard.dtype),
         in_specs=[in_vmem()],
         out_specs=anywhere(),
-        scratch_shapes=[
-            pltpu.SemaphoreType.DMA,
-            pltpu.SemaphoreType.DMA((4, chips)),
-            pltpu.SemaphoreType.DMA((size,)),
-        ],
+        scratch_shapes=[pltpu.SemaphoreType.DMA] + line_semaphores(size),
         compiler_params=pltpu.CompilerParams(collective_id=key, has_side_effects=True),
         cost_estimate=lasting(40),
         name=f"gather_line_{key}",
@@ -231,33 +256,250 @@
     return kept.reshape((size * shard.shape[0],) + shard.shape[1:])
 
 
-def reduce_kernel(
+TILE = 512
+
+
+def each_tile(columns, does):
+    width = min(TILE, columns)
+
+    def step(at, carry):
+        does(pl.ds(pl.multiple_of(at * width, width), width))
+        return carry
+
+    lax.fori_loop(0, columns // width, step, 0)
+
+
+def chip_rows(ref, other):
+    taken = ref[pl.ds(other * 2, 2)]
+    return taken.reshape(2 * taken.shape[1], taken.shape[2])
+
+
+def put_chip(ref, other, columns, values):
+    rows = ref.shape[1]
+    ref[other * 2, :, columns] = values[:rows]
+    ref[other * 2 + 1, :, columns] = values[rows:]
+
+
+def ffn_in_kernel(
     chips,
-    wire,
     given,
-    total,
-    mine,
-    beside,
-    from_left,
-    from_right,
-    outgoing,
-    load_sem,
-    side_send,
-    side_land,
-    line_send,
-    left_land,
-    right_land,
+    w_gate,
+    w_up,
+    rows_out,
+    gate_out,
+    up_out,
+    hidden_out,
+    rows,
+    gate_w,
+    up_w,
+    gate,
+    upward,
+    hidden,
+    own_sem,
+    send_sem,
+    land_sem,
+    out_sem,
 ):
+    own = lax.axis_index("fsdp")
+    local = pltpu.make_async_copy(given, rows.at[own], own_sem.at[0])
+    local.start()
+    load = [
+        pltpu.make_async_copy(w_gate, gate_w, own_sem.at[1]),
+        pltpu.make_async_copy(w_up, up_w, own_sem.at[2]),
+    ]
+    for copy in load:
+        copy.start()
+    greet_line(own, chips)
+
+    def stores(other):
+        place = pl.ds(other * 2, 2)
+        pairs = ((rows, rows_out), (gate, gate_out), (upward, up_out), (hidden, hidden_out))
+        return [
+            pltpu.make_async_copy(source.at[place], target.at[place], out_sem.at[item, other])
+            for item, (source, target) in enumerate(pairs)
+        ]
+
+    def use(other):
+        left = chip_rows(rows, other)
+
+        def tile(columns):
+            gated = jnp.dot(left, gate_w[:, columns], preferred_element_type=f32)
+            raised = jnp.dot(left, up_w[:, columns], preferred_element_type=f32)
+            put_chip(gate, other, columns, gated)
+            put_chip(upward, other, columns, raised)
+            put_chip(
+                hidden, other, columns, (gated * jax.nn.sigmoid(gated) * raised).astype(bf16)
+            )
+
+        each_tile(gate_w.shape[1], tile)
+        for copy in stores(other):
+            copy.start()
+
+    def loaded():
+        for copy in load:
+            copy.wait()
+
+    pass_along(chips, given, rows, local, send_sem, land_sem, loaded, use)
+    for other in range(chips):
+        for copy in stores(other):
+            copy.wait()
+
+
+def ffn_in(shard, w_gate, w_up):
+    owners = lax.axis_size("fsdp")
+    rows, width = shard.shape
+    units = w_gate.shape[1]
+    wide, narrow = (owners, rows, width), (owners, rows, units)
+    return pl.pallas_call(
+        functools.partial(ffn_in_kernel, owners // 2),
+        out_shape=[
+            jax.ShapeDtypeStruct(wide, bf16),
+            jax.ShapeDtypeStruct(narrow, f32),
+            jax.ShapeDtypeStruct(narrow, f32),
+            jax.ShapeDtypeStruct(narrow, bf16),
+        ],
+        in_specs=[in_vmem(), anywhere(), anywhere()],
+        out_specs=[anywhere()] * 4,
+        scratch_shapes=[
+            pltpu.VMEM(wide, bf16),
+            pltpu.VMEM((width, units), bf16),
+            pltpu.VMEM((width, units), bf16),
+            pltpu.VMEM(narrow, f32),
+            pltpu.VMEM(narrow, f32),
+            pltpu.VMEM(narrow, bf16),
+            pltpu.SemaphoreType.DMA((3,)),
+        ]
+        + line_semaphores(owners)
+        + [pltpu.SemaphoreType.DMA((4, owners // 2))],
+        compiler_params=pltpu.CompilerParams(
+            collective_id=4, has_side_effects=True, vmem_limit_bytes=60 * 1024 * 1024
+        ),
+        cost_estimate=lasting(45),
+        name="ffn_in",
+    )(shard, w_gate, w_up)
+
+
+def ffn_back_kernel(
+    chips,
+    given,
+    w_down,
+    gate_in,
+    up_in,
+    rows_out,
+    gate_out,
+    up_out,
+    rows,
+    down_w,
+    gate,
+    upward,
+    grad_gate,
+    grad_up,
+    own_sem,
+    send_sem,
+    land_sem,
+    out_sem,
+):
+    own = lax.axis_index("fsdp")
+    local = pltpu.make_async_copy(given, rows.at[own], own_sem.at[0])
+    local.start()
+    load = [
+        pltpu.make_async_copy(w_down, down_w, own_sem.at[1]),
+        pltpu.make_async_copy(gate_in, gate, own_sem.at[2]),
+        pltpu.make_async_copy(up_in, upward, own_sem.at[3]),
+    ]
+    for copy in load:
+        copy.start()
+    greet_line(own, chips)
+
+    def stores(other):
+        place = pl.ds(other * 2, 2)
+        pairs = ((rows, rows_out), (grad_gate, gate_out), (grad_up, up_out))
+        return [
+            pltpu.make_async_copy(source.at[place], target.at[place], out_sem.at[item, other])
+            for item, (source, target) in enumerate(pairs)
+        ]
+
+    def use(other):
+        left = chip_rows(rows, other)
+        height = rows.shape[1]
+
+        def tile(columns):
+            grad_hidden = lax.dot_general(
+                left, down_w[columns, :], (((1,), (1,)), ((), ())), preferred_element_type=f32
+            )
+            for half in range(2):
+                grad = grad_hidden[half * height : (half + 1) * height]
+                gated, raised = (
+                    gate[other * 2 + half, :, columns],
+                    upward[other * 2 + half, :, columns],
+                )
+                sigma = jax.nn.sigmoid(gated)
+                grad_gate[other * 2 + half, :, columns] = (
+                    grad * raised * sigma * (1.0 + gated * (1.0 - sigma))
+                ).astype(bf16)
+                grad_up[other * 2 + half, :, columns] = (grad * (gated * sigma)).astype(bf16)
+
+        each_tile(down_w.shape[0], tile)
+        for copy in stores(other):
+            copy.start()
+
+    def loaded():
+        for copy in load:
+            copy.wait()
+
+    pass_along(chips, given, rows, local, send_sem, land_sem, loaded, use)
+    for other in range(chips):
+        for copy in stores(other):
+            copy.wait()
+
+
+def ffn_back(shard, w_down, gate, upward):
+    owners = lax.axis_size("fsdp")
+    rows, width = shard.shape
+    units = w_down.shape[0]
+    wide, narrow = (owners, rows, width), (owners, rows, units)
+    return pl.pallas_call(
+        functools.partial(ffn_back_kernel, owners // 2),
+        out_shape=[
+            jax.ShapeDtypeStruct(wide, bf16),
+            jax.ShapeDtypeStruct(narrow, bf16),
+            jax.ShapeDtypeStruct(narrow, bf16),
+        ],
+        in_specs=[in_vmem(), anywhere(), anywhere(), anywhere()],
+        out_specs=[anywhere()] * 3,
+        scratch_shapes=[
+            pltpu.VMEM(wide, bf16),
+            pltpu.VMEM((units, width), bf16),
+            pltpu.VMEM(narrow, f32),
+            pltpu.VMEM(narrow, f32),
+            pltpu.VMEM(narrow, bf16),
+            pltpu.VMEM(narrow, bf16),
+            pltpu.SemaphoreType.DMA((4,)),
+        ]
+        + line_semaphores(owners)
+        + [pltpu.SemaphoreType.DMA((3, owners // 2))],
+        compiler_params=pltpu.CompilerParams(
+            collective_id=5, has_side_effects=True, vmem_limit_bytes=60 * 1024 * 1024
+        ),
+        cost_estimate=lasting(45),
+        name="ffn_back",
+    )(shard, w_down, gate, upward)
+
+
+def reduce_kernel(chips, wire, count, turned, *refs):
+    left_in, right_in, total = refs[:count], refs[count : 2 * count], refs[2 * count]
+    refs = refs[2 * count + 1 :]
+    left, right, refs = refs[:count], refs[count : 2 * count], refs[2 * count :]
+    mine, aside, beside, from_left, from_right, outgoing = refs[:6]
+    load_sem, side_send, side_land, line_send, left_land, right_land = refs[6:]
     own = lax.axis_index("fsdp")
     chip, core = own // 2, own % 2
     sibling = chip * 2 + 1 - core
-
-    def load(other):
-        return pltpu.make_async_copy(given.at[other * 2 + core], mine.at[other], load_sem.at[other])
+    rows = total.shape[0]
 
     def side(other):
         return remote(
-            given.at[other * 2 + 1 - core],
+            aside.at[other],
             beside.at[other],
             side_send.at[other],
             side_land.at[other],
@@ -282,63 +524,97 @@
             {"fsdp": target},
         )
 
-    for other in range(chips):
-        load(other).start()
+    load = [
+        pltpu.make_async_copy(source, target, load_sem.at[item])
+        for item, (source, target) in enumerate(zip(left_in + right_in, left + right))
+    ]
+    for copy in load:
+        copy.start()
     greet_line(own, chips)
-    for tick in range(chips - 1):
-        right_to = chips - 1 - (tick - chip)
-        left_to = tick - (chips - 1 - chip)
-
-        @pl.when((tick >= chip) & (right_to > chip))
+    for copy in load:
+        copy.wait()
+
+    def multiply(other):
+        lefts = [chip_rows(ref, other) for ref in left]
+
+        def tile(columns):
+            product = None
+            for item in range(count):
+                if turned:
+                    part = lax.dot_general(
+                        lefts[item],
+                        right[item][columns, :],
+                        (((1,), (1,)), ((), ())),
+                        preferred_element_type=f32,
+                    )
+                else:
+                    part = jnp.dot(
+                        lefts[item], right[item][:, columns], preferred_element_type=f32
+                    )
+                product = part if product is None else product + part
+
+            @pl.when(core == 0)
+            def _():
+                mine[other, :, columns] = product[:rows]
+                aside[other, :, columns] = product[rows:]
+
+            @pl.when(core == 1)
+            def _():
+                mine[other, :, columns] = product[rows:]
+                aside[other, :, columns] = product[:rows]
+
+        each_tile(total.shape[1], tile)
+        side(other).start()
+
+    def each_turn(right_does, left_does):
+        for tick in range(chips - 1):
+            right_to = chips - 1 - (tick - chip)
+            left_to = tick - (chips - 1 - chip)
+
+            @pl.when((tick >= chip) & (right_to > chip))
+            def _():
+                right_does(right_to)
+
+            @pl.when((left_to >= 0) & (left_to < chip))
+            def _():
+                left_does(left_to)
+
+    each_turn(multiply, multiply)
+    multiply(chip)
+
+    def send_right(other):
+        side(other).wait_recv()
+
+        @pl.when(chip > 0)
         def _():
-            side(right_to).start()
-
-        @pl.when((left_to >= 0) & (left_to < chip))
+            rightward(other, own).wait_recv()
+            outgoing[other] = (
+                mine[other] + beside[other] + from_left[other].astype(f32)
+            ).astype(wire)
+
+        @pl.when(chip == 0)
         def _():
-            side(left_to).start()
-
-    side(chip).start()
-    for tick in range(chips - 1):
-        right_to = chips - 1 - (tick - chip)
-        left_to = tick - (chips - 1 - chip)
-
-        @pl.when((tick >= chip) & (right_to > chip))
+            outgoing[other] = (mine[other] + beside[other]).astype(wire)
+
+        rightward(other, own + 2).start()
+
+    def send_left(other):
+        side(other).wait_recv()
+
+        @pl.when(chip < chips - 1)
         def _():
-            load(right_to).wait()
-            side(right_to).wait_recv()
-
-            @pl.when(chip > 0)
-            def _():
-                rightward(right_to, own).wait_recv()
-                outgoing[right_to] = (
-                    mine[right_to] + beside[right_to] + from_left[right_to].astype(f32)
-                ).astype(wire)
-
-            @pl.when(chip == 0)
-            def _():
-                outgoing[right_to] = (mine[right_to] + beside[right_to]).astype(wire)
-
-            rightward(right_to, own + 2).start()
-
-        @pl.when((left_to >= 0) & (left_to < chip))
+            leftward(other, own).wait_recv()
+            outgoing[other] = (
+                mine[other] + beside[other] + from_right[other].astype(f32)
+            ).astype(wire)
+
+        @pl.when(chip == chips - 1)
         def _():
-            load(left_to).wait()
-            side(left_to).wait_recv()
-
-            @pl.when(chip < chips - 1)
-            def _():
-                leftward(left_to, own).wait_recv()
-                outgoing[left_to] = (
-                    mine[left_to] + beside[left_to] + from_right[left_to].astype(f32)
-                ).astype(wire)
-
-            @pl.when(chip == chips - 1)
-            def _():
-                outgoing[left_to] = (mine[left_to] + beside[left_to]).astype(wire)
-
-            leftward(left_to, own - 2).start()
-
-    load(chip).wait()
+            outgoing[other] = (mine[other] + beside[other]).astype(wire)
+
+        leftward(other, own - 2).start()
+
+    each_turn(send_right, send_left)
     side(chip).wait_recv()
     total[...] = mine[chip] + beside[chip]
 
@@ -360,21 +636,24 @@
             rightward(other, own).wait_send()
 
 
-def reduce_line(partial, key, wire=f32):
-    size, rows, width = partial.shape
-    chips = size // 2
+def reduce_line(lefts, rights, key, turned=False, wire=bf16):
+    owners, rows, _ = lefts[0].shape
+    width = rights[0].shape[0 if turned else 1]
+    chips, count = owners // 2, len(lefts)
     return pl.pallas_call(
-        functools.partial(reduce_kernel, chips, wire),
+        functools.partial(reduce_kernel, chips, wire, count, turned),
         out_shape=jax.ShapeDtypeStruct((rows, width), f32),
-        in_specs=[anywhere()],
+        in_specs=[anywhere()] * (2 * count),
         out_specs=in_vmem(),
-        scratch_shapes=[
+        scratch_shapes=[pltpu.VMEM(item.shape, item.dtype) for item in lefts + rights]
+        + [
+            pltpu.VMEM((chips, rows, width), f32),
             pltpu.VMEM((chips, rows, width), f32),
             pltpu.VMEM((chips, rows, width), f32),
             pltpu.VMEM((chips, rows, width), wire),
             pltpu.VMEM((chips, rows, width), wire),
             pltpu.VMEM((chips, rows, width), wire),
-            pltpu.SemaphoreType.DMA((chips,)),
+            pltpu.SemaphoreType.DMA((2 * count,)),
             pltpu.SemaphoreType.DMA((chips,)),
             pltpu.SemaphoreType.DMA((chips,)),
             pltpu.SemaphoreType.DMA((chips,)),
@@ -382,11 +661,11 @@
             pltpu.SemaphoreType.DMA((chips,)),
         ],
         compiler_params=pltpu.CompilerParams(
-            collective_id=key, has_side_effects=True, vmem_limit_bytes=60 * 1024 * 1024
+            collective_id=key, has_side_effects=True, vmem_limit_bytes=63 * 1024 * 1024
         ),
-        cost_estimate=lasting(78 if wire == f32 else 42),
+        cost_estimate=lasting(45),
         name=f"reduce_line_{key}",
-    )(partial)
+    )(*lefts, *rights)
 
 
 def greet_peers(axes):
@@ -515,7 +794,6 @@
     piece = weights[0].shape[0] // parts
     inverse = rope_base ** (-(np.arange(HEAD_DIM // 2, dtype=np.float32) * 2.0) / HEAD_DIM)
     inverse = jnp.asarray(np.concatenate([inverse, inverse])[None], f32)
-    chips = owners // 2
     return pl.pallas_call(
         functools.partial(start_kernel, owners, parts),
         out_shape=[
@@ -535,9 +813,8 @@
             pltpu.SemaphoreType.DMA((3, owners)),
             pltpu.SemaphoreType.DMA((parts,)),
             pltpu.SemaphoreType.DMA((parts,)),
-            pltpu.SemaphoreType.DMA((4, chips)),
-            pltpu.SemaphoreType.DMA((owners,)),
-        ],
+        ]
+        + line_semaphores(owners),
         compiler_params=pltpu.CompilerParams(collective_id=0, has_side_effects=True),
         cost_estimate=lasting(60),
         name="start",
@@ -1183,35 +1460,30 @@
     projected = mm(mixed_own, full_output)
     proj_scale = norm_stat(projected)
     residual = tokens_f + projected * proj_scale * gains[2]
-    mlp_rows_in = gather_line(residual.astype(bf16), 8)
-    gate = mm(mlp_rows_in, w_gate)
-    upward = mm(mlp_rows_in, w_up)
-    sigma = jax.nn.sigmoid(gate)
-    hidden_b = (gate * sigma * upward).astype(bf16)
-    mlp_out = reduce_line(mm(hidden_b, w_down).reshape(owners, rows, width), 9, wire=bf16)
+    mlp_rows_in, gate, upward, hidden = ffn_in(residual.astype(bf16), w_gate, w_up)
+    mlp_out = reduce_line([hidden], [w_down], 9)
     mlp_scale = norm_stat(mlp_out)
     block_out = residual + mlp_out * mlp_scale * gains[3]
 
     grad_y = out_grad[0].astype(f32)
     grad_mlp, gain_ff = norm_back(mlp_out, mlp_scale, gains[3], grad_y)
-    grad_rows = gather_line(grad_mlp.astype(bf16), 10)
-    grad_rows, down_part = lax.optimization_barrier(
-        (grad_rows, mm_tn(hidden_b, grad_rows).astype(bf16))
-    )
-    grad_hidden = mm_nt(grad_rows, w_down)
-    grad_gate_b = (grad_hidden * upward * sigma * (1.0 + gate * (1.0 - sigma))).astype(bf16)
-    grad_up_b = (grad_hidden * (gate * sigma)).astype(bf16)
-    grad_gate_b, grad_up_b, gate_part, up_part = lax.optimization_barrier(
+    grad_rows, grad_gate, grad_up = ffn_back(grad_mlp.astype(bf16), w_down, gate, upward)
+
+    def summed_over_rows(left, right):
+        left, right = left.reshape(group, -1), right.reshape(group, -1)
+        return mm_tn(left, right).astype(bf16)
+
+    grad_gate, grad_up, *ffn_parts = lax.optimization_barrier(
         (
-            grad_gate_b,
-            grad_up_b,
-            mm_tn(mlp_rows_in, grad_gate_b).astype(bf16),
-            mm_tn(mlp_rows_in, grad_up_b).astype(bf16),
+            grad_gate,
+            grad_up,
+            summed_over_rows(mlp_rows_in, grad_gate),
+            summed_over_rows(mlp_rows_in, grad_up),
+            summed_over_rows(hidden, grad_rows),
         )
     )
-    down_sum, gate_sum, up_sum = lax.psum((down_part, gate_part, up_part), "ctx")
-    back_part = mm_nt(grad_gate_b, w_gate) + mm_nt(grad_up_b, w_up)
-    grad_res = grad_y + reduce_line(back_part.reshape(owners, rows, width), 11, wire=bf16)
+    gate_sum, up_sum, down_sum = lax.psum(tuple(ffn_parts), "ctx")
+    grad_res = grad_y + reduce_line([grad_gate, grad_up], [w_gate, w_up], 11, turned=True)
     grad_proj, gain_attn = norm_back(projected, proj_scale, gains[2], grad_res)
     grad_proj_rows = gather_line(grad_proj.astype(bf16), 12)
     grad_mixed = mm_nt(grad_proj_rows, w_output).astype(bf16)
@@ -1222,11 +1494,10 @@
     grad_heads, gain_heads = heads_back(
         row_blocks, pair_grads, cosines, sines, own_gains[:2], raw, scales, block_rows
     )
-    grad_heads = grad_heads.reshape(group, 3 * own_width)
 
     piece = own_width // parts
-    output_part = mm_tn(mixed_group.reshape(group, own_width), grad_proj_rows).astype(bf16)
-    heads_part = mm_tn(group_tokens.reshape(group, width), grad_heads).astype(bf16)
+    output_part = summed_over_rows(mixed_group, grad_proj_rows)
+    heads_part = summed_over_rows(group_tokens, grad_heads)
     attention_part = jnp.concatenate(
         [
             heads_part.reshape(owners, parts, piece, 3 * own_width)
@@ -1240,9 +1511,7 @@
         (attention_part, down_sum, gate_sum, up_sum)
     )
     attention_part = lax.psum_scatter(attention_part, "ctx", scatter_dimension=0, tiled=False)
-    input_grad = grad_res + reduce_line(
-        mm_nt(grad_heads, w_heads).reshape(owners, rows, width), 16, wire=bf16
-    )
+    input_grad = grad_res + reduce_line([grad_heads], [w_heads], 16, turned=True)
     attention_part, input_grad = lax.optimization_barrier((attention_part, input_grad))
     gain_post = jnp.stack([gain_attn, gain_ff]).reshape(2, owners, own_width).transpose(1, 0, 2)
     attention_all, gain_own = finish(attention_part, gain_post, gain_heads)

time: 783 us -> 767 us (0.980)
  matrix products: 90.4 us -> 39 us
  Pallas kernels: 562 us -> 592 us
    dot_general x5 -> x1, matrix products: 34.7 us -> 4.38 us  [mm_nt(): lax.dot_general(left, right, (((1,), (1,)), ((), ())), preferred_element_...]
    pallas_call x6, Pallas kernels: 260 us -> 290 us  [the longest x3 158 us: reduce_line(): pl.pallas_call(functools.partial(reduce_kernel, chips, wire, count, turne...]
    dot_general x4 -> x1, matrix products: 26 us -> 4.8 us  [mm(): return jnp.dot(left, right, preferred_element_type=f32)]
  transfers between devices with their start and end apart: 3 -> 3, of which waited for: 2 -> 2; matrix products, arithmetic and copies ran while one was open for 9% -> 6% of each run, Pallas kernels for 41% -> 44%
where the time goes in v3:
time: 767 us; the launch traced here: 755 us
  Pallas kernels  592 us (77%)
  waiting for transfers between devices  55.4 us (7%)
  other arithmetic  42.9 us (6%)
  matrix products  39 us (5%)
  between operations  14.5 us (2%)
  local copies, waits for them, and re-layouts  11 us (1%)
    pallas_call x3, Pallas kernels, reduce_line(): pl.pallas_call(functools.partial(reduce_kernel, chips, wire, count, turne...  158 us
    pallas_call x1, Pallas kernels, heads_back(): pl.pallas_call(functools.partial(heads_back_kernel, block_rows), out_shap...  70.8 us
    pallas_call x1, Pallas kernels, start(): pl.pallas_call(functools.partial(start_kernel, owners, parts), out_shape=...  59.1 us
    pallas_call x1, Pallas kernels, finish(): pl.pallas_call(functools.partial(finish_kernel, owners, parts), out_shape...  54.8 us
    pallas_call x1, Pallas kernels, ffn_back(): pl.pallas_call(functools.partial(ffn_back_kernel, owners // 2), out_shape...  49.2 us
    psum x1, waiting for transfers between devices, shards(): gate_sum, up_sum, down_sum = lax.psum(tuple(ffn_parts), 'ctx')  49.2 us
    pallas_call x3, Pallas kernels, exchange(): pl.pallas_call(functools.partial(exchange_kernel, axis, size, scatter, co...  46.3 us
    pallas_call x1, Pallas kernels, ffn_in(): pl.pallas_call(functools.partial(ffn_in_kernel, owners // 2), out_shape=[...  42.6 us
  transfers between devices with their start and end apart: 3, of which 2 were waited for; matrix products, arithmetic and copies ran while one was open for 6% of the time, Pallas kernels for 44%

profile of v3, /device:TPU:0, one launch (start us, length us, event | category | flops | bytes accessed | tf_op | source)
XLA Modules:
  0.0 755.0 jit_solution(6512616713129917077)
XLA Ops:
  9.2 59.1 %start.1 = (bf16[8,128,2048]{2,1,0:T(8,128)(2,1)}, f32[8,5,256]{2,1,0:T(8,128)}, bf16[8,4,64,768]{3,2,1,0:T(8,128)(2,1)}, f32[512,128]{1,0:T(8,128)}, f32[512,128]{1,0:T(8,128)}) custom-call(bf16[128,2048]{1,0:T(8,128)(2,1)} %bitcast.82, f32[5,256]{1,0:T(8,128)} %select_maximum_fusion.small, f32[1,128]{1,0:T(1,128)} %constant.28.clone.inverse, ...), custom_call_target="tpu_custom_call" | custom-call | bytes 198000000 | tf_op jit(solution)/shard_map/start/pallas_call | solution.py:797
  72.0 42.2 %heads.1 = (bf16[4,3,2,128,256]{4,3,2,1,0:T(8,128)(2,1)}, f32[2,8,128,256]{3,2,1,0:T(8,128)}, f32[16,128]{1,0:T(8,128)}) custom-call(s32[8,128,1]{2,1,0:T(8,128)} %broadcast_in_dim_reshape.4.row_blocks, bf16[8,128,2048]{2,1,0:T(8,128)(2,1)} %get-tuple-element.47.tokens, bf16[2048,768]{1,0:T(8,128)(2,1)} %bitcast.79, f32[512,128]{1,0:T(8,128)} %get-tuple-element.49.cosines, ...), custom_call_target="tpu_custom_call" | custom-call | bytes 115500000 | tf_op jit(solution)/shard_map/heads/pallas_call | solution.py:951
  115.6 12.9 %attend.1.refs_0_ = bf16[4,2,128,256]{3,2,1,0:T(8,128)(2,1)} custom-call(bf16[4,3,2,128,256]{4,3,2,1,0:T(8,128)(2,1)} %get-tuple-element.51.query_ref.key_ref.value_ref, bf16[4,3,2,128,256]{4,3,2,1,0:T(8,128)(2,1)} %get-tuple-element.51.query_ref.key_ref.value_ref, bf16[4,3,2,128,256]{4,3,2,1,0:T(8,128)(2,1)} %get-tuple-element.51.query_ref.key_ref.value_ref, ...), custom_call_target="tpu_custom_call" | custom-call | bytes 39600000 | tf_op jit(solution)/shard_map/attend/pallas_call | solution.py:1347
  128.5 10.5 %exchange_ctx_6.1 = bf16[4,2,128,256]{3,2,1,0:T(8,128)(2,1)} custom-call(bf16[4,2,128,256]{3,2,1,0:T(8,128)(2,1)} %attend.1.refs_0_), custom_call_target="tpu_custom_call" | custom-call | bytes 33000000 | tf_op jit(solution)/shard_map/exchange_ctx_6/pallas_call | solution.py:91
  139.1 19.3 %exchange_fsdp_7.1 = bf16[8,128,256]{2,1,0:T(8,128)(2,1)} custom-call(bf16[8,128,256]{2,1,0:T(8,128)(2,1)} %bitcast.87), custom_call_target="tpu_custom_call" | custom-call | bytes 46200000 | tf_op jit(solution)/shard_map/exchange_fsdp_7/pallas_call | solution.py:91
  159.8 6.2 all-gather.2.cloned.1.call-done
  165.9 4.8 multiply_reduce_fusion.3
  172.7 42.6 %ffn_in.1 = (bf16[8,128,2048]{2,1,0:T(8,128)(2,1)}, f32[8,128,1024]{2,1,0:T(8,128)}, f32[8,128,1024]{2,1,0:T(8,128)}, bf16[8,128,1024]{2,1,0:T(8,128)(2,1)}) custom-call(bf16[128,2048]{1,0:T(8,128)(2,1)} %fusion.6.given, bf16[2048,1024]{1,0:T(8,128)(2,1)} %refs_2_.1, bf16[2048,1024]{1,0:T(8,128)(2,1)} %refs_3_.1), custom_call_target="tpu_custom_call" | custom-call | bytes 148500000 | tf_op jit(solution)/shard_map/ffn_in/pallas_call | solution.py:353
  215.3 51.1 %reduce_line_9.1 = f32[128,2048]{1,0:T(8,128)} custom-call(bf16[8,128,1024]{2,1,0:T(8,128)(2,1)} %get-tuple-element.53.refs_0_, bf16[1024,2048]{1,0:T(8,128)(2,1)} %w_down.1), custom_call_target="tpu_custom_call" | custom-call | bytes 148500000 | tf_op jit(solution)/shard_map/reduce_line_9/pallas_call | solution.py:643
  269.4 2.3 fusion.3.given
  271.7 49.2 %ffn_back.1 = (bf16[8,128,2048]{2,1,0:T(8,128)(2,1)}, bf16[8,128,1024]{2,1,0:T(8,128)(2,1)}, bf16[8,128,1024]{2,1,0:T(8,128)(2,1)}) custom-call(bf16[128,2048]{1,0:T(8,128)(2,1)} %fusion.3.given, bf16[1024,2048]{1,0:T(8,128)(2,1)} %w_down.1, f32[8,128,1024]{2,1,0:T(8,128)} %get-tuple-element.54.gate_in, f32[8,128,1024]{2,1,0:T(8,128)} %get-tuple-element.55.up_in), custom_call_target="tpu_custom_call" | custom-call | bytes 148500000 | tf_op jit(solution)/shard_map/ffn_back/pallas_call | solution.py:461
  320.9 9.6 %bitcast_convert_fusion.2 = bf16[2048,1024]{1,0:T(8,128)(2,1)} fusion(bf16[8,128,2048]{2,1,0:T(8,128)(2,1)} %get-tuple-element.58, bf16[8,128,1024]{2,1,0:T(8,128)(2,1)} %get-tuple-element.60.refs_0_), kind=kOutput, calls=%fused_computation.2 | convolution fusion | flops 4297064448 | bytes 10485760 | tf_op jit(solution)/shard_map/dot_general | solution.py:1403
  330.5 6.2 bitcast_convert_fusion.1
  336.8 6.2 bitcast_convert_fusion
  343.1 57.5 %reduce_line_11.1 = f32[128,2048]{1,0:T(8,128)} custom-call(bf16[8,128,1024]{2,1,0:T(8,128)(2,1)} %get-tuple-element.60.refs_0_, bf16[8,128,1024]{2,1,0:T(8,128)(2,1)} %get-tuple-element.61.refs_1_, bf16[2048,1024]{1,0:T(8,128)(2,1)} %refs_2_.1, bf16[2048,1024]{1,0:T(8,128)(2,1)} %refs_3_.1), custom_call_target="tpu_custom_call" | custom-call | bytes 148500000 | tf_op jit(solution)/shard_map/reduce_line_11/pallas_call | solution.py:643
  402.4 3.9 subtract_convert_fusion
  406.3 40.4 %gather_line_12.1 = bf16[8,128,2048]{2,1,0:T(8,128)(2,1)} custom-call(bf16[128,2048]{1,0:T(8,128)(2,1)} %get-tuple-element.91.given), custom_call_target="tpu_custom_call" | custom-call | bytes 132000000 | tf_op jit(solution)/shard_map/gather_line_12/pallas_call | solution.py:246
  446.8 4.4 convolution_convert_fusion.1
  451.2 16.4 %exchange_ctx_13.1.grad_ref = bf16[4,2,128,256]{3,2,1,0:T(8,128)(2,1)} custom-call(bf16[4,2,128,256]{3,2,1,0:T(8,128)(2,1)} %bitcast.93), custom_call_target="tpu_custom_call" | custom-call | bytes 33000000 | tf_op jit(solution)/shard_map/exchange_ctx_13/pallas_call | solution.py:91
  467.6 15.9 %attend_back.1 = (f32[4,2,128,256]{3,2,1,0:T(8,128)}, f32[4,2,128,256]{3,2,1,0:T(8,128)}, bf16[4,2,128,256]{3,2,1,0:T(8,128)(2,1)}) custom-call(bf16[4,3,2,128,256]{4,3,2,1,0:T(8,128)(2,1)} %get-tuple-element.51.query_ref.key_ref.value_ref, bf16[4,3,2,128,256]{4,3,2,1,0:T(8,128)(2,1)} %get-tuple-element.51.query_ref.key_ref.value_ref, ...), custom_call_target="tpu_custom_call" | custom-call | bytes 52800000 | tf_op jit(solution)/shard_map/attend_back/pallas_call | solution.py:1362
  483.5 70.8 %heads_back.1 = (bf16[8,128,768]{2,1,0:T(8,128)(2,1)}, f32[2,256]{1,0:T(2,128)}) custom-call(s32[8,128,1]{2,1,0:T(8,128)} %broadcast_in_dim_reshape.4.row_blocks, f32[4,2,128,256]{3,2,1,0:T(8,128)} %get-tuple-element.62.grad_query, f32[4,2,128,256]{3,2,1,0:T(8,128)} %get-tuple-element.63.grad_key, bf16[4,2,128,256]{3,2,1,0:T(8,128)(2,1)} %get-tuple-element.64.grad_value, ...), custom_call_target="tpu_custom_call" | custom-call | bytes 148500000 | tf_op jit(solution)/shard_map/heads_back/pallas_call | solution.py:1079
  554.3 6.5 bitcast_convert_fusion.3
  566.9 49.2 %all-reduce.5.cloned.1.call-done = (bf16[1024,2048]{1,0:T(8,128)(2,1)}, bf16[2048,1024]{1,0:T(8,128)(2,1)}, bf16[2048,1024]{1,0:T(8,128)(2,1)}) async-done(((bf16[1024,2048]{1,0:T(8,128)(2,1)}, bf16[2048,1024]{1,0:T(8,128)(2,1)}, bf16[2048,1024]{1,0:T(8,128)(2,1)}), (bf16[1024,2048]{1,0:T(8,128)(2,1)}, bf16[2048,1024]{1,0:T(8,128)(2,1)}, bf16[2048,1024]{1,0:T(8,128)(2,1)})) %all-reduce.5.cloned.1.call-update) | async-done | bytes 12582928 | tf_op jit(solution)/shard_map/psum | solution.py:1485
  616.1 49.3 %reduce_line_16.1 = f32[128,2048]{1,0:T(8,128)} custom-call(bf16[8,128,768]{2,1,0:T(8,128)(2,1)} %get-tuple-element.67.refs_0_, bf16[2048,768]{1,0:T(8,128)(2,1)} %bitcast.80), custom_call_target="tpu_custom_call" | custom-call | bytes 148500000 | tf_op jit(solution)/shard_map/reduce_line_16/pallas_call | solution.py:643
  666.1 2.7 fusion.8
  668.8 6.8 convert_element_type.108
  675.6 4.4 convert_element_type.109
  680.1 4.4 convert_element_type.110
  684.5 54.8 %finish.1 = (bf16[4,4,64,2048]{3,2,1,0:T(8,128)(2,1)}, f32[4,256]{1,0:T(4,128)}) custom-call(bf16[64,8192]{1,0:T(8,128)(2,1)} %bitcast.91, f32[8,2,256]{2,1,0:T(2,128)} %maximum_bitcast_fusion.gain_post, f32[2,256]{1,0:T(2,128)} %get-tuple-element.74.gain_heads), custom_call_target="tpu_custom_call" | custom-call | bytes 165000000 | tf_op jit(solution)/shard_map/finish/pallas_call | solution.py:1236
  739.4 2.8 fusion.9
  742.1 2.7 bitcast_convert_fusion.6
  744.8 2.7 bitcast_convert_fusion.4
  (71 shorter events, 22.6 us)
Async XLA Ops:
  7.2 61.2 %copy-start.11 = (bf16[4,256]{1,0:T(4,128)(2,1)S(1)}, bf16[4,256]{1,0:T(4,128)(2,1)}, u32[]{:S(2)}) copy-start(bf16[4,256]{1,0:T(4,128)(2,1)} %param.21) | copy-start | bytes 6148
  7.2 158.8 %all-gather.2.cloned.1.call-start = ((), (), s32[]{:S(2)}) async-start(), calls=%async_computation.1 | async-start | bytes 9437184 | tf_op jit(solution)/shard_map/all_gather | solution.py:1439
  68.3 547.8 %all-reduce.5.cloned.1.call-start = ((), (), s32[]{:S(2)}) async-start(), calls=%async_computation.3 | async-start | bytes 25165824 | tf_op jit(solution)/shard_map/psum | solution.py:1485
  115.6 44.1 %copy-start.10 = (f32[8,5,256]{2,1,0:T(8,128)S(1)}, f32[8,5,256]{2,1,0:T(8,128)}, u32[]{:S(2)}) copy-start(f32[8,5,256]{2,1,0:T(8,128)} %get-tuple-element.45) | copy-start | bytes 122884
  165.9 5.8 copy-start.2
  170.7 1.0 copy-start
  215.3 52.5 %copy-start.1 = (bf16[1,128,2048]{2,1,0:T(8,128)(2,1)S(1)}, bf16[1,128,2048]{2,1,0:T(8,128)(2,1)}, u32[]{:S(2)}) copy-start(bf16[1,128,2048]{2,1,0:T(8,128)(2,1)} %param.22) | copy-start | bytes 1572868
  320.9 9.6 %copy-start.8 = (bf16[8,128,1024]{2,1,0:T(8,128)(2,1)S(1)}, bf16[8,128,1024]{2,1,0:T(8,128)(2,1)}, u32[]{:S(2)}) copy-start(bf16[8,128,1024]{2,1,0:T(8,128)(2,1)} %get-tuple-element.61.refs_1_) | copy-start | bytes 6291460
  320.9 9.6 %copy-start.13 = (bf16[8,128,2048]{2,1,0:T(8,128)(2,1)S(1)}, bf16[8,128,2048]{2,1,0:T(8,128)(2,1)}, u32[]{:S(2)}) copy-start(bf16[8,128,2048]{2,1,0:T(8,128)(2,1)} %get-tuple-element.58) | copy-start | bytes 12582916
  330.5 6.3 copy-start.6
  330.5 6.3 copy-start.14
  343.0 341.5 %reduce-scatter.4.cloned.1.call-start = ((), (), s32[]{:S(2)}) async-start(), calls=%async_computation.2 | async-start | bytes 5242880
  402.4 44.4 %copy-start.9 = (bf16[256,2048]{1,0:T(8,128)(2,1)S(1)}, bf16[256,2048]{1,0:T(8,128)(2,1)}, u32[]{:S(2)}) copy-start(bf16[256,2048]{1,0:T(8,128)(2,1)} %param.17) | copy-start | bytes 3145732
  560.8 2.4 copy-start.5
  560.9 2.6 copy-start.7
  668.8 6.8 copy-start.4
  675.6 4.4 copy-start.3
  744.8 2.7 copy-start.12
Sparse Core Ops, SparseCore 0:
  68.5 97.4 all-gather.1
  343.1 272.9 all-reduce.4
  619.1 52.6 reduce-scatter.3

commit v4 on v3

--- a/solution.py
+++ b/solution.py
@@ -486,41 +486,49 @@
     )(shard, w_down, gate, upward)
 
 
+HALVES = 2
+STRIP = 16
+
+
 def reduce_kernel(chips, wire, count, turned, *refs):
     left_in, right_in, total = refs[:count], refs[count : 2 * count], refs[2 * count]
     refs = refs[2 * count + 1 :]
     left, right, refs = refs[:count], refs[count : 2 * count], refs[2 * count :]
-    mine, aside, beside, from_left, from_right, outgoing = refs[:6]
-    load_sem, side_send, side_land, line_send, left_land, right_land = refs[6:]
+    products, beside, from_left, from_right, outgoing = refs[:5]
+    load_sem, side_send, side_land, line_send, left_land, right_land = refs[5:]
     own = lax.axis_index("fsdp")
     chip, core = own // 2, own % 2
     sibling = chip * 2 + 1 - core
-    rows = total.shape[0]
-
-    def side(other):
+    height = total.shape[0] // HALVES
+    last = chips - 1
+
+    def side(other, half):
+        rows = pl.ds(half * height, height)
         return remote(
-            aside.at[other],
-            beside.at[other],
-            side_send.at[other],
-            side_land.at[other],
+            products.at[other * 2 + 1 - core, rows],
+            beside.at[other, rows],
+            side_send.at[other, half],
+            side_land.at[other, half],
             {"fsdp": sibling},
         )
 
-    def rightward(other, target):
+    def rightward(other, half, target):
+        rows = pl.ds(half * height, height)
         return remote(
-            outgoing.at[other],
-            from_left.at[other],
-            line_send.at[other],
-            left_land.at[other],
+            outgoing.at[other, rows],
+            from_left.at[other, rows],
+            line_send.at[other, half],
+            left_land.at[other, half],
             {"fsdp": target},
         )
 
-    def leftward(other, target):
+    def leftward(other, half, target):
+        rows = pl.ds(half * height, height)
         return remote(
-            outgoing.at[other],
-            from_right.at[other],
-            line_send.at[other],
-            right_land.at[other],
+            outgoing.at[other, rows],
+            from_right.at[other, rows],
+            line_send.at[other, half],
+            right_land.at[other, half],
             {"fsdp": target},
         )
 
@@ -552,88 +560,117 @@
                         lefts[item], right[item][:, columns], preferred_element_type=f32
                     )
                 product = part if product is None else product + part
-
-            @pl.when(core == 0)
+            put_chip(products, other, columns, product)
+
+        each_tile(total.shape[1], tile)
+        for half in range(HALVES):
+            side(other, half).start()
+
+    def add_up(other, half, inbound, target):
+        def strip(at, carry):
+            rows = pl.ds(pl.multiple_of(half * height + at * STRIP, STRIP), STRIP)
+            value = products[other * 2 + core, rows] + beside[other, rows]
+            for ref in inbound:
+                value += ref[other, rows].astype(f32)
+            if target is total:
+                total[rows] = value
+            else:
+                target[other, rows] = value.astype(wire)
+            return carry
+
+        lax.fori_loop(0, height // STRIP, strip, 0)
+
+    def send_right(other, inbound):
+        for half in range(HALVES):
+            side(other, half).wait_recv()
+            if inbound:
+                rightward(other, half, own).wait_recv()
+            add_up(other, half, inbound, outgoing)
+            rightward(other, half, own + 2).start()
+
+    def send_left(other, inbound):
+        for half in range(HALVES):
+            side(other, half).wait_recv()
+            if inbound:
+                leftward(other, half, own).wait_recv()
+            add_up(other, half, inbound, outgoing)
+            leftward(other, half, own - 2).start()
+
+    def each_turn(does):
+        def turn(at, carry):
+            tick, leftwards = at // 2, at % 2
+            right_to, left_to = last - (tick - chip), tick - (last - chip)
+            goes_right = (leftwards == 0) & (tick >= chip) & (right_to > chip)
+            goes_left = (leftwards == 1) & (left_to >= 0) & (left_to < chip)
+            does(jnp.where(leftwards == 0, right_to, left_to), goes_right, goes_left, tick)
+            return carry
+
+        lax.fori_loop(0, 2 * last, turn, 0)
+
+    def multiply_turn(other, goes_right, goes_left, tick):
+        @pl.when(goes_right | goes_left)
+        def _():
+            multiply(other)
+
+        @pl.when(goes_right & (chip == 0) & (tick > 0))
+        def _():
+            send_right(other + 1, ())
+
+        @pl.when(goes_left & (chip == last) & (tick > 0))
+        def _():
+            send_left(other - 1, ())
+
+    def send_turn(other, goes_right, goes_left, tick):
+        @pl.when(goes_right & (chip > 0))
+        def _():
+            send_right(other, (from_left,))
+
+        @pl.when(goes_left & (chip < last))
+        def _():
+            send_left(other, (from_right,))
+
+    each_turn(multiply_turn)
+    multiply(chip)
+
+    @pl.when(chip == 0)
+    def _():
+        send_right(1, ())
+
+    @pl.when(chip == last)
+    def _():
+        send_left(last - 1, ())
+
+    each_turn(send_turn)
+    for half in range(HALVES):
+        side(chip, half).wait_recv()
+
+        @pl.when(chip > 0)
+        def _():
+            rightward(chip, half, own).wait_recv()
+
+        @pl.when(chip < last)
+        def _():
+            leftward(chip, half, own).wait_recv()
+
+        @pl.when(chip == 0)
+        def _():
+            add_up(chip, half, (from_right,), total)
+
+        @pl.when(chip == last)
+        def _():
+            add_up(chip, half, (from_left,), total)
+
+        @pl.when((chip > 0) & (chip < last))
+        def _():
+            add_up(chip, half, (from_left, from_right), total)
+
+    for other in range(chips):
+        for half in range(HALVES):
+            side(other, half).wait_send()
+
+            @pl.when(chip != other)
             def _():
-                mine[other, :, columns] = product[:rows]
-                aside[other, :, columns] = product[rows:]
-
-            @pl.when(core == 1)
-            def _():
-                mine[other, :, columns] = product[rows:]
-                aside[other, :, columns] = product[:rows]
-
-        each_tile(total.shape[1], tile)
-        side(other).start()
-
-    def each_turn(right_does, left_does):
-        for tick in range(chips - 1):
-            right_to = chips - 1 - (tick - chip)
-            left_to = tick - (chips - 1 - chip)
-
-            @pl.when((tick >= chip) & (right_to > chip))
-            def _():
-                right_does(right_to)
-
-            @pl.when((left_to >= 0) & (left_to < chip))
-            def _():
-                left_does(left_to)
-
-    each_turn(multiply, multiply)
-    multiply(chip)
-
-    def send_right(other):
-        side(other).wait_recv()
-
-        @pl.when(chip > 0)
-        def _():
-            rightward(other, own).wait_recv()
-            outgoing[other] = (
-                mine[other] + beside[other] + from_left[other].astype(f32)
-            ).astype(wire)
-
-        @pl.when(chip == 0)
-        def _():
-            outgoing[other] = (mine[other] + beside[other]).astype(wire)
-
-        rightward(other, own + 2).start()
-
-    def send_left(other):
-        side(other).wait_recv()
-
-        @pl.when(chip < chips - 1)
-        def _():
-            leftward(other, own).wait_recv()
-            outgoing[other] = (
-                mine[other] + beside[other] + from_right[other].astype(f32)
-            ).astype(wire)
-
-        @pl.when(chip == chips - 1)
-        def _():
-            outgoing[other] = (mine[other] + beside[other]).astype(wire)
-
-        leftward(other, own - 2).start()
-
-    each_turn(send_right, send_left)
-    side(chip).wait_recv()
-    total[...] = mine[chip] + beside[chip]
-
-    @pl.when(chip > 0)
-    def _():
-        rightward(chip, own).wait_recv()
-        total[...] += from_left[chip].astype(f32)
-
-    @pl.when(chip < chips - 1)
-    def _():
-        leftward(chip, own).wait_recv()
-        total[...] += from_right[chip].astype(f32)
-
-    for other in range(chips):
-        side(other).wait_send()
-
-        @pl.when(chip != other)
-        def _():
-            rightward(other, own).wait_send()
+                rightward(other, half, own).wait_send()
 
 
 def reduce_line(lefts, rights, key, turned=False, wire=bf16):
@@ -647,19 +684,14 @@
         out_specs=in_vmem(),
         scratch_shapes=[pltpu.VMEM(item.shape, item.dtype) for item in lefts + rights]
         + [
-            pltpu.VMEM((chips, rows, width), f32),
-            pltpu.VMEM((chips, rows, width), f32),
+            pltpu.VMEM((owners, rows, width), f32),
             pltpu.VMEM((chips, rows, width), f32),
             pltpu.VMEM((chips, rows, width), wire),
             pltpu.VMEM((chips, rows, width), wire),
             pltpu.VMEM((chips, rows, width), wire),
             pltpu.SemaphoreType.DMA((2 * count,)),
-            pltpu.SemaphoreType.DMA((chips,)),
-            pltpu.SemaphoreType.DMA((chips,)),
-            pltpu.SemaphoreType.DMA((chips,)),
-            pltpu.SemaphoreType.DMA((chips,)),
-            pltpu.SemaphoreType.DMA((chips,)),
-        ],
+        ]
+        + [pltpu.SemaphoreType.DMA((chips, HALVES))] * 5,
         compiler_params=pltpu.CompilerParams(
             collective_id=key, has_side_effects=True, vmem_limit_bytes=63 * 1024 * 1024
         ),
@@ -988,8 +1020,8 @@
     scales,
     grads,
     gain_sums,
-    pair_grads,
-    pair_values,
+    landed,
+    weighted,
     stats,
     everyone,
     own_sem,
@@ -999,14 +1031,14 @@
     part_land,
 ):
     kinds, owners, rows, own_width = raw.shape
-    parts = pair_values.shape[0]
+    parts = landed.shape[1]
     pair = owners // parts
     width = owners * own_width
     part = lax.axis_index("ctx")
     sources = (grad_query, grad_key, grad_value)
 
     def landing(item, place):
-        return pair_values.at[place] if item == 2 else pair_grads.at[item, place]
+        return landed.at[item, place]
 
     local = [
         pltpu.make_async_copy(sources[item].at[part], landing(item, part), own_sem.at[item])
@@ -1043,14 +1075,14 @@
             scale = as_column(scales[pl.ds(kind * owners + seq, 1), :])
             products = jnp.zeros((rows, 1), f32)
             for head in each_head(own_width):
-                rotated = pair_grads[kind, seq // pair, seq % pair, :, head]
+                rotated = landed[kind, seq // pair, seq % pair, :, head].astype(f32)
                 values = rotated * cosine - pltpu.roll(rotated, HEAD_DIM // 2, 1) * sine
                 plain = raw[kind, seq, :, head]
                 gain_sums[kind : kind + 1, head] += jnp.sum(
                     values * (plain * scale), axis=0, keepdims=True
                 )
                 values = values * gains[kind : kind + 1, head]
-                pair_grads[kind, seq // pair, seq % pair, :, head] = values
+                weighted[kind, seq, :, head] = values
                 products += jnp.sum(values * plain, axis=-1, keepdims=True)
             stats[pl.ds(kind * owners + seq, 1), :] = as_row(products)
         return carry
@@ -1064,10 +1096,10 @@
             row = pl.ds(kind * owners + seq, 1)
             scale, mean = as_column(scales[row, :]), as_column(stats[row, :])
             grads[seq, :, kind * own_width : (kind + 1) * own_width] = (
-                scale * pair_grads[kind, seq // pair, seq % pair]
+                scale * weighted[kind, seq]
                 - raw[kind, seq] * (scale * scale * scale * mean)
             ).astype(bf16)
-        grads[seq, :, 2 * own_width :] = pair_values[seq // pair, seq % pair]
+        grads[seq, :, 2 * own_width :] = landed[2, seq // pair, seq % pair]
         return carry
 
     lax.fori_loop(0, owners, through_norm, 0)
@@ -1085,8 +1117,8 @@
         in_specs=[in_vmem()] * 9,
         out_specs=[in_vmem(), in_vmem()],
         scratch_shapes=[
-            pltpu.VMEM((2, parts, pair, rows, own_width), f32),
-            pltpu.VMEM((parts, pair, rows, own_width), bf16),
+            pltpu.VMEM((3, parts, pair, rows, own_width), bf16),
+            pltpu.VMEM((2, owners, rows, own_width), f32),
             pltpu.VMEM((2 * owners, rows), f32),
             pltpu.VMEM((owners, 2 * owners, rows), f32),
             pltpu.SemaphoreType.DMA((3,)),
@@ -1110,6 +1142,7 @@
     gain_post,
     gain_heads,
     kept,
+    kept_output,
     gain_own,
     post_all,
     gain_mine,
@@ -1141,15 +1174,15 @@
     local = [
         pltpu.make_async_copy(cut(item, own), slot(item), own_sem.at[item]) for item in range(3)
     ]
-    local.append(pltpu.make_async_copy(output_rows, kept.at[part, 3], own_sem.at[3]))
+    local.append(pltpu.make_async_copy(output_rows, kept_output.at[part], own_sem.at[3]))
     for copy in local:
         copy.start()
     greet_peers(("fsdp", "ctx"))
     first, posts, second = [], [], []
     for step in range(1, owners):
         peer = lax.rem(own + step, owners)
-        for item in range(3):
-            first.append(
+        first.append(
+            [
                 remote(
                     cut(item, peer),
                     slot(item),
@@ -1157,7 +1190,9 @@
                     piece_land.at[item, step],
                     {"fsdp": peer},
                 )
-            )
+                for item in range(3)
+            ]
+        )
         posts.append(
             remote(
                 gain_post.at[peer],
@@ -1167,35 +1202,38 @@
                 {"fsdp": peer},
             )
         )
-    for copy in first + posts:
+    for copy in sum(first, []) + posts:
         copy.start()
-    for step in range(1, parts):
-        second.append(
-            remote(
-                output_rows,
-                kept.at[part, 3],
-                part_send.at[0, step],
-                part_land.at[0, step],
-                {"ctx": lax.rem(part + step, parts)},
+
+    def spread(region, turn):
+        for step in range(1, parts):
+            second.append(
+                remote(
+                    region,
+                    region,
+                    part_send.at[turn, step],
+                    part_land.at[turn, step],
+                    {"ctx": lax.rem(part + step, parts)},
+                )
             )
+            second[-1].start()
+
+    local[3].wait()
+    spread(kept_output.at[part], owners)
+    post_all[own] = gain_post[own]
+    for copy in local[:3]:
+        copy.wait()
+    for turn in range(owners):
+        if turn:
+            for copy in first[turn - 1]:
+                copy.wait_recv()
+        place = lax.rem(own - turn + owners, owners)
+        spread(
+            kept.at[
+                part, :, :, pl.ds(pl.multiple_of(place * own_width, own_width), own_width)
+            ],
+            turn,
         )
-        second[-1].start()
-    post_all[own] = gain_post[own]
-    for copy in local:
-        copy.wait()
-    for copy in first:
-        copy.wait_recv()
-    for step in range(1, parts):
-        second.append(
-            remote(
-                kept.at[part, pl.ds(0, 3)],
-                kept.at[part, pl.ds(0, 3)],
-                part_send.at[1, step],
-                part_land.at[1, step],
-                {"ctx": lax.rem(part + step, parts)},
-            )
-        )
-        second[-1].start()
     for copy in posts:
         copy.wait()
     post = post_all[0]
@@ -1222,7 +1260,7 @@
     for place in range(1, parts):
         total += part_all[place]
     gain_own[...] = total
-    for copy in first:
+    for copy in sum(first, []):
         copy.wait_send()
     for copy in second:
         copy.wait()
@@ -1236,11 +1274,12 @@
     return pl.pallas_call(
         functools.partial(finish_kernel, owners, parts),
         out_shape=[
-            jax.ShapeDtypeStruct((parts, 4, piece, width), bf16),
+            jax.ShapeDtypeStruct((parts, 3, piece, width), bf16),
+            jax.ShapeDtypeStruct((parts, piece, width), bf16),
             jax.ShapeDtypeStruct((4, own_width), f32),
         ],
         in_specs=[in_vmem(), in_vmem(), in_vmem()],
-        out_specs=[anywhere(), in_vmem()],
+        out_specs=[anywhere(), anywhere(), in_vmem()],
         scratch_shapes=[
             pltpu.VMEM((owners, 2, own_width), f32),
             pltpu.VMEM((4, own_width), f32),
@@ -1248,8 +1287,8 @@
             pltpu.SemaphoreType.DMA((4,)),
             pltpu.SemaphoreType.DMA((3, owners)),
             pltpu.SemaphoreType.DMA((3, owners)),
-            pltpu.SemaphoreType.DMA((2, parts)),
-            pltpu.SemaphoreType.DMA((2, parts)),
+            pltpu.SemaphoreType.DMA((owners + 1, parts)),
+            pltpu.SemaphoreType.DMA((owners + 1, parts)),
             pltpu.SemaphoreType.DMA((owners,)),
             pltpu.SemaphoreType.DMA((owners,)),
             pltpu.SemaphoreType.DMA((parts,)),
@@ -1259,6 +1298,28 @@
         cost_estimate=lasting(50),
         name="finish",
     )(sums, gain_post, gain_heads)
+
+
+def widen_kernel(heads_ref, output_ref, *outs):
+    for item in range(3):
+        outs[item][...] = heads_ref[item].astype(f32)
+    outs[3][...] = output_ref[...].astype(f32)
+
+
+def widen(heads_sum, output_sum):
+    parts, kinds, piece, width = heads_sum.shape
+    return pl.pallas_call(
+        widen_kernel,
+        grid=(parts,),
+        out_shape=[jax.ShapeDtypeStruct((parts * piece, width), f32)] * 4,
+        in_specs=[
+            pl.BlockSpec((None, kinds, piece, width), lambda c: (c, 0, 0, 0)),
+            pl.BlockSpec((None, piece, width), lambda c: (c, 0, 0)),
+        ],
+        out_specs=[pl.BlockSpec((piece, width), lambda c: (c, 0))] * 4,
+        cost_estimate=lasting(4),
+        name="widen",
+    )(heads_sum, output_sum)
 
 
 def probs_of(query, key, query_pos, key_pos):
@@ -1305,7 +1366,9 @@
     grad_scores = (
         probs * (grad_probs - jnp.sum(probs * grad_probs, axis=-1, keepdims=True))
     ).astype(bf16)
-    grad_query_ref[...] = jnp.dot(grad_scores, key, preferred_element_type=f32) * score_scale
+    grad_query_ref[...] = (
+        jnp.dot(grad_scores, key, preferred_element_type=f32) * score_scale
+    ).astype(bf16)
     value_part = lax.dot_general(
         probs.astype(bf16), grad, (((0,), (0,)), ((), ())), preferred_element_type=f32
     )
@@ -1325,7 +1388,7 @@
 
     @pl.when(step == steps - 1)
     def _():
-        grad_key_ref[...] = (key_sum[...] * score_scale).reshape(grad_key_ref.shape)
+        grad_key_ref[...] = (key_sum[...] * score_scale).astype(bf16).reshape(grad_key_ref.shape)
         grad_value_ref[...] = value_sum[...].astype(bf16).reshape(grad_value_ref.shape)
 
 
@@ -1362,11 +1425,7 @@
     return pl.pallas_call(
         attend_back_kernel,
         grid=(pair, width // HEAD_DIM, parts),
-        out_shape=[
-            jax.ShapeDtypeStruct((parts, pair, rows, width), f32),
-            jax.ShapeDtypeStruct((parts, pair, rows, width), f32),
-            jax.ShapeDtypeStruct((parts, pair, rows, width), bf16),
-        ],
+        out_shape=[jax.ShapeDtypeStruct((parts, pair, rows, width), bf16)] * 3,
         in_specs=in_specs + [row_block],
         out_specs=[row_block, all_block, all_block],
         scratch_shapes=[
@@ -1507,24 +1566,20 @@
         ],
         axis=2,
     )
-    attention_part, down_sum, gate_sum, up_sum = lax.optimization_barrier(
-        (attention_part, down_sum, gate_sum, up_sum)
+    input_grad = grad_res + reduce_line([grad_heads], [w_heads], 16, turned=True)
+    attention_part, input_grad, down_sum, gate_sum, up_sum = lax.optimization_barrier(
+        (attention_part, input_grad, down_sum, gate_sum, up_sum)
     )
     attention_part = lax.psum_scatter(attention_part, "ctx", scatter_dimension=0, tiled=False)
-    input_grad = grad_res + reduce_line([grad_heads], [w_heads], 16, turned=True)
-    attention_part, input_grad = lax.optimization_barrier((attention_part, input_grad))
     gain_post = jnp.stack([gain_attn, gain_ff]).reshape(2, owners, own_width).transpose(1, 0, 2)
-    attention_all, gain_own = finish(attention_part, gain_post, gain_heads)
-    attention_all = [
-        attention_all[:, item].reshape(own_width, width).astype(f32) for item in range(4)
-    ]
+    ffn_sums = [item.astype(f32) for item in (gate_sum, up_sum, down_sum)]
+    attention_part, *ffn_sums = lax.optimization_barrier((attention_part, *ffn_sums))
+    heads_sum, output_sum, gain_own = finish(attention_part, gain_post, gain_heads)
     return (
         block_out.astype(bf16)[None],
         input_grad[None],
-        *attention_all,
-        gate_sum.astype(f32),
-        up_sum.astype(f32),
-        down_sum.astype(f32),
+        *widen(heads_sum, output_sum),
+        *ffn_sums,
         gain_own,
     )
 

time: 767 us -> 725 us (0.945)
  Pallas kernels: 592 us -> 556 us
    unnamed x4, waiting for transfers between devices: 0.05 us -> 39.3 us
    psum x1, waiting for transfers between devices: 49.2 us -> 15.7 us  [shards(): gate_sum, up_sum, down_sum = lax.psum(tuple(ffn_parts), 'ctx')]
    pallas_call x3, Pallas kernels: 158 us -> 140 us  [reduce_line(): pl.pallas_call(functools.partial(reduce_kernel, chips, wire, count, turne...]
    pallas_call x1, Pallas kernels: 70.8 us -> 54.4 us  [heads_back(): pl.pallas_call(functools.partial(heads_back_kernel, block_rows), out_shap...]
    pallas_call x1, Pallas kernels: 49.2 us -> 40.2 us  [ffn_back(): pl.pallas_call(functools.partial(ffn_back_kernel, owners // 2), out_shape...]
    convert_element_type x5 -> x3, other arithmetic: 21 us -> 15.7 us  [shards(): ffn_sums = [item.astype(f32) for item in (gate_sum, up_sum, down_sum)]]
  transfers between devices with their start and end apart: 3 -> 3, of which waited for: 2 -> 3; matrix products, arithmetic and copies ran while one was open for 6% -> 6% of each run, Pallas kernels for 44% -> 43%
where the time goes in v4:
time: 725 us; the launch traced here: 715 us
  Pallas kernels  556 us (77%)
  waiting for transfers between devices  61.2 us (8%)
  matrix products  39 us (5%)
  other arithmetic  36 us (5%)
  between operations  14.3 us (2%)
  local copies, waits for them, and re-layouts  7.97 us (1%)
    pallas_call x3, Pallas kernels, reduce_line(): pl.pallas_call(functools.partial(reduce_kernel, chips, wire, count, turne...  140 us
    pallas_call x1, Pallas kernels, start(): pl.pallas_call(functools.partial(start_kernel, owners, parts), out_shape=...  59.1 us
    pallas_call x1, Pallas kernels, finish(): pl.pallas_call(functools.partial(finish_kernel, owners, parts), out_shape...  54.8 us
    pallas_call x1, Pallas kernels, heads_back(): pl.pallas_call(functools.partial(heads_back_kernel, block_rows), out_shap...  54.4 us
    pallas_call x3, Pallas kernels, exchange(): pl.pallas_call(functools.partial(exchange_kernel, axis, size, scatter, co...  47.6 us
    pallas_call x1, Pallas kernels, ffn_in(): pl.pallas_call(functools.partial(ffn_in_kernel, owners // 2), out_shape=[...  42.6 us
    pallas_call x1, Pallas kernels, heads(): pl.pallas_call(functools.partial(heads_kernel, block_rows), out_shape=[ja...  42.2 us
    pallas_call x1, Pallas kernels, gather_line(): pl.pallas_call(functools.partial(gather_kernel, size // 2), out_shape=jax...  40.8 us
  transfers between devices with their start and end apart: 3, of which 3 were waited for; matrix products, arithmetic and copies ran while one was open for 6% of the time, Pallas kernels for 43%

profile of v4, /device:TPU:0, one launch (start us, length us, event | category | flops | bytes accessed | tf_op | source)
XLA Modules:
  0.0 714.8 jit_solution(3868844421139800924)
XLA Ops:
  9.2 59.1 %start.1 = (bf16[8,128,2048]{2,1,0:T(8,128)(2,1)}, f32[8,5,256]{2,1,0:T(8,128)}, bf16[8,4,64,768]{3,2,1,0:T(8,128)(2,1)}, f32[512,128]{1,0:T(8,128)}, f32[512,128]{1,0:T(8,128)}) custom-call(bf16[128,2048]{1,0:T(8,128)(2,1)} %bitcast.70, f32[5,256]{1,0:T(8,128)} %select_maximum_fusion.small, f32[1,128]{1,0:T(1,128)} %constant.28.clone.inverse, ...), custom_call_target="tpu_custom_call" | custom-call | bytes 198000000 | tf_op jit(solution)/shard_map/start/pallas_call | solution.py:829
  72.0 42.2 %heads.1 = (bf16[4,3,2,128,256]{4,3,2,1,0:T(8,128)(2,1)}, f32[2,8,128,256]{3,2,1,0:T(8,128)}, f32[16,128]{1,0:T(8,128)}) custom-call(s32[8,128,1]{2,1,0:T(8,128)} %broadcast_in_dim_reshape.4.row_blocks, bf16[8,128,2048]{2,1,0:T(8,128)(2,1)} %get-tuple-element.55.tokens, bf16[2048,768]{1,0:T(8,128)(2,1)} %bitcast.67, f32[512,128]{1,0:T(8,128)} %get-tuple-element.57.cosines, ...), custom_call_target="tpu_custom_call" | custom-call | bytes 115500000 | tf_op jit(solution)/shard_map/heads/pallas_call | solution.py:983
  115.6 12.9 %attend.1.refs_0_ = bf16[4,2,128,256]{3,2,1,0:T(8,128)(2,1)} custom-call(bf16[4,3,2,128,256]{4,3,2,1,0:T(8,128)(2,1)} %get-tuple-element.59.query_ref.key_ref.value_ref, bf16[4,3,2,128,256]{4,3,2,1,0:T(8,128)(2,1)} %get-tuple-element.59.query_ref.key_ref.value_ref, bf16[4,3,2,128,256]{4,3,2,1,0:T(8,128)(2,1)} %get-tuple-element.59.query_ref.key_ref.value_ref, ...), custom_call_target="tpu_custom_call" | custom-call | bytes 39600000 | tf_op jit(solution)/shard_map/attend/pallas_call | solution.py:1410
  128.5 10.6 %exchange_ctx_6.1 = bf16[4,2,128,256]{3,2,1,0:T(8,128)(2,1)} custom-call(bf16[4,2,128,256]{3,2,1,0:T(8,128)(2,1)} %attend.1.refs_0_), custom_call_target="tpu_custom_call" | custom-call | bytes 33000000 | tf_op jit(solution)/shard_map/exchange_ctx_6/pallas_call | solution.py:91
  139.1 19.3 %exchange_fsdp_7.1 = bf16[8,128,256]{2,1,0:T(8,128)(2,1)} custom-call(bf16[8,128,256]{2,1,0:T(8,128)(2,1)} %bitcast.75), custom_call_target="tpu_custom_call" | custom-call | bytes 46200000 | tf_op jit(solution)/shard_map/exchange_fsdp_7/pallas_call | solution.py:91
  159.8 6.2 all-gather.2.cloned.1.call-done
  165.9 4.8 multiply_reduce_fusion.3
  172.7 42.6 %ffn_in.1 = (bf16[8,128,2048]{2,1,0:T(8,128)(2,1)}, f32[8,128,1024]{2,1,0:T(8,128)}, f32[8,128,1024]{2,1,0:T(8,128)}, bf16[8,128,1024]{2,1,0:T(8,128)(2,1)}) custom-call(bf16[128,2048]{1,0:T(8,128)(2,1)} %fusion.6.given, bf16[2048,1024]{1,0:T(8,128)(2,1)} %refs_2_.1, bf16[2048,1024]{1,0:T(8,128)(2,1)} %refs_3_.1), custom_call_target="tpu_custom_call" | custom-call | bytes 148500000 | tf_op jit(solution)/shard_map/ffn_in/pallas_call | solution.py:353
  215.3 46.7 %reduce_line_9.1 = f32[128,2048]{1,0:T(8,128)} custom-call(bf16[8,128,1024]{2,1,0:T(8,128)(2,1)} %get-tuple-element.61.refs_0_, bf16[1024,2048]{1,0:T(8,128)(2,1)} %w_down.1), custom_call_target="tpu_custom_call" | custom-call | bytes 148500000 | tf_op jit(solution)/shard_map/reduce_line_9/pallas_call | solution.py:680
  265.0 2.3 fusion.3.given
  267.3 40.2 %ffn_back.1 = (bf16[8,128,2048]{2,1,0:T(8,128)(2,1)}, bf16[8,128,1024]{2,1,0:T(8,128)(2,1)}, bf16[8,128,1024]{2,1,0:T(8,128)(2,1)}) custom-call(bf16[128,2048]{1,0:T(8,128)(2,1)} %fusion.3.given, bf16[1024,2048]{1,0:T(8,128)(2,1)} %w_down.1, f32[8,128,1024]{2,1,0:T(8,128)} %get-tuple-element.62.gate_in, f32[8,128,1024]{2,1,0:T(8,128)} %get-tuple-element.63.up_in), custom_call_target="tpu_custom_call" | custom-call | bytes 148500000 | tf_op jit(solution)/shard_map/ffn_back/pallas_call | solution.py:461
  307.5 9.6 %bitcast_convert_fusion.2 = bf16[2048,1024]{1,0:T(8,128)(2,1)} fusion(bf16[8,128,2048]{2,1,0:T(8,128)(2,1)} %get-tuple-element.66, bf16[8,128,1024]{2,1,0:T(8,128)(2,1)} %get-tuple-element.68.refs_0_), kind=kOutput, calls=%fused_computation.2 | convolution fusion | flops 4297064448 | bytes 10485760 | tf_op jit(solution)/shard_map/dot_general | solution.py:1462
  317.1 6.2 bitcast_convert_fusion.1
  323.3 6.2 bitcast_convert_fusion
  329.6 48.8 %reduce_line_11.1 = f32[128,2048]{1,0:T(8,128)} custom-call(bf16[8,128,1024]{2,1,0:T(8,128)(2,1)} %get-tuple-element.68.refs_0_, bf16[8,128,1024]{2,1,0:T(8,128)(2,1)} %get-tuple-element.69.refs_1_, bf16[2048,1024]{1,0:T(8,128)(2,1)} %refs_2_.1, bf16[2048,1024]{1,0:T(8,128)(2,1)} %refs_3_.1), custom_call_target="tpu_custom_call" | custom-call | bytes 148500000 | tf_op jit(solution)/shard_map/reduce_line_11/pallas_call | solution.py:680
  378.5 1.9 multiply_reduce_fusion
  380.4 3.9 subtract_convert_fusion
  384.3 40.8 %gather_line_12.1 = bf16[8,128,2048]{2,1,0:T(8,128)(2,1)} custom-call(bf16[128,2048]{1,0:T(8,128)(2,1)} %get-tuple-element.103.given), custom_call_target="tpu_custom_call" | custom-call | bytes 132000000 | tf_op jit(solution)/shard_map/gather_line_12/pallas_call | solution.py:246
  425.1 4.3 convolution_convert_fusion.1
  429.4 17.7 %exchange_ctx_13.1.grad_ref = bf16[4,2,128,256]{3,2,1,0:T(8,128)(2,1)} custom-call(bf16[4,2,128,256]{3,2,1,0:T(8,128)(2,1)} %bitcast.81), custom_call_target="tpu_custom_call" | custom-call | bytes 33000000 | tf_op jit(solution)/shard_map/exchange_ctx_13/pallas_call | solution.py:91
  447.1 15.6 %attend_back.1 = (bf16[4,2,128,256]{3,2,1,0:T(8,128)(2,1)}, bf16[4,2,128,256]{3,2,1,0:T(8,128)(2,1)}, bf16[4,2,128,256]{3,2,1,0:T(8,128)(2,1)}) custom-call(bf16[4,3,2,128,256]{4,3,2,1,0:T(8,128)(2,1)} %get-tuple-element.59.query_ref.key_ref.value_ref, bf16[4,3,2,128,256]{4,3,2,1,0:T(8,128)(2,1)} %get-tuple-element.59.query_ref.key_ref.value_ref, ...), custom_call_target="tpu_custom_call" | custom-call | bytes 52800000 | tf_op jit(solution)/shard_map/attend_back/pallas_call | solution.py:1425
  462.7 54.4 %heads_back.1 = (bf16[8,128,768]{2,1,0:T(8,128)(2,1)}, f32[2,256]{1,0:T(2,128)}) custom-call(s32[8,128,1]{2,1,0:T(8,128)} %broadcast_in_dim_reshape.4.row_blocks, bf16[4,2,128,256]{3,2,1,0:T(8,128)(2,1)} %get-tuple-element.70.grad_query, bf16[4,2,128,256]{3,2,1,0:T(8,128)(2,1)} %get-tuple-element.71.grad_key, ...), custom_call_target="tpu_custom_call" | custom-call | bytes 148500000 | tf_op jit(solution)/shard_map/heads_back/pallas_call | solution.py:1111
  517.1 44.9 %reduce_line_16.1 = f32[128,2048]{1,0:T(8,128)} custom-call(bf16[8,128,768]{2,1,0:T(8,128)(2,1)} %get-tuple-element.75.refs_0_, bf16[2048,768]{1,0:T(8,128)(2,1)} %bitcast.68), custom_call_target="tpu_custom_call" | custom-call | bytes 148500000 | tf_op jit(solution)/shard_map/reduce_line_16/pallas_call | solution.py:680
  561.9 6.6 bitcast_convert_fusion.3
  573.3 2.2 pad_maximum_fusion
  575.6 15.7 %all-reduce.5.cloned.1.call-done = (bf16[1024,2048]{1,0:T(8,128)(2,1)}, bf16[2048,1024]{1,0:T(8,128)(2,1)}, bf16[2048,1024]{1,0:T(8,128)(2,1)}) async-done(((bf16[1024,2048]{1,0:T(8,128)(2,1)}, bf16[2048,1024]{1,0:T(8,128)(2,1)}, bf16[2048,1024]{1,0:T(8,128)(2,1)}), (bf16[1024,2048]{1,0:T(8,128)(2,1)}, bf16[2048,1024]{1,0:T(8,128)(2,1)}, bf16[2048,1024]{1,0:T(8,128)(2,1)})) %all-reduce.5.cloned.1.call-update) | async-done | bytes 12582928 | tf_op jit(solution)/shard_map/psum | solution.py:1544
  591.9 6.8 convert_element_type.76
  598.7 4.4 convert_element_type.77
  603.2 4.4 convert_element_type.78
  607.6 39.3 %reduce-scatter.4.cloned.1.call-done = bf16[1,64,8192]{2,1,0:T(8,128)(2,1)} async-done(((bf16[4,64,8192]{2,1,0:T(8,128)(2,1)}), bf16[1,64,8192]{2,1,0:T(8,128)(2,1)}) %reduce-scatter.4.cloned.1.call-update) | async-done | bytes 1048592
  646.9 54.8 %finish.1 = (bf16[4,3,64,2048]{3,2,1,0:T(8,128)(2,1)}, bf16[4,64,2048]{2,1,0:T(8,128)(2,1)}, f32[4,256]{1,0:T(4,128)}) custom-call(bf16[64,8192]{1,0:T(8,128)(2,1)} %bitcast.79, f32[8,2,256]{2,1,0:T(2,128)} %maximum_bitcast_fusion.gain_post, f32[2,256]{1,0:T(2,128)} %get-tuple-element.85.gain_heads), custom_call_target="tpu_custom_call" | custom-call | bytes 165000000 | tf_op jit(solution)/shard_map/finish/pallas_call | solution.py:1274
  701.7 5.8 widen.1
  (73 shorter events, 19.4 us)
Async XLA Ops:
  7.2 61.2 %copy-start.13 = (bf16[4,256]{1,0:T(4,128)(2,1)S(1)}, bf16[4,256]{1,0:T(4,128)(2,1)}, u32[]{:S(2)}) copy-start(bf16[4,256]{1,0:T(4,128)(2,1)} %param.21) | copy-start | bytes 6148
  7.2 158.7 %all-gather.2.cloned.1.call-start = ((), (), s32[]{:S(2)}) async-start(), calls=%async_computation.1 | async-start | bytes 9437184 | tf_op jit(solution)/shard_map/all_gather | solution.py:1498
  68.3 522.9 %all-reduce.5.cloned.1.call-start = ((), (), s32[]{:S(2)}) async-start(), calls=%async_computation.3 | async-start | bytes 25165824 | tf_op jit(solution)/shard_map/psum | solution.py:1544
  115.6 44.1 %copy-start.12 = (f32[8,5,256]{2,1,0:T(8,128)S(1)}, f32[8,5,256]{2,1,0:T(8,128)}, u32[]{:S(2)}) copy-start(f32[8,5,256]{2,1,0:T(8,128)} %get-tuple-element.53) | copy-start | bytes 122884
  165.9 5.8 copy-start.3
  170.7 1.0 copy-start
  215.3 48.1 %copy-start.2 = (bf16[1,128,2048]{2,1,0:T(8,128)(2,1)S(1)}, bf16[1,128,2048]{2,1,0:T(8,128)(2,1)}, u32[]{:S(2)}) copy-start(bf16[1,128,2048]{2,1,0:T(8,128)(2,1)} %param.22) | copy-start | bytes 1572868
  307.5 9.6 %copy-start.10 = (bf16[8,128,1024]{2,1,0:T(8,128)(2,1)S(1)}, bf16[8,128,1024]{2,1,0:T(8,128)(2,1)}, u32[]{:S(2)}) copy-start(bf16[8,128,1024]{2,1,0:T(8,128)(2,1)} %get-tuple-element.69.refs_1_) | copy-start | bytes 6291460
  307.5 9.6 %copy-start.15 = (bf16[8,128,2048]{2,1,0:T(8,128)(2,1)S(1)}, bf16[8,128,2048]{2,1,0:T(8,128)(2,1)}, u32[]{:S(2)}) copy-start(bf16[8,128,2048]{2,1,0:T(8,128)(2,1)} %get-tuple-element.66) | copy-start | bytes 12582916
  317.1 6.3 copy-start.8
  317.1 6.3 copy-start.16
  329.6 317.3 %reduce-scatter.4.cloned.1.call-start = ((), (), s32[]{:S(2)}) async-start(), calls=%async_computation.2 | async-start | bytes 5242880
  380.3 44.8 %copy-start.11 = (bf16[256,2048]{1,0:T(8,128)(2,1)S(1)}, bf16[256,2048]{1,0:T(8,128)(2,1)}, u32[]{:S(2)}) copy-start(bf16[256,2048]{1,0:T(8,128)(2,1)} %param.17) | copy-start | bytes 3145732
  568.6 2.2 copy-start.6
  568.6 2.3 copy-start.9
  569.0 3.2 copy-start.1
  569.0 3.2 copy-start.7
  591.9 6.8 copy-start.5
  598.7 4.5 copy-start.4
  701.7 5.8 copy-start.14
Sparse Core Ops, SparseCore 0:
  68.5 97.4 all-gather.1
  329.7 261.5 all-reduce.4
  594.3 52.5 reduce-scatter.3
